TPU v7x, 32 devices: a whole 2x2x4 slice. The times are simulated.
32 devices in a mesh: dp: 16 (over z, y, x), tensor: 2 (over core).
Axes of the slice: x: 2, y: 2, z: 4, core: 2. Of those that a mesh axis runs over, the one named last changes fastest.
Arguments:
- tokens: bfloat16 [16384, 768], P('dp'), may hold values from -6 to 6
- memory: bfloat16 [16384, 768], P('dp'), may hold values from -6 to 6
- segment: int32 [16384], P('dp'), may hold values from 0 to 3, as said below
- cotangent: bfloat16 [16384, 768], P('dp'), may hold values from -6 to 6
- self_query: bfloat16 [768, 768], P(None, 'tensor'), may hold values from -0.21875 to 0.21875
- self_query_bias: bfloat16 [768], P('tensor'), may hold values from -3 to 3
- self_key: bfloat16 [768, 768], P(None, 'tensor'), may hold values from -0.21875 to 0.21875
- self_value: bfloat16 [768, 768], P(None, 'tensor'), may hold values from -0.21875 to 0.21875
- self_value_bias: bfloat16 [768], P('tensor'), may hold values from -3 to 3
- self_output: bfloat16 [768, 768], P('tensor'), may hold values from -0.75 to 0.75
- self_output_bias: bfloat16 [768], replicated, may hold values from -3 to 3
- cross_query: bfloat16 [768, 768], P(None, 'tensor'), may hold values from -0.21875 to 0.21875
- cross_query_bias: bfloat16 [768], P('tensor'), may hold values from -3 to 3
- cross_key: bfloat16 [768, 768], P(None, 'tensor'), may hold values from -0.21875 to 0.21875
- cross_value: bfloat16 [768, 768], P(None, 'tensor'), may hold values from -0.21875 to 0.21875
- cross_value_bias: bfloat16 [768], P('tensor'), may hold values from -3 to 3
- cross_output: bfloat16 [768, 768], P('tensor'), may hold values from -0.75 to 0.75
- cross_output_bias: bfloat16 [768], replicated, may hold values from -3 to 3
- first_gain: bfloat16 [768], replicated, may hold values from 0.5 to 1.5
- first_shift: bfloat16 [768], replicated, may hold values from -3 to 3
- second_gain: bfloat16 [768], replicated, may hold values from 0.5 to 1.5
- second_shift: bfloat16 [768], replicated, may hold values from -3 to 3
- third_gain: bfloat16 [768], replicated, may hold values from 0.5 to 1.5
- third_shift: bfloat16 [768], replicated, may hold values from -3 to 3
- inner_weight: bfloat16 [768, 3072], P(None, 'tensor'), may hold values from -0.21875 to 0.21875
- inner_bias: bfloat16 [3072], P('tensor'), may hold values from -3 to 3
- outer_weight: bfloat16 [3072, 768], P('tensor'), may hold values from -0.21875 to 0.21875
- outer_bias: bfloat16 [768], replicated, may hold values from -3 to 3
Outputs:
- output: bfloat16 [16384, 768], P('dp')
- grad_tokens: float32 [16384, 768], P(('dp', 'tensor'))
- grad_memory: float32 [16384, 768], P(('dp', 'tensor'))
- grad_self_query: float32 [768, 768], P('dp', 'tensor')
- grad_self_query_bias: float32 [768], P('tensor')
- grad_self_key: float32 [768, 768], P('dp', 'tensor')
- grad_self_value: float32 [768, 768], P('dp', 'tensor')
- grad_self_value_bias: float32 [768], P('tensor')
- grad_self_output: float32 [768, 768], P('tensor', 'dp')
- grad_self_output_bias: float32 [768], replicated
- grad_cross_query: float32 [768, 768], P('dp', 'tensor')
- grad_cross_query_bias: float32 [768], P('tensor')
- grad_cross_key: float32 [768, 768], P('dp', 'tensor')
- grad_cross_value: float32 [768, 768], P('dp', 'tensor')
- grad_cross_value_bias: float32 [768], P('tensor')
- grad_cross_output: float32 [768, 768], P('tensor', 'dp')
- grad_cross_output_bias: float32 [768], replicated
- grad_first_gain: float32 [768], replicated
- grad_first_shift: float32 [768], replicated
- grad_second_gain: float32 [768], replicated
- grad_second_shift: float32 [768], replicated
- grad_third_gain: float32 [768], replicated
- grad_third_shift: float32 [768], replicated
- grad_inner_weight: float32 [768, 3072], P('dp', 'tensor')
- grad_inner_bias: float32 [3072], P('tensor')
- grad_outer_weight: float32 [3072, 768], P('tensor', 'dp')
- grad_outer_bias: float32 [768], replicated
Inputs may be any that keep to these rules, and one draw needn't show every extreme that they name: Within each block of 1024 consecutive positions the segment is either 0 throughout (one long row) or position // 256 (four rows of 256); half of the blocks are of each kind.
All inputs are finite; a program needn't handle non-finite values.
Results may differ from a plain program's by a relative error of at most 0.028.
Values may be sent and summed in bfloat16 or wider, within the bound.
A program may use at most 256 MiB of HBM per device.

v0:
```python
from functools import partial

import jax
import jax.numpy as jnp
from jax import lax
from jax.sharding import Mesh, PartitionSpec as P
import numpy as np

DP = ("outer", "inner")

HD = 64


EPSILON = 1e-05
NEGATIVE = -1e30


def normalize(hidden, gain, shift):
    center = hidden - jnp.mean(hidden, -1, keepdims=True)
    spread = jnp.mean(center * center, -1, keepdims=True)
    return center * lax.rsqrt(spread + EPSILON) * gain + shift


def project(data, weight):
    return jnp.dot(data, weight, preferred_element_type=jnp.float32)


def column_sums(values):
    return jnp.sum(values.astype(jnp.float32), 0)


def heads_of(matrix):
    return matrix.reshape(matrix.shape[0], -1, HD)


def allowed_pairs(query_segment, key_segment, start, causal):
    same = query_segment[:, None] == key_segment[None, :]
    if causal:
        query_place = start + jnp.arange(query_segment.shape[0], dtype=jnp.int32)
        key_place = jnp.arange(key_segment.shape[0], dtype=jnp.int32)
        same = same & (key_place[None, :] <= query_place[:, None])
    return same[None]


def attend_forward(queries, keys, values, segment, causal):
    length = queries.shape[0]
    block_rows = min(256 if causal else 512, length)
    contexts = []
    totals = []
    for index in range(length // block_rows):
        start = index * block_rows
        end = start + block_rows if causal else length
        piece = queries[start : start + block_rows]
        scores = jnp.einsum(
            "qhe,khe->hqk", piece, keys[:end], preferred_element_type=jnp.float32
        )
        scores = jnp.where(
            allowed_pairs(segment[start : start + block_rows], segment[:end], start, causal),
            scores,
            NEGATIVE,
        )
        highest = jnp.max(scores, -1, keepdims=True)
        powers = jnp.exp(scores - highest)
        summed = jnp.sum(powers, -1, keepdims=True)
        weights = (powers / summed).astype(jnp.bfloat16)
        contexts.append(
            jnp.einsum("hqk,khe->qhe", weights, values[:end], preferred_element_type=jnp.float32)
        )
        totals.append(highest + jnp.log(summed))
    return (jnp.concatenate(contexts, 0), jnp.concatenate(totals, 1))


def attend_backward(queries, keys, values, grad_context, totals, segment, causal, exact_context):
    length = queries.shape[0]
    block_rows = min(256 if causal else 512, length)
    inner = jnp.einsum(
        "qhe,qhe->hq", grad_context.astype(jnp.float32), exact_context
    )[..., None]
    grad_queries = []
    grad_keys = jnp.zeros(keys.shape, jnp.float32)
    grad_values = jnp.zeros(values.shape, jnp.float32)
    for index in range(length // block_rows):
        start = index * block_rows
        end = start + block_rows if causal else length
        piece = queries[start : start + block_rows]
        grad_piece = grad_context[start : start + block_rows]
        near_keys = keys[:end]
        scores = jnp.einsum("qhe,khe->hqk", piece, near_keys, preferred_element_type=jnp.float32)
        scores = jnp.where(
            allowed_pairs(segment[start : start + block_rows], segment[:end], start, causal),
            scores,
            NEGATIVE,
        )
        probs = jnp.exp(scores - totals[:, start : start + block_rows])
        grad_probs = jnp.einsum(
            "qhe,khe->hqk", grad_piece, values[:end], preferred_element_type=jnp.float32
        )
        row_inner = inner[:, start : start + block_rows]
        grad_scores = (probs * (grad_probs - row_inner)).astype(jnp.bfloat16)
        grad_queries.append(
            jnp.einsum("hqk,khe->qhe", grad_scores, near_keys, preferred_element_type=jnp.float32)
        )
        grad_keys = grad_keys.at[:end].add(
            jnp.einsum("hqk,qhe->khe", grad_scores, piece, preferred_element_type=jnp.float32)
        )
        grad_values = grad_values.at[:end].add(
            jnp.einsum(
                "hqk,qhe->khe",
                probs.astype(jnp.bfloat16),
                grad_piece,
                preferred_element_type=jnp.float32,
            )
        )
    return (jnp.concatenate(grad_queries, 0), grad_keys, grad_values)


def on_device(
    tokens,
    memory,
    segment,
    cotangent,
    self_query,
    self_query_bias,
    self_key,
    self_value,
    self_value_bias,
    self_output,
    self_output_bias,
    cross_query,
    cross_query_bias,
    cross_key,
    cross_value,
    cross_value_bias,
    cross_output,
    cross_output_bias,
    first_gain,
    first_shift,
    second_gain,
    second_shift,
    third_gain,
    third_shift,
    inner_weight,
    inner_bias,
    outer_weight,
    outer_bias,
):
    scale = HD ** (-0.5)
    length = tokens.shape[0]
    groups = lax.axis_size("tensor")
    member = lax.axis_index("tensor")
    half = length // groups

    def rows_of(values):
        return lax.dynamic_slice_in_dim(values, member * half, half, 0)

    def spread_out(values):
        whole = jnp.zeros((values.shape[0] * groups,), jnp.float32)
        return lax.dynamic_update_slice_in_dim(whole, values, member * values.shape[0], 0)

    def own_share(values, count):
        return lax.dynamic_slice_in_dim(values, member * count, count, 0)

    def swap(values):
        return lax.ppermute(values, "tensor", [(0, 1), (1, 0)])

    def gather_rows(values):
        if groups != 2:
            return lax.all_gather(values, "tensor", axis=0, tiled=True)
        other = swap(values)
        lead = member == 0
        return jnp.concatenate(
            [jnp.where(lead, values, other), jnp.where(lead, other, values)], 0
        )

    def scatter_rows(values):
        if groups != 2:
            return lax.psum_scatter(
                values, "tensor", scatter_dimension=0, tiled=True
            ).astype(jnp.float32)
        top = values[:half]
        bottom = values[half:]
        lead = member == 0
        keep = jnp.where(lead, top, bottom)
        send = jnp.where(lead, bottom, top)
        return keep.astype(jnp.float32) + swap(send).astype(jnp.float32)

    def sum_pair(values):
        if groups != 2:
            return lax.psum(values, "tensor").astype(jnp.float32)
        return values.astype(jnp.float32) + swap(values).astype(jnp.float32)

    queries = ((project(tokens, self_query) + self_query_bias.astype(jnp.float32)) * scale).astype(
        jnp.bfloat16
    )
    keys = project(tokens, self_key).astype(jnp.bfloat16)
    values = (project(tokens, self_value) + self_value_bias.astype(jnp.float32)).astype(
        jnp.bfloat16
    )
    self_queries = heads_of(queries)
    self_keys = heads_of(keys)
    self_values = heads_of(values)
    self_context, self_totals = attend_forward(self_queries, self_keys, self_values, segment, True)
    self_exact = self_context
    self_context = self_context.reshape(length, -1).astype(jnp.bfloat16)
    attended = scatter_rows(project(self_context, self_output)) + self_output_bias.astype(
        jnp.float32
    )
    first, first_back = jax.vjp(
        normalize,
        rows_of(tokens).astype(jnp.float32) + attended,
        first_gain.astype(jnp.float32),
        first_shift.astype(jnp.float32),
    )
    first_low = gather_rows(first.astype(jnp.bfloat16))
    queries = (
        (project(first_low, cross_query) + cross_query_bias.astype(jnp.float32)) * scale
    ).astype(jnp.bfloat16)
    keys = project(memory, cross_key).astype(jnp.bfloat16)
    values = (project(memory, cross_value) + cross_value_bias.astype(jnp.float32)).astype(
        jnp.bfloat16
    )
    cross_queries = heads_of(queries)
    cross_keys = heads_of(keys)
    cross_values = heads_of(values)
    cross_context, cross_totals = attend_forward(
        cross_queries, cross_keys, cross_values, segment, False
    )
    cross_exact = cross_context
    cross_context = cross_context.reshape(length, -1).astype(jnp.bfloat16)
    crossed = scatter_rows(
        project(cross_context, cross_output).astype(jnp.bfloat16)
    ) + cross_output_bias.astype(jnp.float32)
    second_part, second_back = jax.vjp(
        normalize,
        first + crossed,
        second_gain.astype(jnp.float32),
        second_shift.astype(jnp.float32),
    )
    second = gather_rows(second_part.astype(jnp.bfloat16)).astype(second_part.dtype)
    second_low = second.astype(jnp.bfloat16)
    inner = project(second_low, inner_weight) + inner_bias.astype(jnp.float32)
    hidden = jax.nn.gelu(inner, approximate=False).astype(jnp.bfloat16)
    outer = sum_pair(project(hidden, outer_weight).astype(jnp.bfloat16)) + outer_bias.astype(
        jnp.float32
    )
    result, third_back = jax.vjp(
        normalize, second + outer, third_gain.astype(jnp.float32), third_shift.astype(jnp.float32)
    )
    output = result.astype(jnp.bfloat16)
    grad_third, grad_third_gain, grad_third_shift = third_back(cotangent.astype(jnp.float32))
    grad_outer = grad_third.astype(jnp.bfloat16)
    grad_outer_bias = column_sums(grad_outer)
    gelu_back = jax.vjp(partial(jax.nn.gelu, approximate=False), inner)[1]
    grad_inner = gelu_back(project(grad_outer, outer_weight.T))[0].astype(jnp.bfloat16)
    grad_inner_weight = project(second_low.T, grad_inner)
    grad_inner_bias = column_sums(grad_inner)
    grad_second = rows_of(grad_third) + scatter_rows(
        project(grad_inner, inner_weight.T).astype(jnp.bfloat16)
    )
    grad_second_in, grad_second_gain, grad_second_shift = second_back(grad_second)
    grad_cross_rows = grad_second_in.astype(jnp.bfloat16)
    grad_cross = gather_rows(grad_cross_rows)
    grad_cross_output_bias = column_sums(grad_cross)
    grad_cross_context = heads_of(project(grad_cross, cross_output.T).astype(jnp.bfloat16))
    cross_grad_q, cross_grad_k, cross_grad_v = attend_backward(
        cross_queries,
        cross_keys,
        cross_values,
        grad_cross_context,
        cross_totals,
        segment,
        False,
        cross_exact,
    )
    cross_grad_q = (cross_grad_q.astype(jnp.bfloat16) * scale).reshape(length, -1)
    cross_grad_k = cross_grad_k.astype(jnp.bfloat16).reshape(length, -1)
    cross_grad_v = cross_grad_v.astype(jnp.bfloat16).reshape(length, -1)
    grad_cross_query = project(first_low.T, cross_grad_q)
    grad_cross_query_bias = column_sums(cross_grad_q)
    grad_cross_key = project(memory.T, cross_grad_k)
    grad_cross_value = project(memory.T, cross_grad_v)
    grad_cross_value_bias = column_sums(cross_grad_v)
    memory_term = project(cross_grad_k, cross_key.T) + project(cross_grad_v, cross_value.T)
    grad_first = grad_second_in + scatter_rows(
        project(cross_grad_q, cross_query.T).astype(jnp.bfloat16)
    )
    grad_cross_output_t = project(grad_cross.T, cross_context)
    cross = [grad_cross_query, grad_cross_key, grad_cross_value, grad_cross_output_t]
    cross_joined = jnp.concatenate(cross, 1).astype(jnp.bfloat16)
    cross_joined, grad_first = lax.optimization_barrier((cross_joined, grad_first))
    grad_first_in, grad_first_gain, grad_first_shift = first_back(grad_first)
    grad_self_rows = grad_first_in.astype(jnp.bfloat16)
    grad_self = gather_rows(grad_self_rows)
    grad_self_output_bias = column_sums(grad_self)
    grad_self_context = heads_of(project(grad_self, self_output.T).astype(jnp.bfloat16))
    outer_size = lax.axis_size("outer")
    inner_size = lax.axis_size("inner")
    dp_size = outer_size * inner_size
    self_grad_q, self_grad_k, self_grad_v = attend_backward(
        self_queries,
        self_keys,
        self_values,
        grad_self_context,
        self_totals,
        segment,
        True,
        self_exact,
    )
    self_grad_q = (self_grad_q.astype(jnp.bfloat16) * scale).reshape(length, -1)
    self_grad_k = self_grad_k.astype(jnp.bfloat16).reshape(length, -1)
    self_grad_v = self_grad_v.astype(jnp.bfloat16).reshape(length, -1)
    grad_self_query = project(tokens.T, self_grad_q)
    grad_self_query_bias = column_sums(self_grad_q)
    grad_self_key = project(tokens.T, self_grad_k)
    grad_self_value = project(tokens.T, self_grad_v)
    grad_self_value_bias = column_sums(self_grad_v)
    tokens_term = (
        project(self_grad_q, self_query.T)
        + project(self_grad_k, self_key.T)
        + project(self_grad_v, self_value.T)
    )
    tokens_part = scatter_rows(tokens_term.astype(jnp.bfloat16))
    memory_part = scatter_rows(memory_term.astype(jnp.bfloat16))
    grad_tokens = tokens_part + grad_first_in
    grad_self_output_t = project(grad_self.T, self_context)
    grad_outer_weight_t = project(grad_outer.T, hidden)

    def split_columns(summed, pieces, flipped):
        parts = []
        offset = 0
        for position, piece in enumerate(pieces):
            width = piece.shape[1]
            part = summed[:, offset : offset + width]
            offset += width
            if position in flipped:
                part = part.T
            parts.append(part)
        return parts

    def exchange_sum(joined, extra=None):
        rows = joined.shape[0] // dp_size
        width = joined.shape[1]
        blocks = joined.reshape(dp_size, rows, width)
        if inner_size == 1 or outer_size == 1:
            if extra is not None:
                blocks = jnp.concatenate(
                    [blocks, jnp.broadcast_to(extra[None], (dp_size,) + extra.shape)], 1
                )
            received = lax.all_to_all(blocks, DP, 0, 0, tiled=True)
            return jnp.sum(received.astype(jnp.float32), 0)
        staged = blocks.reshape(outer_size, inner_size, rows, width)
        staged = jnp.swapaxes(staged, 0, 1).reshape(inner_size, outer_size * rows, width)
        if extra is not None:
            staged = jnp.concatenate(
                [staged, jnp.broadcast_to(extra[None], (inner_size,) + extra.shape)], 1
            )
        first = lax.all_to_all(staged, "inner", 0, 0, tiled=True)
        partial = jnp.sum(first.astype(jnp.float32), 0)
        middle = partial[: outer_size * rows].astype(jnp.bfloat16).reshape(
            outer_size, rows, width
        )
        if extra is not None:
            lines = extra.shape[0] // 2
            tail = partial[outer_size * rows :]
            merged = tail[:lines] + tail[lines:]
            high = merged.astype(jnp.bfloat16)
            low = (merged - high.astype(jnp.float32)).astype(jnp.bfloat16)
            pair = jnp.concatenate([high, low], 0)
            middle = jnp.concatenate(
                [middle, jnp.broadcast_to(pair[None], (outer_size,) + pair.shape)], 1
            )
        second = lax.all_to_all(middle, "outer", 0, 0, tiled=True)
        return jnp.sum(second.astype(jnp.float32), 0)

    ffn = [grad_inner_weight, grad_outer_weight_t]
    ffn_sum = lax.psum_scatter(
        jnp.concatenate(ffn, 1).astype(jnp.bfloat16), DP, scatter_dimension=0, tiled=True
    ).astype(jnp.float32)
    ffn_sums = split_columns(ffn_sum, ffn, (1,))
    cross_sums = split_columns(exchange_sum(cross_joined), cross, (3,))
    late = [grad_self_query, grad_self_key, grad_self_value, grad_self_output_t]
    late_joined = jnp.concatenate(late, 1).astype(jnp.bfloat16)
    norm_pairs = sum_pair(
        jnp.concatenate([grad_first_gain, grad_first_shift, grad_second_gain, grad_second_shift])
    )
    width = late_joined.shape[1]
    sections = norm_pairs.shape[0] // 4
    biases = [
        grad_self_query_bias,
        grad_self_value_bias,
        grad_self_output_bias,
        grad_cross_query_bias,
        grad_cross_value_bias,
        grad_cross_output_bias,
        norm_pairs[:sections],
        norm_pairs[sections : 2 * sections],
        norm_pairs[2 * sections : 3 * sections],
        norm_pairs[3 * sections :],
        grad_third_gain,
        grad_third_shift,
        grad_inner_bias,
        grad_outer_bias,
    ]
    lines = []
    current = []
    used = 0
    places = []
    for bias in biases:
        chunks = []
        for begin in range(0, bias.shape[0], width):
            chunk = bias[begin : begin + width]
            if used + chunk.shape[0] > width:
                if used < width:
                    current.append(jnp.zeros((width - used,), jnp.float32))
                lines.append(jnp.concatenate(current))
                current = []
                used = 0
            chunks.append((len(lines), used, chunk.shape[0]))
            current.append(chunk)
            used += chunk.shape[0]
        places.append(chunks)
    if used < width:
        current.append(jnp.zeros((width - used,), jnp.float32))
    lines.append(jnp.concatenate(current))
    padded = jnp.stack(lines)
    count = padded.shape[0]
    high = padded.astype(jnp.bfloat16)
    low = (padded - high.astype(jnp.float32)).astype(jnp.bfloat16)
    late_rows = late_joined.shape[0] // dp_size
    late_total = exchange_sum(late_joined, jnp.concatenate([high, low], 0))
    self_sums = split_columns(late_total[:late_rows], late, (3,))
    summed_lines = late_total[late_rows : late_rows + count] + late_total[late_rows + count :]
    smalls = []
    for chunks in places:
        smalls.append(
            jnp.concatenate(
                [summed_lines[line, begin : begin + size] for line, begin, size in chunks]
            )
        )
    return (
        output,
        grad_tokens,
        memory_part,
        self_sums[0],
        smalls[0],
        self_sums[1],
        self_sums[2],
        smalls[1],
        self_sums[3],
        smalls[2],
        cross_sums[0],
        smalls[3],
        cross_sums[1],
        cross_sums[2],
        smalls[4],
        cross_sums[3],
        smalls[5],
        smalls[6],
        smalls[7],
        smalls[8],
        smalls[9],
        smalls[10],
        smalls[11],
        ffn_sums[0],
        smalls[12],
        ffn_sums[1],
        smalls[13],
    )


def solution(mesh):
    dp_size = mesh.shape["dp"]
    inner = 4 if dp_size % 4 == 0 and dp_size > 4 else 1
    devices = np.asarray(mesh.devices).reshape(dp_size // inner, inner, mesh.shape["tensor"])
    staged = Mesh(devices, ("outer", "inner", "tensor"))
    return jax.shard_map(
        on_device,
        mesh=staged,
        in_specs=(
            P(DP, None),
            P(DP, None),
            P(DP),
            P(DP, None),
            P(None, "tensor"),
            P("tensor"),
            P(None, "tensor"),
            P(None, "tensor"),
            P("tensor"),
            P("tensor", None),
            P(),
            P(None, "tensor"),
            P("tensor"),
            P(None, "tensor"),
            P(None, "tensor"),
            P("tensor"),
            P("tensor", None),
            P(),
            P(),
            P(),
            P(),
            P(),
            P(),
            P(),
            P(None, "tensor"),
            P("tensor"),
            P("tensor", None),
            P(),
        ),
        out_specs=(
            P(DP, None),
            P(("outer", "inner", "tensor"), None),
            P(("outer", "inner", "tensor"), None),
            P(DP, "tensor"),
            P("tensor"),
            P(DP, "tensor"),
            P(DP, "tensor"),
            P("tensor"),
            P("tensor", DP),
            P(),
            P(DP, "tensor"),
            P("tensor"),
            P(DP, "tensor"),
            P(DP, "tensor"),
            P("tensor"),
            P("tensor", DP),
            P(),
            P(),
            P(),
            P(),
            P(),
            P(),
            P(),
            P(DP, "tensor"),
            P("tensor"),
            P("tensor", DP),
            P(),
        ),
        check_vma=False,
    )
```

profile of v0, /device:TPU:0, one launch (start us, length us, event | category | flops | bytes accessed | tf_op | source)
XLA Modules:
  0.0 384.7 jit_solution(6881410127725269737)
XLA Ops:
  12.4 2.5 add_convert_fusion.8
  21.3 2.4 multiply_convert_fusion.8
  30.9 2.2 fusion.156
  36.5 2.3 fusion.155
  40.1 1.6 fusion.22
  42.8 2.9 fusion.154
  48.0 1.8 slice_select_fusion
  54.0 2.9 fusion.145
  63.1 6.6 %select_reduce_fusion = (f32[6,512]{1,0:T(8,128)S(1)}, f32[6,512,1024]{2,1,0:T(8,128)}) fusion(pred[512,1024]{1,0:T(8,128)(4,1)S(1)} %get-tuple-element.414, bf16[512,6,64]{0,2,1:T(8,128)(2,1)S(1)} %bitcast.289, bf16[1024,6,64]{0,2,1:T(8,128)(2,1)S(1)} %bitcast.277), kind=kOutput, calls=%fused_computation.12 | convolution fusion | flops 408941568 | bytes 14299136 | tf_op jit(solution)/shard_map/qhe,khe->hqk/dot_general | solution.py:54
  69.8 2.1 select_reduce_fusion.1
  71.9 12.1 %fusion = (f32[6,512]{1,0:T(8,128)S(1)}, f32[6,512]{1,0:T(8,128)S(1)}) fusion(f32[6,512,1024]{2,1,0:T(8,128)S(1)} %get-tuple-element.432, f32[6,512]{1,0:T(8,128)S(1)} %get-tuple-element.431, pred[512,1024]{1,0:T(8,128)(4,1)S(1)} %get-tuple-element.413, f32[6,512]{1,0:T(8,128)S(1)} %get-tuple-element.429, f32[6,512,1024]{2,1,0:T(8,128)} %get-tuple-element.430, ...), kind=kLoop, calls=%fused_computation.8 | loop fusion | flops 18868224 | bytes 26263552 | tf_op jit(solution)/shard_map/reduce_sum | solution.py:64
  84.0 6.9 %fusion.82 = f32[512,6,64]{0,2,1:T(8,128)S(1)} fusion(bf16[1024,6,64]{0,2,1:T(8,128)(2,1)S(1)} %bitcast.367, f32[6,512,1024]{2,1,0:T(8,128)} %get-tuple-element.430, f32[6,512]{1,0:T(8,128)S(1)} %get-tuple-element.449, f32[6,512]{1,0:T(8,128)S(1)} %get-tuple-element.429, pred[512,1024]{1,0:T(8,128)(4,1)S(1)} %get-tuple-element.414), kind=kOutput, calls=%fused_computation.181 | convolution fusion | flops 415236096 | bytes 14704640 | tf_op jit(solution)/shard_map/hqk,khe->qhe/dot_general | solution.py:67
  90.9 3.2 fusion.83
  97.3 1.9 collective-permute-done.2
  100.9 1.9 collective-permute-done.3
  103.3 18.2 %multiply_convert_fusion.3 = (bf16[1024,1536]{1,0:T(8,128)(2,1)S(1)}, f32[1024,1536]{1,0:T(8,128)}, f32[1024,1536]{1,0:T(8,128)}) fusion(f32[1536]{0:T(1024)S(1)} %convert_element_type.352, bf16[768,1536]{1,0:T(8,128)(2,1)S(1)} %copy-done, bf16[512,768]{0,1:T(8,128)(2,1)S(1)} %get-tuple-element.380, bf16[512,768]{0,1:T(8,128)(2,1)S(1)} %get-tuple-element.379), kind=kOutput, calls=%fused_computation.24 | convolution fusion | flops 2522873856 | bytes 19666944 | tf_op jit(solution)/shard_map/dot_general | solution.py:25
  121.5 3.8 convolution_convert_fusion.5
  126.9 1.8 copy.150
  128.7 2.7 copy.135
  131.4 1.7 copy.151
  133.1 1.8 copy.152
  134.9 1.8 copy.153
  140.0 3.2 fusion.142
  145.6 2.7 convert_reduce_fusion.3
  148.3 6.9 %convert_reduce_fusion = (f32[1536]{0:T(1024)S(1)}, bf16[1024,1536]{1,0:T(8,128)(2,1)S(1)}) fusion(f32[1024,1536]{1,0:T(8,128)S(1)} %bitcast.372, bf16[1536,768]{1,0:T(8,128)(2,1)S(1)} %copy-done.168, f32[1024,768]{0,1:T(8,128)S(1)} %get-tuple-element.360, f32[1024,1536]{1,0:T(8,128)} %get-tuple-element.433, f32[1536]{0:T(1024)S(1)} %copy-done.150), kind=kOutput, calls=%fused_computation.18 | convolution fusion | flops 2443442688 | bytes 21245952 | tf_op jit(solution)/shard_map/dot_general | solution.py:25
  155.3 2.6 convolution_convert_fusion.4
  160.1 2.8 convolution_convert_fusion
  167.0 3.0 convolution_convert_fusion.1
  170.0 2.7 pad_maximum_fusion
  175.5 1.6 convolution_convert_fusion.14
  179.2 7.2 %multiply_convert_fusion.1 = bf16[6,512,1024]{2,1,0:T(8,128)(2,1)S(1)} fusion(f32[6,512,1024]{2,1,0:T(8,128)} %copy-done.2, f32[6,512]{1,0:T(8,128)S(1)} %get-tuple-element.408, f32[6,512]{1,0:T(8,128)S(1)} %log_add_fusion.1, pred[512,1024]{1,0:T(8,128)(4,1)S(1)} %get-tuple-element.413, bf16[512,6,64]{0,2,1:T(8,128)(2,1)S(1)} %bitcast.342, ...), kind=kOutput, calls=%fused_computation.2 | convolution fusion | flops 418381824 | bytes 20602880 | tf_op jit(solution)/shard_map/qhe,khe->hqk/dot_general | solution.py:95
  186.4 2.8 convolution_convert_fusion.19
  190.5 3.2 fusion.5
  193.7 8.9 %multiply_convert_fusion = bf16[6,512,1024]{2,1,0:T(8,128)(2,1)} fusion(f32[6,512,1024]{2,1,0:T(8,128)} %get-tuple-element.430, f32[6,512]{1,0:T(8,128)S(1)} %get-tuple-element.407, f32[6,512]{1,0:T(8,128)S(1)} %log_add_fusion, pred[512,1024]{1,0:T(8,128)(4,1)S(1)} %get-tuple-element.414, bf16[512,6,64]{0,2,1:T(8,128)(2,1)S(1)} %bitcast.345, ...), kind=kOutput, calls=%fused_computation | convolution fusion | flops 418381824 | bytes 20602880 | tf_op jit(solution)/shard_map/qhe,khe->hqk/dot_general | solution.py:95
  202.6 4.9 %convert_reduce_fusion.7 = (f32[6,64]{1,0:T(8,128)S(1)}, bf16[6,64,1024]{2,1,0:T(8,128)(2,1)}) fusion(f32[6,64,1024]{2,1,0:T(8,128)S(1)} %fusion.5, bf16[512,6,64]{0,2,1:T(8,128)(2,1)S(1)} %bitcast.343, f32[6,512,1024]{2,1,0:T(8,128)S(1)} %bitcast.270, f32[6,512]{1,0:T(8,128)S(1)} %log_add_fusion.1, pred[512,1024]{1,0:T(8,128)(4,1)S(1)} %get-tuple-element.413), kind=kOutput, calls=%fused_computation.120 | convolution fusion | flops 413662848 | bytes 15873536 | tf_op jit(solution)/shard_map/hqk,qhe->khe/dot_general | solution.py:107
  207.6 5.1 %convolution_convert_fusion.18 = bf16[6,64,512]{2,1,0:T(8,128)(2,1)S(1)} fusion(bf16[1024,6,64]{0,2,1:T(8,128)(2,1)S(1)} %bitcast.280, bf16[6,512,1024]{2,1,0:T(8,128)(2,1)} %multiply_convert_fusion), kind=kOutput, calls=%fused_computation.190 | convolution fusion | flops 402849792 | bytes 7471104 | tf_op jit(solution)/shard_map/hqk,khe->qhe/dot_general | solution.py:101
  218.7 1.6 pad_maximum_fusion.2
  220.3 2.6 fusion.161
  228.7 2.4 copy.156
  231.2 3.3 copy.157
  234.5 5.2 %all-to-all-start.2 = ((bf16[4,192,1536]{2,1,0:T(8,128)(2,1)}), bf16[4,192,1536]{2,1,0:T(8,128)(2,1)}, u32[]{:S(2)}, u32[]{:S(2)}) async-start(bf16[4,192,1536]{2,1,0:T(8,128)(2,1)} %bitcast.284), calls=%async_computation.2 | async-start | bytes 4718592 | tf_op jit(solution)/shard_map/all_to_all | solution.py:357
  253.7 1.7 multiply_convert_fusion.4
  255.6 2.5 convert_reduce_fusion.9
  258.1 2.5 multiply_convert_fusion.2
  265.0 2.9 fusion.90
  272.3 1.6 fusion.89
  273.9 1.6 fusion.88
  277.8 2.1 copy.147
  283.5 1.8 pad_maximum_fusion.1
  285.2 4.7 %all-to-all-start = ((bf16[4,206,1536]{2,1,0:T(8,128)(2,1)}), bf16[4,206,1536]{2,1,0:T(8,128)(2,1)}, u32[]{:S(2)}, u32[]{:S(2)}) async-start(bf16[4,206,1536]{2,1,0:T(8,128)(2,1)} %pad_maximum_fusion.1), calls=%async_computation | async-start | bytes 5111808 | tf_op jit(solution)/shard_map/all_to_all | solution.py:357
  289.9 2.9 add_convert_fusion.1
  299.4 3.0 reduce_sum.415
  302.4 20.0 %all-to-all-done = bf16[4,206,1536]{2,1,0:T(8,128)(2,1)} async-done(((bf16[4,206,1536]{2,1,0:T(8,128)(2,1)}), bf16[4,206,1536]{2,1,0:T(8,128)(2,1)}, u32[]{:S(2)}, u32[]{:S(2)}) %all-to-all-start) | async-done | bytes 2531360 | tf_op jit(solution)/shard_map/all_to_all | solution.py:357
  322.4 4.6 %all-to-all-start.3 = ((bf16[4,48,1536]{2,1,0:T(8,128)(2,1)}), bf16[4,48,1536]{2,1,0:T(8,128)(2,1)S(1)}, u32[]{:S(2)}, u32[]{:S(2)}) async-start(bf16[4,48,1536]{2,1,0:T(8,128)(2,1)} %bitcast.97), calls=%async_computation.3 | async-start | bytes 1179648 | tf_op jit(solution)/shard_map/all_to_all | solution.py:372
  327.0 2.2 convert_reduce_fusion.1
  330.3 16.5 %all-to-all-done.3 = bf16[4,48,1536]{2,1,0:T(8,128)(2,1)S(1)} async-done(((bf16[4,48,1536]{2,1,0:T(8,128)(2,1)}), bf16[4,48,1536]{2,1,0:T(8,128)(2,1)S(1)}, u32[]{:S(2)}, u32[]{:S(2)}) %all-to-all-start.3) | async-done | bytes 589856 | tf_op jit(solution)/shard_map/all_to_all | solution.py:372
  347.6 3.7 all-to-all-start.1
  351.3 2.6 copy.158
  353.9 2.6 convert_add_fusion
  356.5 3.1 copy.160
  359.6 3.2 add_add_fusion.4
  362.8 3.0 copy.159
  367.9 3.6 all-to-all-done.1
  375.9 1.6 slice.717
  (580 shorter events, 115.9 us)
Async XLA Ops:
  7.2 96.1 %copy-start = (bf16[768,1536]{1,0:T(8,128)(2,1)S(1)}, bf16[768,1536]{1,0:T(8,128)(2,1)}, u32[]{:S(2)}) copy-start(bf16[768,1536]{1,0:T(8,128)(2,1)} %param.88) | copy-start | bytes 7077892
  7.2 367.0 %reduce-scatter.2.cloned.1.call-start = ((), (), s32[]{:S(2)}) async-start(), calls=%async_computation.5 | async-start | bytes 5013504 | tf_op jit(solution)/shard_map/reduce_scatter | solution.py:376
  12.4 4.9 %copy-start.113 = (bf16[768,384]{1,0:T(8,128)(2,1)S(1)}, bf16[768,384]{1,0:T(8,128)(2,1)}, u32[]{:S(2)}) copy-start(bf16[768,384]{1,0:T(8,128)(2,1)} %param.70) | copy-start | bytes 1769476
  12.4 4.9 %copy-start.120 = (bf16[1024,768]{1,0:T(8,128)(2,1)S(1)}, bf16[1024,768]{1,0:T(8,128)(2,1)}, u32[]{:S(2)}) copy-start(bf16[1024,768]{1,0:T(8,128)(2,1)} %param.64) | copy-start | bytes 4718596
  18.2 20.7 %copy-start.30 = (bf16[1024,384]{0,1:T(8,128)(2,1)}, bf16[1024,384]{0,1:T(8,128)(2,1)S(1)}, u32[]{:S(2)}) copy-start(bf16[1024,384]{0,1:T(8,128)(2,1)S(1)} %convolution_convert_fusion.9) | copy-start | bytes 2359300
  19.0 9.9 %copy-start.47 = (bf16[512,384]{0,1:T(8,128)(2,1)}, bf16[512,384]{0,1:T(8,128)(2,1)S(1)}, u32[]{:S(2)}) copy-start(bf16[512,384]{0,1:T(8,128)(2,1)S(1)} %slice.659) | copy-start | bytes 1179652
  25.7 16.1 %copy-start.45 = (pred[256,1024]{1,0:T(8,128)(4,1)}, pred[256,1024]{1,0:T(8,128)(4,1)S(1)}, u32[]{:S(2)}) copy-start(pred[256,1024]{1,0:T(8,128)(4,1)S(1)} %fusion.94) | copy-start | bytes 786436
  28.7 17.0 %copy-start.90 = (f32[256,6,64]{0,2,1:T(8,128)}, f32[256,6,64]{0,2,1:T(8,128)S(1)}, u32[]{:S(2)}) copy-start(f32[256,6,64]{0,2,1:T(8,128)S(1)} %get-tuple-element.447) | copy-start | bytes 1179652
  29.7 3.5 copy-start.11
  33.1 12.6 %copy-start.92 = (f32[256,6,64]{0,2,1:T(8,128)}, f32[256,6,64]{0,2,1:T(8,128)S(1)}, u32[]{:S(2)}) copy-start(f32[256,6,64]{0,2,1:T(8,128)S(1)} %get-tuple-element.445) | copy-start | bytes 1179652
  38.9 6.8 %copy-start.94 = (f32[256,6,64]{0,2,1:T(8,128)}, f32[256,6,64]{0,2,1:T(8,128)S(1)}, u32[]{:S(2)}) copy-start(f32[256,6,64]{0,2,1:T(8,128)S(1)} %get-tuple-element.443) | copy-start | bytes 1179652
  41.7 3.9 %copy-start.136 = (f32[6,256]{1,0:T(8,128)}, f32[6,256]{1,0:T(8,128)S(1)}, u32[]{:S(2)}) copy-start(f32[6,256]{1,0:T(8,128)S(1)} %fusion.22) | copy-start | bytes 18436
  50.1 3.9 %collective-permute-start = (f32[512,768]{0,1:T(8,128)}, f32[512,768]{0,1:T(8,128)}, u32[]{:S(2)}, u32[]{:S(2)}) collective-permute-start(f32[512,768]{0,1:T(8,128)} %slice_select_fusion), channel_id=1, source_target_pairs={{0,1},{1,0},{2,3},{3,2},{4,5},{5,4},{6,7},{7,6},{8,9},{9,8},{10,11... | collective-permute-start | bytes 4718600 | tf_op jit(solution)/shard_map/ppermute | solution.py:164
  56.9 42.3 %copy-start.3 = (f32[512,768]{0,1:T(8,128)}, f32[512,768]{0,1:T(8,128)S(1)}, u32[]{:S(2)}) copy-start(f32[512,768]{0,1:T(8,128)S(1)} %get-tuple-element.373) | copy-start | bytes 4718596
  57.5 3.3 collective-permute-start.1
  59.9 9.8 %copy-start.28 = (bf16[1024,384]{0,1:T(8,128)(2,1)}, bf16[1024,384]{0,1:T(8,128)(2,1)S(1)}, u32[]{:S(2)}) copy-start(bf16[1024,384]{0,1:T(8,128)(2,1)S(1)} %convolution_convert_fusion.8) | copy-start | bytes 2359300
  60.8 30.1 %copy-start.175 = (bf16[1024,384]{0,1:T(8,128)(2,1)}, bf16[1024,384]{0,1:T(8,128)(2,1)S(1)}, u32[]{:S(2)}) copy-start(bf16[1024,384]{0,1:T(8,128)(2,1)S(1)} %add_convert_fusion.7) | copy-start | bytes 2359300
  63.1 6.6 %copy-start.41 = (bf16[512,384]{0,1:T(8,128)(2,1)}, bf16[512,384]{0,1:T(8,128)(2,1)S(1)}, u32[]{:S(2)}) copy-start(bf16[512,384]{0,1:T(8,128)(2,1)S(1)} %get-tuple-element.390) | copy-start | bytes 1179652
  63.1 6.6 %copy-start.43 = (bf16[512,384]{0,1:T(8,128)(2,1)}, bf16[512,384]{0,1:T(8,128)(2,1)S(1)}, u32[]{:S(2)}) copy-start(bf16[512,384]{0,1:T(8,128)(2,1)S(1)} %get-tuple-element.389) | copy-start | bytes 1179652
  71.9 19.0 %copy-start.2 = (f32[6,512,1024]{2,1,0:T(8,128)}, f32[6,512,1024]{2,1,0:T(8,128)S(1)}, u32[]{:S(2)}) copy-start(f32[6,512,1024]{2,1,0:T(8,128)S(1)} %get-tuple-element.432) | copy-start | bytes 37748740
  96.8 2.4 collective-permute-start.2
  100.4 2.4 collective-permute-start.3
  100.9 20.6 %copy-start.149 = (f32[1536]{0:T(1024)}, f32[1536]{0:T(1024)S(1)}, u32[]{:S(2)}) copy-start(f32[1536]{0:T(1024)S(1)} %convert_element_type.352) | copy-start | bytes 18436
  103.2 18.2 %copy-start.53 = (bf16[512,768]{0,1:T(8,128)(2,1)}, bf16[512,768]{0,1:T(8,128)(2,1)S(1)}, u32[]{:S(2)}) copy-start(bf16[512,768]{0,1:T(8,128)(2,1)S(1)} %get-tuple-element.379) | copy-start | bytes 2359300
  103.3 18.2 %copy-start.55 = (bf16[512,768]{0,1:T(8,128)(2,1)}, bf16[512,768]{0,1:T(8,128)(2,1)S(1)}, u32[]{:S(2)}) copy-start(bf16[512,768]{0,1:T(8,128)(2,1)S(1)} %get-tuple-element.380) | copy-start | bytes 2359300
  103.3 18.2 %copy-start.167 = (bf16[1536,768]{1,0:T(8,128)(2,1)S(1)}, bf16[1536,768]{1,0:T(8,128)(2,1)}, u32[]{:S(2)}) copy-start(bf16[1536,768]{1,0:T(8,128)(2,1)} %param.90) | copy-start | bytes 7077892
  121.5 3.8 copy-start.177
  121.5 4.2 %copy-start.160 = (bf16[768]{0:T(1024)(128)(2,1)S(1)}, bf16[768]{0:T(1024)(128)(2,1)}, u32[]{:S(2)}) copy-start(bf16[768]{0:T(1024)(128)(2,1)} %param.86) | copy-start | bytes 4612
  121.5 4.2 %copy-start.161 = (bf16[768]{0:T(1024)(128)(2,1)S(1)}, bf16[768]{0:T(1024)(128)(2,1)}, u32[]{:S(2)}) copy-start(bf16[768]{0:T(1024)(128)(2,1)} %param.87) | copy-start | bytes 4612
  121.5 4.8 %copy-start.162 = (bf16[768]{0:T(1024)(128)(2,1)S(1)}, bf16[768]{0:T(1024)(128)(2,1)}, u32[]{:S(2)}) copy-start(bf16[768]{0:T(1024)(128)(2,1)} %param.91) | copy-start | bytes 4612
  125.3 14.7 %collective-permute-start.4 = (bf16[1024,768]{0,1:T(8,128)(2,1)}, bf16[1024,768]{0,1:T(8,128)(2,1)}, u32[]{:S(2)}, u32[]{:S(2)}) collective-permute-start(bf16[1024,768]{0,1:T(8,128)(2,1)} %convolution_convert_fusion.5), channel_id=1, source_target_pairs={{0,1},{1,0},{2,3},{3,2},{4,5},{5,4},{6,7},{7,6},{8,9},{9,8},{10,11... | collective-permute-start | bytes 4718600 | tf_op jit(solution)/shard_map/ppermute | solution.py:164
  126.9 9.8 %copy-start.130 = (f32[6,256]{1,0:T(8,128)S(1)}, f32[6,256]{1,0:T(8,128)}, u32[]{:S(2)}) copy-start(f32[6,256]{1,0:T(8,128)} %copy-done.129) | copy-start | bytes 18436
  126.9 9.8 %copy-start.133 = (f32[6,256]{1,0:T(8,128)S(1)}, f32[6,256]{1,0:T(8,128)}, u32[]{:S(2)}) copy-start(f32[6,256]{1,0:T(8,128)} %copy-done.132) | copy-start | bytes 18436
  143.2 5.1 %slice-start.10 = ((s8[6291456]{0:T(1024)(128)(4,1)}), s8[4194304]{0:T(1024)(128)(4,1)S(1)}, s32[]{:S(2)}) async-start(s8[6291456]{0:T(1024)(128)(4,1)} %bitcast.371), calls=%async_computation.16 | async-start | bytes 8388608
  144.0 4.3 %slice-start.11 = ((s8[6291456]{0:T(1024)(128)(4,1)}), s8[2097152]{0:T(1024)(128)(4,1)S(1)}, s32[]{:S(2)}) async-start(s8[6291456]{0:T(1024)(128)(4,1)} %bitcast.371), calls=%async_computation.17 | async-start | bytes 4194304
  155.3 4.8 %copy-start.178 = (bf16[1024,1536]{1,0:T(8,128)(2,1)S(1)}, bf16[1024,1536]{1,0:T(8,128)(2,1)}, u32[]{:S(2)}) copy-start(bf16[1024,1536]{1,0:T(8,128)(2,1)} %copy-done.177) | copy-start | bytes 9437188
  158.0 4.9 %collective-permute-start.5 = (bf16[512,768]{0,1:T(8,128)(2,1)S(1)}, bf16[512,768]{0,1:T(8,128)(2,1)S(1)}, u32[]{:S(2)}, u32[]{:S(2)}) collective-permute-start(bf16[512,768]{0,1:T(8,128)(2,1)S(1)} %broadcast_select_fusion.7), channel_id=1, source_target_pairs={{0,1},{1,0},{2,3},{3,2},{4,5},{5,4},{6,7},{7,6},{8,9},{9,8},{10,11... | collective-permute-start | bytes 2359304 | tf_op jit(solution)/shard_map/ppermute | solution.py:164
  166.6 6.2 %collective-permute-start.6 = (bf16[512,768]{0,1:T(8,128)(2,1)}, bf16[512,768]{0,1:T(8,128)(2,1)}, u32[]{:S(2)}, u32[]{:S(2)}) collective-permute-start(bf16[512,768]{0,1:T(8,128)(2,1)} %add_convert_fusion.10), channel_id=1, source_target_pairs={{0,1},{1,0},{2,3},{3,2},{4,5},{5,4},{6,7},{7,6},{8,9},{9,8},{10,11... | collective-permute-start | bytes 2359304 | tf_op jit(solution)/shard_map/ppermute | solution.py:164
  179.2 7.2 %copy-start.29 = (bf16[1024,384]{0,1:T(8,128)(2,1)S(1)}, bf16[1024,384]{0,1:T(8,128)(2,1)}, u32[]{:S(2)}) copy-start(bf16[1024,384]{0,1:T(8,128)(2,1)} %copy-done.28) | copy-start | bytes 2359300
  179.2 11.2 %slice-start.3 = ((s8[12582912]{0:T(1024)(128)(4,1)}), s8[4194304]{0:T(1024)(128)(4,1)S(1)}, s32[]{:S(2)}) async-start(s8[12582912]{0:T(1024)(128)(4,1)} %bitcast.271), calls=%async_computation.9 | async-start | bytes 8388608
  179.2 11.2 %slice-start.4 = ((s8[12582912]{0:T(1024)(128)(4,1)}), s8[4194304]{0:T(1024)(128)(4,1)S(1)}, s32[]{:S(2)}) async-start(s8[12582912]{0:T(1024)(128)(4,1)} %bitcast.271), calls=%async_computation.10 | async-start | bytes 8388608
  186.4 4.0 %slice-start.5 = ((s8[12582912]{0:T(1024)(128)(4,1)}), s8[4194304]{0:T(1024)(128)(4,1)S(1)}, s32[]{:S(2)}) async-start(s8[12582912]{0:T(1024)(128)(4,1)} %bitcast.271), calls=%async_computation.11 | async-start | bytes 8388608
  190.4 12.1 %slice-start = ((s8[12582912]{0:T(1024)(128)(4,1)}), s8[4194304]{0:T(1024)(128)(4,1)S(1)}, s32[]{:S(2)}) async-start(s8[12582912]{0:T(1024)(128)(4,1)} %bitcast.269), calls=%async_computation.6 | async-start | bytes 8388608
  190.4 12.1 %slice-start.1 = ((s8[12582912]{0:T(1024)(128)(4,1)}), s8[4194304]{0:T(1024)(128)(4,1)S(1)}, s32[]{:S(2)}) async-start(s8[12582912]{0:T(1024)(128)(4,1)} %bitcast.269), calls=%async_computation.7 | async-start | bytes 8388608
  193.7 8.9 %slice-start.2 = ((s8[12582912]{0:T(1024)(128)(4,1)}), s8[4194304]{0:T(1024)(128)(4,1)S(1)}, s32[]{:S(2)}) async-start(s8[12582912]{0:T(1024)(128)(4,1)} %bitcast.269), calls=%async_computation.8 | async-start | bytes 8388608
  207.6 5.1 %copy-start.10 = (bf16[6,512,1024]{2,1,0:T(8,128)(2,1)S(1)}, bf16[6,512,1024]{2,1,0:T(8,128)(2,1)}, u32[]{:S(2)}) copy-start(bf16[6,512,1024]{2,1,0:T(8,128)(2,1)} %multiply_convert_fusion) | copy-start | bytes 18874372
  207.6 5.1 %copy-start.42 = (bf16[512,384]{0,1:T(8,128)(2,1)S(1)}, bf16[512,384]{0,1:T(8,128)(2,1)}, u32[]{:S(2)}) copy-start(bf16[512,384]{0,1:T(8,128)(2,1)} %copy-done.41) | copy-start | bytes 1179652
  217.6 5.3 %collective-permute-start.7 = (bf16[512,768]{0,1:T(8,128)(2,1)S(1)}, bf16[512,768]{0,1:T(8,128)(2,1)S(1)}, u32[]{:S(2)}, u32[]{:S(2)}) collective-permute-start(bf16[512,768]{0,1:T(8,128)(2,1)S(1)} %broadcast_select_fusion.4), channel_id=1, source_target_pairs={{0,1},{1,0},{2,3},{3,2},{4,5},{5,4},{6,7},{7,6},{8,9},{9,8},{10,11... | collective-permute-start | bytes 2359304 | tf_op jit(solution)/shard_map/ppermute | solution.py:164
  225.8 15.1 %collective-permute-start.8 = (bf16[512,768]{0,1:T(8,128)(2,1)S(1)}, bf16[512,768]{0,1:T(8,128)(2,1)}, u32[]{:S(2)}, u32[]{:S(2)}) collective-permute-start(bf16[512,768]{0,1:T(8,128)(2,1)S(1)} %add_convert_fusion.9), channel_id=1, source_target_pairs={{0,1},{1,0},{2,3},{3,2},{4,5},{5,4},{6,7},{7,6},{8,9},{9,8},{10,11... | collective-permute-start | bytes 2359304 | tf_op jit(solution)/shard_map/ppermute | solution.py:164
  227.8 11.9 %collective-permute-start.11 = (f32[3072]{0:T(1024)S(1)}, f32[3072]{0:T(1024)S(1)}, u32[]{:S(2)}, u32[]{:S(2)}) collective-permute-start(f32[3072]{0:T(1024)S(1)} %pad_maximum_fusion.18), channel_id=1, source_target_pairs={{0,1},{1,0},{2,3},{3,2},{4,5},{5,4},{6,7},{7,6},{8,9},{9,8},{10,11... | collective-permute-start | bytes 36872 | tf_op jit(solution)/shard_map/ppermute | solution.py:164
  234.5 6.4 %copy-start.17 = (f32[512,768]{0,1:T(8,128)S(1)}, f32[512,768]{0,1:T(8,128)}, u32[]{:S(2)}) copy-start(f32[512,768]{0,1:T(8,128)} %copy-done.16) | copy-start | bytes 4718596
  234.5 50.8 %all-to-all-start.2 = ((bf16[4,192,1536]{2,1,0:T(8,128)(2,1)}), bf16[4,192,1536]{2,1,0:T(8,128)(2,1)}, u32[]{:S(2)}, u32[]{:S(2)}) async-start(bf16[4,192,1536]{2,1,0:T(8,128)(2,1)} %bitcast.284), calls=%async_computation.2 | async-start | bytes 4718592 | tf_op jit(solution)/shard_map/all_to_all | solution.py:357
  247.2 5.1 %slice-start.8 = ((s8[4718592]{0:T(1024)(128)(4,1)}), s8[4194304]{0:T(1024)(128)(4,1)S(1)}, s32[]{:S(2)}) async-start(s8[4718592]{0:T(1024)(128)(4,1)} %bitcast.275), calls=%async_computation.14 | async-start | bytes 8388608
  255.5 6.2 %copy-start.33 = (bf16[6,256,768]{2,1,0:T(8,128)(2,1)}, bf16[6,256,768]{2,1,0:T(8,128)(2,1)S(1)}, u32[]{:S(2)}) copy-start(bf16[6,256,768]{2,1,0:T(8,128)(2,1)S(1)} %multiply_convert_fusion.4) | copy-start | bytes 7077892
  285.2 4.7 %copy-start.50 = (bf16[6,64,1024]{2,1,0:T(8,128)(2,1)S(1)}, bf16[6,64,1024]{2,1,0:T(8,128)(2,1)}, u32[]{:S(2)}) copy-start(bf16[6,64,1024]{2,1,0:T(8,128)(2,1)} %get-tuple-element.437) | copy-start | bytes 2359300
  285.2 4.7 %copy-start.112 = (bf16[768,384]{1,0:T(8,128)(2,1)S(1)}, bf16[768,384]{1,0:T(8,128)(2,1)}, u32[]{:S(2)}) copy-start(bf16[768,384]{1,0:T(8,128)(2,1)} %param.78) | copy-start | bytes 1769476
  285.2 37.1 %all-to-all-start = ((bf16[4,206,1536]{2,1,0:T(8,128)(2,1)}), bf16[4,206,1536]{2,1,0:T(8,128)(2,1)}, u32[]{:S(2)}, u32[]{:S(2)}) async-start(bf16[4,206,1536]{2,1,0:T(8,128)(2,1)} %pad_maximum_fusion.1), calls=%async_computation | async-start | bytes 5111808 | tf_op jit(solution)/shard_map/all_to_all | solution.py:357
  293.8 60.1 %collective-permute-start.10 = (bf16[512,768]{0,1:T(8,128)(2,1)}, bf16[512,768]{0,1:T(8,128)(2,1)}, u32[]{:S(2)}, u32[]{:S(2)}) collective-permute-start(bf16[512,768]{0,1:T(8,128)(2,1)} %broadcast_select_fusion), channel_id=1, source_target_pairs={{0,1},{1,0},{2,3},{3,2},{4,5},{5,4},{6,7},{7,6},{8,9},{9,8},{10,11... | collective-permute-start | bytes 2359304 | tf_op jit(solution)/shard_map/ppermute | solution.py:164
  298.3 4.1 %copy-start.23 = (bf16[1024,768]{0,1:T(8,128)(2,1)}, bf16[1024,768]{0,1:T(8,128)(2,1)S(1)}, u32[]{:S(2)}) copy-start(bf16[1024,768]{0,1:T(8,128)(2,1)S(1)} %add_convert_fusion.2) | copy-start | bytes 4718596
  299.4 60.3 %collective-permute-start.9 = (bf16[512,768]{0,1:T(8,128)(2,1)}, bf16[512,768]{0,1:T(8,128)(2,1)}, u32[]{:S(2)}, u32[]{:S(2)}) collective-permute-start(bf16[512,768]{0,1:T(8,128)(2,1)} %broadcast_select_fusion.1), channel_id=1, source_target_pairs={{0,1},{1,0},{2,3},{3,2},{4,5},{5,4},{6,7},{7,6},{8,9},{9,8},{10,11... | collective-permute-start | bytes 2359304 | tf_op jit(solution)/shard_map/ppermute | solution.py:164
  322.4 24.4 %all-to-all-start.3 = ((bf16[4,48,1536]{2,1,0:T(8,128)(2,1)}), bf16[4,48,1536]{2,1,0:T(8,128)(2,1)S(1)}, u32[]{:S(2)}, u32[]{:S(2)}) async-start(bf16[4,48,1536]{2,1,0:T(8,128)(2,1)} %bitcast.97), calls=%async_computation.3 | async-start | bytes 1179648 | tf_op jit(solution)/shard_map/all_to_all | solution.py:372
  330.3 23.6 %copy-start.25 = (bf16[1024,768]{0,1:T(8,128)(2,1)S(1)}, bf16[1024,768]{0,1:T(8,128)(2,1)}, u32[]{:S(2)}) copy-start(bf16[1024,768]{0,1:T(8,128)(2,1)} %copy-done.24) | copy-start | bytes 4718596
  347.6 23.9 %all-to-all-start.1 = ((bf16[4,62,1536]{2,1,0:T(8,128)(2,1)}), bf16[4,62,1536]{2,1,0:T(8,128)(2,1)S(1)}, u32[]{:S(2)}, u32[]{:S(2)}) async-start(bf16[4,62,1536]{2,1,0:T(8,128)(2,1)} %pad_maximum_fusion.11), calls=%async_computation.1 | async-start | bytes 1572864 | tf_op jit(solution)/shard_map/all_to_all | solution.py:372
  365.8 11.8 %copy-start.1 = (bf16[768,1536]{1,0:T(8,128)(2,1)S(1)}, bf16[768,1536]{1,0:T(8,128)(2,1)}, u32[]{:S(2)}) copy-start(bf16[768,1536]{1,0:T(8,128)(2,1)} %param.88) | copy-start | bytes 7077892
  (144 other events, 264.8 us)
Sparse Core Ops, SparseCore 0:
  172.9 168.3 reduce-scatter.1
where the time goes:
time: 391 us; the launch traced here: 385 us
  matrix products  153 us (39%)
  local copies, waits for them, and re-layouts  74.3 us (19%)
  other arithmetic  74 us (19%)
  waiting for transfers between devices  44.8 us (11%)
  starting transfers between devices  21.9 us (6%)
  between operations  16.9 us (4%)
    dot_general x30, matrix products, project(): return jnp.dot(data, weight, preferred_element_type=jnp.float32)  69.7 us
    unnamed x387, local copies, waits for them, and re-layouts  36.1 us
    dot_general x6, matrix products, attend_backward(): jnp.einsum('qhe,khe->hqk', grad_piece, values[:end], preferred_element_ty...  22.1 us
    all_to_all x2, waiting for transfers between devices, exchange_sum(): second = lax.all_to_all(middle, 'outer', 0, 0, tiled=True)  20.1 us
    all_to_all x2, waiting for transfers between devices, exchange_sum(): first = lax.all_to_all(staged, 'inner', 0, 0, tiled=True)  20 us
    dot_general x6, matrix products, attend_forward(): jnp.einsum('hqk,khe->qhe', weights, values[:end], preferred_element_type=...  18.7 us
    reduce_sum x5, other arithmetic, attend_forward(): summed = jnp.sum(powers, -1, keepdims=True)  15.8 us
    dot_general x6, matrix products, attend_backward(): jnp.einsum('hqk,qhe->khe', probs.astype(jnp.bfloat16), grad_piece, prefer...  13.3 us
  transfers between devices with their start and end apart: 17, of which 6 were waited for; matrix products, arithmetic and copies ran while one was open for 40% of the time, Pallas kernels for 0%

commit v1 on v0

--- a/solution.py
+++ b/solution.py
@@ -369,8 +369,32 @@
             middle = jnp.concatenate(
                 [middle, jnp.broadcast_to(pair[None], (outer_size,) + pair.shape)], 1
             )
-        second = lax.all_to_all(middle, "outer", 0, 0, tiled=True)
-        return jnp.sum(second.astype(jnp.float32), 0)
+        if outer_size > 4:
+            second = lax.all_to_all(middle, "outer", 0, 0, tiled=True)
+            return jnp.sum(second.astype(jnp.float32), 0)
+        place = lax.axis_index("outer")
+        by_source = [None] * outer_size
+        for shift in range(outer_size):
+            piece = lax.dynamic_index_in_dim(
+                middle, (place + shift) % outer_size, 0, keepdims=False
+            )
+            if shift:
+                piece = lax.ppermute(
+                    piece,
+                    "outer",
+                    [(peer, (peer + shift) % outer_size) for peer in range(outer_size)],
+                )
+            by_source[shift] = piece
+        total = None
+        for source in range(outer_size):
+            chosen = by_source[0]
+            for shift in range(1, outer_size):
+                chosen = jnp.where(
+                    (place - shift) % outer_size == source, by_source[shift], chosen
+                )
+            chosen = chosen.astype(jnp.float32)
+            total = chosen if total is None else total + chosen
+        return total
 
     ffn = [grad_inner_weight, grad_outer_weight_t]
     ffn_sum = lax.psum_scatter(

time: 391 us -> 375 us (0.959)
  waiting for transfers between devices: 44.8 us -> 38.1 us
  local copies, waits for them, and re-layouts: 74.3 us -> 68 us
  matrix products: 153 us -> 148 us
    ppermute x0 -> x6, waiting for transfers between devices: none -> 26 us  [exchange_sum(): lax.ppermute(piece, 'outer', [(peer, (peer + shift) % outer_size) for pee...]
    all_to_all x2 -> x0, waiting for transfers between devices: 20.1 us -> none  [exchange_sum(): second = lax.all_to_all(middle, 'outer', 0, 0, tiled=True)]
    all_to_all x2, waiting for transfers between devices: 20 us -> 7.35 us  [exchange_sum(): first = lax.all_to_all(staged, 'inner', 0, 0, tiled=True)]
    ppermute x0 -> x6, starting transfers between devices: none -> 11 us  [exchange_sum(): lax.ppermute(piece, 'outer', [(peer, (peer + shift) % outer_size) for pee...]
    all_to_all x2 -> x0, starting transfers between devices: 8.35 us -> none  [exchange_sum(): second = lax.all_to_all(middle, 'outer', 0, 0, tiled=True)]
    unnamed x387 -> x375, local copies, waits for them, and re-layouts: 36.1 us -> 30.3 us
  transfers between devices with their start and end apart: 17 -> 21, of which waited for: 6 -> 8; matrix products, arithmetic and copies ran while one was open for 40% -> 40% of each run, Pallas kernels for 0% -> 0%
where the time goes in v1:
time: 375 us; the launch traced here: 369 us
  matrix products  148 us (39%)
  other arithmetic  72.9 us (19%)
  local copies, waits for them, and re-layouts  68 us (18%)
  waiting for transfers between devices  38.1 us (10%)
  starting transfers between devices  25.1 us (7%)
  between operations  17.1 us (5%)
    dot_general x30, matrix products, project(): return jnp.dot(data, weight, preferred_element_type=jnp.float32)  71.8 us
    unnamed x375, local copies, waits for them, and re-layouts  30.3 us
    ppermute x6, waiting for transfers between devices, exchange_sum(): lax.ppermute(piece, 'outer', [(peer, (peer + shift) % outer_size) for pee...  26 us
    dot_general x6, matrix products, attend_backward(): jnp.einsum('qhe,khe->hqk', grad_piece, values[:end], preferred_element_ty...  19.3 us
    dot_general x6, matrix products, attend_forward(): jnp.einsum('hqk,khe->qhe', weights, values[:end], preferred_element_type=...  18.7 us
    reduce_sum x5, other arithmetic, attend_forward(): summed = jnp.sum(powers, -1, keepdims=True)  15.8 us
    dot_general x6, matrix products, attend_forward(): jnp.einsum('qhe,khe->hqk', piece, keys[:end], preferred_element_type=jnp....  13.2 us
    ppermute x6, starting transfers between devices, exchange_sum(): lax.ppermute(piece, 'outer', [(peer, (peer + shift) % outer_size) for pee...  11 us
  transfers between devices with their start and end apart: 21, of which 8 were waited for; matrix products, arithmetic and copies ran while one was open for 40% of the time, Pallas kernels for 0%

profile of v1, /device:TPU:0, one launch (start us, length us, event | category | flops | bytes accessed | tf_op | source)
XLA Modules:
  0.0 368.8 jit_solution(1359285627674170077)
XLA Ops:
  12.4 2.5 add_convert_fusion.8
  21.3 2.4 multiply_convert_fusion.8
  30.9 2.2 fusion.172
  36.5 2.4 fusion.171
  42.7 2.9 fusion.170
  48.0 1.8 slice_select_fusion
  53.9 2.9 fusion.161
  63.1 6.6 %select_reduce_fusion = (f32[6,512]{1,0:T(8,128)S(1)}, f32[6,512,1024]{2,1,0:T(8,128)}) fusion(pred[512,1024]{1,0:T(8,128)(4,1)S(1)} %get-tuple-element.366, bf16[512,6,64]{0,2,1:T(8,128)(2,1)S(1)} %bitcast.336, bf16[1024,6,64]{0,2,1:T(8,128)(2,1)S(1)} %bitcast.322), kind=kOutput, calls=%fused_computation.12 | convolution fusion | flops 408941568 | bytes 14299136 | tf_op jit(solution)/shard_map/qhe,khe->hqk/dot_general | solution.py:54
  69.8 2.1 select_reduce_fusion.1
  71.9 12.1 %fusion = (f32[6,512]{1,0:T(8,128)S(1)}, f32[6,512]{1,0:T(8,128)S(1)}) fusion(f32[6,512,1024]{2,1,0:T(8,128)S(1)} %get-tuple-element.384, f32[6,512]{1,0:T(8,128)S(1)} %get-tuple-element.383, pred[512,1024]{1,0:T(8,128)(4,1)S(1)} %get-tuple-element.365, f32[6,512]{1,0:T(8,128)S(1)} %get-tuple-element.381, f32[6,512,1024]{2,1,0:T(8,128)} %get-tuple-element.382, ...), kind=kLoop, calls=%fused_computation.8 | loop fusion | flops 18868224 | bytes 26263552 | tf_op jit(solution)/shard_map/reduce_sum | solution.py:64
  84.0 6.9 %fusion.82 = f32[512,6,64]{0,2,1:T(8,128)S(1)} fusion(bf16[1024,6,64]{0,2,1:T(8,128)(2,1)S(1)} %bitcast.415, f32[6,512,1024]{2,1,0:T(8,128)} %get-tuple-element.382, f32[6,512]{1,0:T(8,128)S(1)} %get-tuple-element.401, f32[6,512]{1,0:T(8,128)S(1)} %get-tuple-element.381, pred[512,1024]{1,0:T(8,128)(4,1)S(1)} %get-tuple-element.366), kind=kOutput, calls=%fused_computation.184 | convolution fusion | flops 415236096 | bytes 14704640 | tf_op jit(solution)/shard_map/hqk,khe->qhe/dot_general | solution.py:67
  90.9 3.2 fusion.83
  97.3 1.9 collective-permute-done.2
  100.9 1.9 collective-permute-done.3
  103.3 18.2 %multiply_convert_fusion.3 = (bf16[1024,1536]{1,0:T(8,128)(2,1)S(1)}, f32[1024,1536]{1,0:T(8,128)}, f32[1024,1536]{1,0:T(8,128)}) fusion(f32[1536]{0:T(1024)S(1)} %convert_element_type.370, bf16[768,1536]{1,0:T(8,128)(2,1)S(1)} %copy-done, bf16[512,768]{0,1:T(8,128)(2,1)S(1)} %get-tuple-element.326, bf16[512,768]{0,1:T(8,128)(2,1)S(1)} %get-tuple-element.325), kind=kOutput, calls=%fused_computation.24 | convolution fusion | flops 2522873856 | bytes 19666944 | tf_op jit(solution)/shard_map/dot_general | solution.py:25
  121.6 3.8 %convolution_convert_fusion.5 = bf16[1024,768]{0,1:T(8,128)(2,1)} fusion(bf16[1024,1536]{1,0:T(8,128)(2,1)S(1)} %get-tuple-element.314, bf16[1536,768]{1,0:T(8,128)(2,1)S(1)} %copy-done.160), kind=kOutput, calls=%fused_computation.101 | convolution fusion | flops 2416705536 | bytes 7077888 | tf_op jit(solution)/shard_map/dot_general | solution.py:25
  126.9 1.8 copy.96
  128.7 2.7 copy.81
  131.4 1.7 copy.97
  133.1 1.8 copy.98
  134.9 1.8 copy.99
  139.4 3.2 fusion.158
  145.0 2.7 convert_reduce_fusion.3
  147.7 7.0 %convert_reduce_fusion = (f32[1536]{0:T(1024)S(1)}, bf16[1024,1536]{1,0:T(8,128)(2,1)S(1)}) fusion(f32[1024,1536]{1,0:T(8,128)S(1)} %bitcast.420, bf16[1536,768]{1,0:T(8,128)(2,1)S(1)} %copy-done.161, f32[1024,768]{0,1:T(8,128)S(1)} %get-tuple-element.306, f32[1024,1536]{1,0:T(8,128)} %get-tuple-element.385, f32[1536]{0:T(1024)S(1)} %copy-done.144), kind=kOutput, calls=%fused_computation.18 | convolution fusion | flops 2443442688 | bytes 21245952 | tf_op jit(solution)/shard_map/dot_general | solution.py:25
  154.7 2.6 convolution_convert_fusion.4
  159.5 2.8 convolution_convert_fusion
  165.8 3.0 convolution_convert_fusion.1
  168.8 2.8 pad_maximum_fusion
  176.6 7.1 %multiply_convert_fusion.1 = bf16[6,512,1024]{2,1,0:T(8,128)(2,1)S(1)} fusion(f32[6,512,1024]{2,1,0:T(8,128)} %copy-done.2, f32[6,512]{1,0:T(8,128)S(1)} %get-tuple-element.360, f32[6,512]{1,0:T(8,128)S(1)} %log_add_fusion.1, pred[512,1024]{1,0:T(8,128)(4,1)S(1)} %get-tuple-element.365, bf16[512,6,64]{0,2,1:T(8,128)(2,1)S(1)} %bitcast.390, ...), kind=kOutput, calls=%fused_computation.2 | convolution fusion | flops 418381824 | bytes 20602880 | tf_op jit(solution)/shard_map/qhe,khe->hqk/dot_general | solution.py:95
  183.7 2.0 convolution_convert_fusion.19
  187.0 2.9 fusion.5
  189.9 6.1 %multiply_convert_fusion = bf16[6,512,1024]{2,1,0:T(8,128)(2,1)S(1)} fusion(f32[6,512,1024]{2,1,0:T(8,128)S(1)} %bitcast.317, f32[6,512]{1,0:T(8,128)S(1)} %get-tuple-element.359, f32[6,512]{1,0:T(8,128)S(1)} %log_add_fusion, pred[512,1024]{1,0:T(8,128)(4,1)S(1)} %get-tuple-element.366, bf16[512,6,64]{0,2,1:T(8,128)(2,1)S(1)} %bitcast.393, ...), kind=kOutput, calls=%fused_computation | convolution fusion | flops 418381824 | bytes 20602880 | tf_op jit(solution)/shard_map/qhe,khe->hqk/dot_general | solution.py:95
  196.1 2.0 convolution_convert_fusion.18
  202.5 3.4 convert_reduce_fusion.6
  212.9 2.3 convolution_convert_fusion.17
  219.3 1.7 add_add_fusion.5
  225.8 2.9 copy.101
  230.4 5.2 %all-to-all-start.1 = ((bf16[4,192,1536]{2,1,0:T(8,128)(2,1)}), bf16[4,192,1536]{2,1,0:T(8,128)(2,1)}, u32[]{:S(2)}, u32[]{:S(2)}) async-start(bf16[4,192,1536]{2,1,0:T(8,128)(2,1)} %bitcast.329), calls=%async_computation.1 | async-start | bytes 4718592 | tf_op jit(solution)/shard_map/all_to_all | solution.py:357
  246.9 1.7 multiply_convert_fusion.4
  248.7 1.7 convert_reduce_fusion.8
  250.5 2.5 multiply_convert_fusion.2
  259.4 2.2 copy.94
  263.0 2.2 convolution_convert_fusion.21
  271.8 1.7 maximum_bitcast_fusion
  273.9 1.9 copy.100
  276.1 1.8 pad_maximum_fusion.1
  277.9 2.6 fusion.154
  280.5 2.6 fusion.176
  283.2 4.7 %all-to-all-start = ((bf16[4,206,1536]{2,1,0:T(8,128)(2,1)}), bf16[4,206,1536]{2,1,0:T(8,128)(2,1)}, u32[]{:S(2)}, u32[]{:S(2)}) async-start(bf16[4,206,1536]{2,1,0:T(8,128)(2,1)} %pad_maximum_fusion.1), calls=%async_computation | async-start | bytes 5111808 | tf_op jit(solution)/shard_map/all_to_all | solution.py:357
  287.9 3.8 %add_convert_fusion.2 = bf16[1024,768]{0,1:T(8,128)(2,1)S(1)} fusion(f32[1024,768]{0,1:T(8,128)} %fusion.154, f32[1024,768]{0,1:T(8,128)} %fusion.176, bf16[768,384]{1,0:T(8,128)(2,1)S(1)} %copy-done.108, bf16[1024,384]{0,1:T(8,128)(2,1)S(1)} %bitcast.347), kind=kOutput, calls=%fused_computation.73 | convolution fusion | flops 606339072 | bytes 9240576 | tf_op jit(solution)/shard_map/dot_general | solution.py:25
  292.0 2.8 copy.103
  294.9 1.9 convert_add_fusion
  298.4 2.4 reduce_sum.396
  301.6 2.2 collective-permute-start.17
  303.8 2.7 collective-permute-start.16
  308.0 3.2 add_add_fusion.4
  311.2 3.0 copy.104
  314.3 3.6 collective-permute-done.16
  318.0 7.3 %all-to-all-done = bf16[4,206,1536]{2,1,0:T(8,128)(2,1)} async-done(((bf16[4,206,1536]{2,1,0:T(8,128)(2,1)}), bf16[4,206,1536]{2,1,0:T(8,128)(2,1)}, u32[]{:S(2)}, u32[]{:S(2)}) %all-to-all-start) | async-done | bytes 2531360 | tf_op jit(solution)/shard_map/all_to_all | solution.py:357
  325.3 2.2 convert_reduce_fusion.1
  329.3 2.3 collective-permute-start.12
  333.0 5.1 %collective-permute-done.14 = bf16[62,1536]{1,0:T(8,128)(2,1)S(1)} collective-permute-done((bf16[62,1536]{1,0:T(8,128)(2,1)S(1)}, bf16[62,1536]{1,0:T(8,128)(2,1)S(1)}, u32[]{:S(2)}, u32[]{:S(2)}) %collective-permute-start.14) | collective-permute-done | bytes 190496 | tf_op jit(solution)/shard_map/ppermute | solution.py:382
  338.1 6.7 %collective-permute-done.12 = bf16[62,1536]{1,0:T(8,128)(2,1)S(1)} collective-permute-done((bf16[62,1536]{1,0:T(8,128)(2,1)S(1)}, bf16[62,1536]{1,0:T(8,128)(2,1)S(1)}, u32[]{:S(2)}, u32[]{:S(2)}) %collective-permute-start.12) | collective-permute-done | bytes 190496 | tf_op jit(solution)/shard_map/ppermute | solution.py:382
  344.8 10.6 %collective-permute-done.13 = bf16[62,1536]{1,0:T(8,128)(2,1)S(1)} collective-permute-done((bf16[62,1536]{1,0:T(8,128)(2,1)S(1)}, bf16[62,1536]{1,0:T(8,128)(2,1)S(1)}, u32[]{:S(2)}, u32[]{:S(2)}) %collective-permute-start.13) | collective-permute-done | bytes 190496 | tf_op jit(solution)/shard_map/ppermute | solution.py:382
  (577 shorter events, 122.8 us)
Async XLA Ops:
  7.2 96.1 %copy-start = (bf16[768,1536]{1,0:T(8,128)(2,1)S(1)}, bf16[768,1536]{1,0:T(8,128)(2,1)}, u32[]{:S(2)}) copy-start(bf16[768,1536]{1,0:T(8,128)(2,1)} %param.88) | copy-start | bytes 7077892
  7.2 351.1 %reduce-scatter.2.cloned.1.call-start = ((), (), s32[]{:S(2)}) async-start(), calls=%async_computation.3 | async-start | bytes 5013504 | tf_op jit(solution)/shard_map/reduce_scatter | solution.py:400
  12.4 4.9 %copy-start.106 = (bf16[768,384]{1,0:T(8,128)(2,1)S(1)}, bf16[768,384]{1,0:T(8,128)(2,1)}, u32[]{:S(2)}) copy-start(bf16[768,384]{1,0:T(8,128)(2,1)} %param.70) | copy-start | bytes 1769476
  12.4 4.9 %copy-start.113 = (bf16[1024,768]{1,0:T(8,128)(2,1)S(1)}, bf16[1024,768]{1,0:T(8,128)(2,1)}, u32[]{:S(2)}) copy-start(bf16[1024,768]{1,0:T(8,128)(2,1)} %param.64) | copy-start | bytes 4718596
  18.1 20.8 %copy-start.27 = (bf16[1024,384]{0,1:T(8,128)(2,1)}, bf16[1024,384]{0,1:T(8,128)(2,1)S(1)}, u32[]{:S(2)}) copy-start(bf16[1024,384]{0,1:T(8,128)(2,1)S(1)} %convolution_convert_fusion.9) | copy-start | bytes 2359300
  18.9 9.9 %copy-start.44 = (bf16[512,384]{0,1:T(8,128)(2,1)}, bf16[512,384]{0,1:T(8,128)(2,1)S(1)}, u32[]{:S(2)}) copy-start(bf16[512,384]{0,1:T(8,128)(2,1)S(1)} %slice.659) | copy-start | bytes 1179652
  25.7 16.1 %copy-start.42 = (pred[256,1024]{1,0:T(8,128)(4,1)}, pred[256,1024]{1,0:T(8,128)(4,1)S(1)}, u32[]{:S(2)}) copy-start(pred[256,1024]{1,0:T(8,128)(4,1)S(1)} %fusion.94) | copy-start | bytes 786436
  28.6 17.0 %copy-start.85 = (f32[256,6,64]{0,2,1:T(8,128)}, f32[256,6,64]{0,2,1:T(8,128)S(1)}, u32[]{:S(2)}) copy-start(f32[256,6,64]{0,2,1:T(8,128)S(1)} %get-tuple-element.399) | copy-start | bytes 1179652
  33.1 12.6 %copy-start.87 = (f32[256,6,64]{0,2,1:T(8,128)}, f32[256,6,64]{0,2,1:T(8,128)S(1)}, u32[]{:S(2)}) copy-start(f32[256,6,64]{0,2,1:T(8,128)S(1)} %get-tuple-element.397) | copy-start | bytes 1179652
  38.9 6.8 %copy-start.89 = (f32[256,6,64]{0,2,1:T(8,128)}, f32[256,6,64]{0,2,1:T(8,128)S(1)}, u32[]{:S(2)}) copy-start(f32[256,6,64]{0,2,1:T(8,128)S(1)} %get-tuple-element.395) | copy-start | bytes 1179652
  50.1 3.9 %collective-permute-start = (f32[512,768]{0,1:T(8,128)}, f32[512,768]{0,1:T(8,128)}, u32[]{:S(2)}, u32[]{:S(2)}) collective-permute-start(f32[512,768]{0,1:T(8,128)} %slice_select_fusion), channel_id=1, source_target_pairs={{0,1},{1,0},{2,3},{3,2},{4,5},{5,4},{6,7},{7,6},{8,9},{9,8},{10,11... | collective-permute-start | bytes 4718600 | tf_op jit(solution)/shard_map/ppermute | solution.py:164
  56.9 42.3 %copy-start.3 = (f32[512,768]{0,1:T(8,128)}, f32[512,768]{0,1:T(8,128)S(1)}, u32[]{:S(2)}) copy-start(f32[512,768]{0,1:T(8,128)S(1)} %get-tuple-element.319) | copy-start | bytes 4718596
  57.5 3.3 collective-permute-start.1
  59.9 9.9 %copy-start.25 = (bf16[1024,384]{0,1:T(8,128)(2,1)}, bf16[1024,384]{0,1:T(8,128)(2,1)S(1)}, u32[]{:S(2)}) copy-start(bf16[1024,384]{0,1:T(8,128)(2,1)S(1)} %convolution_convert_fusion.8) | copy-start | bytes 2359300
  60.8 30.1 %copy-start.169 = (bf16[1024,384]{0,1:T(8,128)(2,1)}, bf16[1024,384]{0,1:T(8,128)(2,1)S(1)}, u32[]{:S(2)}) copy-start(bf16[1024,384]{0,1:T(8,128)(2,1)S(1)} %add_convert_fusion.7) | copy-start | bytes 2359300
  63.1 6.7 %copy-start.38 = (bf16[512,384]{0,1:T(8,128)(2,1)}, bf16[512,384]{0,1:T(8,128)(2,1)S(1)}, u32[]{:S(2)}) copy-start(bf16[512,384]{0,1:T(8,128)(2,1)S(1)} %get-tuple-element.339) | copy-start | bytes 1179652
  63.1 6.7 %copy-start.40 = (bf16[512,384]{0,1:T(8,128)(2,1)}, bf16[512,384]{0,1:T(8,128)(2,1)S(1)}, u32[]{:S(2)}) copy-start(bf16[512,384]{0,1:T(8,128)(2,1)S(1)} %get-tuple-element.338) | copy-start | bytes 1179652
  71.9 19.0 %copy-start.2 = (f32[6,512,1024]{2,1,0:T(8,128)}, f32[6,512,1024]{2,1,0:T(8,128)S(1)}, u32[]{:S(2)}) copy-start(f32[6,512,1024]{2,1,0:T(8,128)S(1)} %get-tuple-element.384) | copy-start | bytes 37748740
  96.8 2.4 collective-permute-start.2
  100.4 2.4 collective-permute-start.3
  100.9 20.6 %copy-start.143 = (f32[1536]{0:T(1024)}, f32[1536]{0:T(1024)S(1)}, u32[]{:S(2)}) copy-start(f32[1536]{0:T(1024)S(1)} %convert_element_type.370) | copy-start | bytes 18436
  103.3 18.2 %copy-start.48 = (bf16[512,768]{0,1:T(8,128)(2,1)}, bf16[512,768]{0,1:T(8,128)(2,1)S(1)}, u32[]{:S(2)}) copy-start(bf16[512,768]{0,1:T(8,128)(2,1)S(1)} %get-tuple-element.325) | copy-start | bytes 2359300
  103.3 18.2 %copy-start.50 = (bf16[512,768]{0,1:T(8,128)(2,1)}, bf16[512,768]{0,1:T(8,128)(2,1)S(1)}, u32[]{:S(2)}) copy-start(bf16[512,768]{0,1:T(8,128)(2,1)S(1)} %get-tuple-element.326) | copy-start | bytes 2359300
  103.3 18.2 %copy-start.160 = (bf16[1536,768]{1,0:T(8,128)(2,1)S(1)}, bf16[1536,768]{1,0:T(8,128)(2,1)}, u32[]{:S(2)}) copy-start(bf16[1536,768]{1,0:T(8,128)(2,1)} %param.90) | copy-start | bytes 7077892
  121.6 4.8 %copy-start.155 = (bf16[768]{0:T(1024)(128)(2,1)S(1)}, bf16[768]{0:T(1024)(128)(2,1)}, u32[]{:S(2)}) copy-start(bf16[768]{0:T(1024)(128)(2,1)} %param.91) | copy-start | bytes 4612
  125.3 14.1 %collective-permute-start.4 = (bf16[1024,768]{0,1:T(8,128)(2,1)}, bf16[1024,768]{0,1:T(8,128)(2,1)}, u32[]{:S(2)}, u32[]{:S(2)}) collective-permute-start(bf16[1024,768]{0,1:T(8,128)(2,1)} %convolution_convert_fusion.5), channel_id=1, source_target_pairs={{0,1},{1,0},{2,3},{3,2},{4,5},{5,4},{6,7},{7,6},{8,9},{9,8},{10,11... | collective-permute-start | bytes 4718600 | tf_op jit(solution)/shard_map/ppermute | solution.py:164
  126.9 9.7 %copy-start.124 = (f32[6,256]{1,0:T(8,128)S(1)}, f32[6,256]{1,0:T(8,128)}, u32[]{:S(2)}) copy-start(f32[6,256]{1,0:T(8,128)} %copy-done.123) | copy-start | bytes 18436
  126.9 9.7 %copy-start.127 = (f32[6,256]{1,0:T(8,128)S(1)}, f32[6,256]{1,0:T(8,128)}, u32[]{:S(2)}) copy-start(f32[6,256]{1,0:T(8,128)} %copy-done.126) | copy-start | bytes 18436
  142.6 5.1 %slice-start.10 = ((s8[6291456]{0:T(1024)(128)(4,1)}), s8[4194304]{0:T(1024)(128)(4,1)S(1)}, s32[]{:S(2)}) async-start(s8[6291456]{0:T(1024)(128)(4,1)} %bitcast.419), calls=%async_computation.14 | async-start | bytes 8388608
  143.4 4.3 %slice-start.11 = ((s8[6291456]{0:T(1024)(128)(4,1)}), s8[2097152]{0:T(1024)(128)(4,1)S(1)}, s32[]{:S(2)}) async-start(s8[6291456]{0:T(1024)(128)(4,1)} %bitcast.419), calls=%async_computation.15 | async-start | bytes 4194304
  154.7 4.8 %copy-start.172 = (bf16[1024,1536]{1,0:T(8,128)(2,1)S(1)}, bf16[1024,1536]{1,0:T(8,128)(2,1)}, u32[]{:S(2)}) copy-start(bf16[1024,1536]{1,0:T(8,128)(2,1)} %copy-done.171) | copy-start | bytes 9437188
  157.5 4.9 %collective-permute-start.5 = (bf16[512,768]{0,1:T(8,128)(2,1)S(1)}, bf16[512,768]{0,1:T(8,128)(2,1)S(1)}, u32[]{:S(2)}, u32[]{:S(2)}) collective-permute-start(bf16[512,768]{0,1:T(8,128)(2,1)S(1)} %broadcast_select_fusion.7), channel_id=1, source_target_pairs={{0,1},{1,0},{2,3},{3,2},{4,5},{5,4},{6,7},{7,6},{8,9},{9,8},{10,11... | collective-permute-start | bytes 2359304 | tf_op jit(solution)/shard_map/ppermute | solution.py:164
  165.2 6.4 %collective-permute-start.6 = (bf16[512,768]{0,1:T(8,128)(2,1)S(1)}, bf16[512,768]{0,1:T(8,128)(2,1)}, u32[]{:S(2)}, u32[]{:S(2)}) collective-permute-start(bf16[512,768]{0,1:T(8,128)(2,1)S(1)} %add_convert_fusion.10), channel_id=1, source_target_pairs={{0,1},{1,0},{2,3},{3,2},{4,5},{5,4},{6,7},{7,6},{8,9},{9,8},{10,11... | collective-permute-start | bytes 2359304 | tf_op jit(solution)/shard_map/ppermute | solution.py:164
  174.3 36.1 %copy-start.58 = (bf16[512,768]{0,1:T(8,128)(2,1)}, bf16[512,768]{0,1:T(8,128)(2,1)S(1)}, u32[]{:S(2)}) copy-start(bf16[512,768]{0,1:T(8,128)(2,1)S(1)} %get-tuple-element.323) | copy-start | bytes 2359300
  174.3 36.1 %copy-start.60 = (bf16[512,768]{0,1:T(8,128)(2,1)}, bf16[512,768]{0,1:T(8,128)(2,1)S(1)}, u32[]{:S(2)}) copy-start(bf16[512,768]{0,1:T(8,128)(2,1)S(1)} %get-tuple-element.324) | copy-start | bytes 2359300
  176.5 7.2 %copy-start.26 = (bf16[1024,384]{0,1:T(8,128)(2,1)S(1)}, bf16[1024,384]{0,1:T(8,128)(2,1)}, u32[]{:S(2)}) copy-start(bf16[1024,384]{0,1:T(8,128)(2,1)} %copy-done.25) | copy-start | bytes 2359300
  176.5 10.4 %slice-start.3 = ((s8[12582912]{0:T(1024)(128)(4,1)}), s8[4194304]{0:T(1024)(128)(4,1)S(1)}, s32[]{:S(2)}) async-start(s8[12582912]{0:T(1024)(128)(4,1)} %bitcast.316), calls=%async_computation.7 | async-start | bytes 8388608
  176.5 10.5 %slice-start.4 = ((s8[12582912]{0:T(1024)(128)(4,1)}), s8[4194304]{0:T(1024)(128)(4,1)S(1)}, s32[]{:S(2)}) async-start(s8[12582912]{0:T(1024)(128)(4,1)} %bitcast.316), calls=%async_computation.8 | async-start | bytes 8388608
  185.8 20.1 %copy-start.83 = (bf16[6,64,512]{2,1,0:T(8,128)(2,1)}, bf16[6,64,512]{2,1,0:T(8,128)(2,1)S(1)}, u32[]{:S(2)}) copy-start(bf16[6,64,512]{2,1,0:T(8,128)(2,1)S(1)} %convolution_convert_fusion.19) | copy-start | bytes 1179652
  196.0 6.1 %slice-start = ((s8[12582912]{0:T(1024)(128)(4,1)}), s8[4194304]{0:T(1024)(128)(4,1)S(1)}, s32[]{:S(2)}) async-start(s8[12582912]{0:T(1024)(128)(4,1)} %bitcast.314), calls=%async_computation.4 | async-start | bytes 8388608
  198.1 4.4 %slice-start.2 = ((s8[12582912]{0:T(1024)(128)(4,1)}), s8[4194304]{0:T(1024)(128)(4,1)S(1)}, s32[]{:S(2)}) async-start(s8[12582912]{0:T(1024)(128)(4,1)} %bitcast.314), calls=%async_computation.6 | async-start | bytes 8388608
  208.0 10.0 %collective-permute-start.7 = (bf16[512,768]{0,1:T(8,128)(2,1)}, bf16[512,768]{0,1:T(8,128)(2,1)}, u32[]{:S(2)}, u32[]{:S(2)}) collective-permute-start(bf16[512,768]{0,1:T(8,128)(2,1)} %broadcast_select_fusion.4), channel_id=1, source_target_pairs={{0,1},{1,0},{2,3},{3,2},{4,5},{5,4},{6,7},{7,6},{8,9},{9,8},{10,11... | collective-permute-start | bytes 2359304 | tf_op jit(solution)/shard_map/ppermute | solution.py:164
  223.4 13.4 %collective-permute-start.8 = (bf16[512,768]{0,1:T(8,128)(2,1)}, bf16[512,768]{0,1:T(8,128)(2,1)}, u32[]{:S(2)}, u32[]{:S(2)}) collective-permute-start(bf16[512,768]{0,1:T(8,128)(2,1)} %add_convert_fusion.9), channel_id=1, source_target_pairs={{0,1},{1,0},{2,3},{3,2},{4,5},{5,4},{6,7},{7,6},{8,9},{9,8},{10,11... | collective-permute-start | bytes 2359304 | tf_op jit(solution)/shard_map/ppermute | solution.py:164
  224.7 10.9 %collective-permute-start.11 = (f32[3072]{0:T(1024)S(1)}, f32[3072]{0:T(1024)S(1)}, u32[]{:S(2)}, u32[]{:S(2)}) collective-permute-start(f32[3072]{0:T(1024)S(1)} %pad_maximum_fusion.17), channel_id=1, source_target_pairs={{0,1},{1,0},{2,3},{3,2},{4,5},{5,4},{6,7},{7,6},{8,9},{9,8},{10,11... | collective-permute-start | bytes 36872 | tf_op jit(solution)/shard_map/ppermute | solution.py:164
  225.7 69.2 %collective-permute-start.10 = (bf16[512,768]{0,1:T(8,128)(2,1)}, bf16[512,768]{0,1:T(8,128)(2,1)}, u32[]{:S(2)}, u32[]{:S(2)}) collective-permute-start(bf16[512,768]{0,1:T(8,128)(2,1)} %broadcast_select_fusion), channel_id=1, source_target_pairs={{0,1},{1,0},{2,3},{3,2},{4,5},{5,4},{6,7},{7,6},{8,9},{9,8},{10,11... | collective-permute-start | bytes 2359304 | tf_op jit(solution)/shard_map/ppermute | solution.py:164
  230.4 6.4 %copy-start.16 = (f32[512,768]{0,1:T(8,128)S(1)}, f32[512,768]{0,1:T(8,128)}, u32[]{:S(2)}) copy-start(f32[512,768]{0,1:T(8,128)} %copy-done.15) | copy-start | bytes 4718596
  230.4 52.8 %all-to-all-start.1 = ((bf16[4,192,1536]{2,1,0:T(8,128)(2,1)}), bf16[4,192,1536]{2,1,0:T(8,128)(2,1)}, u32[]{:S(2)}, u32[]{:S(2)}) async-start(bf16[4,192,1536]{2,1,0:T(8,128)(2,1)} %bitcast.329), calls=%async_computation.1 | async-start | bytes 4718592 | tf_op jit(solution)/shard_map/all_to_all | solution.py:357
  244.4 9.4 %copy-start.33 = (bf16[6,256,512]{2,1,0:T(8,128)(2,1)}, bf16[6,256,512]{2,1,0:T(8,128)(2,1)S(1)}, u32[]{:S(2)}) copy-start(bf16[6,256,512]{2,1,0:T(8,128)(2,1)S(1)} %multiply_convert_fusion.5) | copy-start | bytes 4718596
  248.6 6.0 %copy-start.29 = (bf16[6,256,768]{2,1,0:T(8,128)(2,1)}, bf16[6,256,768]{2,1,0:T(8,128)(2,1)S(1)}, u32[]{:S(2)}) copy-start(bf16[6,256,768]{2,1,0:T(8,128)(2,1)S(1)} %multiply_convert_fusion.4) | copy-start | bytes 7077892
  258.3 4.6 %copy-start.45 = (bf16[512,384]{0,1:T(8,128)(2,1)S(1)}, bf16[512,384]{0,1:T(8,128)(2,1)}, u32[]{:S(2)}) copy-start(bf16[512,384]{0,1:T(8,128)(2,1)} %copy-done.44) | copy-start | bytes 1179652
  259.4 5.8 %copy-start.37 = (bf16[768,384]{0,1:T(8,128)(2,1)S(1)}, bf16[768,384]{0,1:T(8,128)(2,1)}, u32[]{:S(2)}) copy-start(bf16[768,384]{0,1:T(8,128)(2,1)} %slice.662) | copy-start | bytes 1769476
  262.9 6.4 %copy-start.71 = (bf16[6,64,256]{2,1,0:T(8,128)(2,1)}, bf16[6,64,256]{2,1,0:T(8,128)(2,1)S(1)}, u32[]{:S(2)}) copy-start(bf16[6,64,256]{2,1,0:T(8,128)(2,1)S(1)} %convolution_convert_fusion.23) | copy-start | bytes 589828
  283.2 4.7 %copy-start.53 = (bf16[1024,6,64]{0,2,1:T(8,128)(2,1)S(1)}, bf16[1024,6,64]{0,2,1:T(8,128)(2,1)}, u32[]{:S(2)}) copy-start(bf16[1024,6,64]{0,2,1:T(8,128)(2,1)} %copy-done.52) | copy-start | bytes 2359300
  283.2 4.7 %copy-start.108 = (bf16[768,384]{1,0:T(8,128)(2,1)S(1)}, bf16[768,384]{1,0:T(8,128)(2,1)}, u32[]{:S(2)}) copy-start(bf16[768,384]{1,0:T(8,128)(2,1)} %param.71) | copy-start | bytes 1769476
  283.2 42.2 %all-to-all-start = ((bf16[4,206,1536]{2,1,0:T(8,128)(2,1)}), bf16[4,206,1536]{2,1,0:T(8,128)(2,1)}, u32[]{:S(2)}, u32[]{:S(2)}) async-start(bf16[4,206,1536]{2,1,0:T(8,128)(2,1)} %pad_maximum_fusion.1), calls=%async_computation | async-start | bytes 5111808 | tf_op jit(solution)/shard_map/all_to_all | solution.py:357
  291.8 16.2 %collective-permute-start.9 = (bf16[512,768]{0,1:T(8,128)(2,1)S(1)}, bf16[512,768]{0,1:T(8,128)(2,1)}, u32[]{:S(2)}, u32[]{:S(2)}) collective-permute-start(bf16[512,768]{0,1:T(8,128)(2,1)S(1)} %broadcast_select_fusion.1), channel_id=1, source_target_pairs={{0,1},{1,0},{2,3},{3,2},{4,5},{5,4},{6,7},{7,6},{8,9},{9,8},{10,11... | collective-permute-start | bytes 2359304 | tf_op jit(solution)/shard_map/ppermute | solution.py:164
  298.4 9.6 %copy-start.17 = (f32[512,768]{0,1:T(8,128)S(1)}, f32[512,768]{0,1:T(8,128)}, u32[]{:S(2)}) copy-start(f32[512,768]{0,1:T(8,128)} %copy-done.15) | copy-start | bytes 4718596
  301.6 12.7 %collective-permute-start.17 = (bf16[48,1536]{1,0:T(8,128)(2,1)}, bf16[48,1536]{1,0:T(8,128)(2,1)S(1)}, u32[]{:S(2)}, u32[]{:S(2)}) collective-permute-start(bf16[48,1536]{1,0:T(8,128)(2,1)} %get-tuple-element.344), channel_id=1, source_target_pairs={{0,8},{8,16},{16,24},{24,0},{1,9},{9,17},{17,25},{25,1},{2,10},{10... | collective-permute-start | bytes 442376 | tf_op jit(solution)/shard_map/ppermute | solution.py:382
  303.8 14.1 %collective-permute-start.16 = (bf16[48,1536]{1,0:T(8,128)(2,1)}, bf16[48,1536]{1,0:T(8,128)(2,1)S(1)}, u32[]{:S(2)}, u32[]{:S(2)}) collective-permute-start(bf16[48,1536]{1,0:T(8,128)(2,1)} %get-tuple-element.345), channel_id=1, source_target_pairs={{0,16},{8,24},{16,0},{24,8},{1,17},{9,25},{17,1},{25,9},{2,18},{10... | collective-permute-start | bytes 442376 | tf_op jit(solution)/shard_map/ppermute | solution.py:382
  306.5 11.4 %collective-permute-start.15 = (bf16[48,1536]{1,0:T(8,128)(2,1)}, bf16[48,1536]{1,0:T(8,128)(2,1)S(1)}, u32[]{:S(2)}, u32[]{:S(2)}) collective-permute-start(bf16[48,1536]{1,0:T(8,128)(2,1)} %get-tuple-element.346), channel_id=1, source_target_pairs={{0,24},{8,0},{16,8},{24,16},{1,25},{9,1},{17,9},{25,17},{2,26},{10... | collective-permute-start | bytes 442376 | tf_op jit(solution)/shard_map/ppermute | solution.py:382
  327.8 10.3 %collective-permute-start.14 = (bf16[62,1536]{1,0:T(8,128)(2,1)S(1)}, bf16[62,1536]{1,0:T(8,128)(2,1)S(1)}, u32[]{:S(2)}, u32[]{:S(2)}) collective-permute-start(bf16[62,1536]{1,0:T(8,128)(2,1)S(1)} %get-tuple-element.329), channel_id=1, source_target_pairs={{0,8},{8,16},{16,24},{24,0},{1,9},{9,17},{17,25},{25,1},{2,10},{10... | collective-permute-start | bytes 571400 | tf_op jit(solution)/shard_map/ppermute | solution.py:382
  329.3 15.4 %collective-permute-start.12 = (bf16[62,1536]{1,0:T(8,128)(2,1)S(1)}, bf16[62,1536]{1,0:T(8,128)(2,1)S(1)}, u32[]{:S(2)}, u32[]{:S(2)}) collective-permute-start(bf16[62,1536]{1,0:T(8,128)(2,1)S(1)} %get-tuple-element.330), channel_id=1, source_target_pairs={{0,24},{8,0},{16,8},{24,16},{1,25},{9,1},{17,9},{25,17},{2,26},{10... | collective-permute-start | bytes 571400 | tf_op jit(solution)/shard_map/ppermute | solution.py:382
  331.7 23.7 %collective-permute-start.13 = (bf16[62,1536]{1,0:T(8,128)(2,1)S(1)}, bf16[62,1536]{1,0:T(8,128)(2,1)S(1)}, u32[]{:S(2)}, u32[]{:S(2)}) collective-permute-start(bf16[62,1536]{1,0:T(8,128)(2,1)S(1)} %get-tuple-element.331), channel_id=1, source_target_pairs={{0,16},{8,24},{16,0},{24,8},{1,17},{9,25},{17,1},{25,9},{2,18},{10... | collective-permute-start | bytes 571400 | tf_op jit(solution)/shard_map/ppermute | solution.py:382
  332.3 29.4 %copy-start.1 = (bf16[768,1536]{1,0:T(8,128)(2,1)S(1)}, bf16[768,1536]{1,0:T(8,128)(2,1)}, u32[]{:S(2)}) copy-start(bf16[768,1536]{1,0:T(8,128)(2,1)} %param.88) | copy-start | bytes 7077892
  (142 other events, 298.8 us)
Sparse Core Ops, SparseCore 0:
  171.7 180.5 reduce-scatter.1

commit v2 on v1

--- a/solution.py
+++ b/solution.py
@@ -354,8 +354,26 @@
             staged = jnp.concatenate(
                 [staged, jnp.broadcast_to(extra[None], (inner_size,) + extra.shape)], 1
             )
-        first = lax.all_to_all(staged, "inner", 0, 0, tiled=True)
-        partial = jnp.sum(first.astype(jnp.float32), 0)
+        if inner_size == 4:
+            spot = lax.axis_index("inner")
+            swapped = []
+            for mask in range(inner_size):
+                piece = lax.dynamic_index_in_dim(staged, spot ^ mask, 0, keepdims=False)
+                if mask:
+                    piece = lax.ppermute(
+                        piece, "inner", [(peer, peer ^ mask) for peer in range(inner_size)]
+                    )
+                swapped.append(piece)
+            partial = None
+            for source in range(inner_size):
+                chosen = swapped[0]
+                for mask in range(1, inner_size):
+                    chosen = jnp.where(spot ^ mask == source, swapped[mask], chosen)
+                chosen = chosen.astype(jnp.float32)
+                partial = chosen if partial is None else partial + chosen
+        else:
+            first = lax.all_to_all(staged, "inner", 0, 0, tiled=True)
+            partial = jnp.sum(first.astype(jnp.float32), 0)
         middle = partial[: outer_size * rows].astype(jnp.bfloat16).reshape(
             outer_size, rows, width
         )

time: 375 us -> 411 us (1.096)
  waiting for transfers between devices: 38.1 us -> 67.8 us
  other arithmetic: 72.9 us -> 68.3 us
    ppermute x0 -> x6, waiting for transfers between devices: none -> 47.4 us  [exchange_sum(): lax.ppermute(piece, 'inner', [(peer, peer ^ mask) for peer in range(inner...]
    ppermute x6, waiting for transfers between devices: 26 us -> 15.6 us  [exchange_sum(): lax.ppermute(piece, 'outer', [(peer, (peer + shift) % outer_size) for pee...]
    all_to_all x2 -> x0, starting transfers between devices: 9.88 us -> none  [exchange_sum(): first = lax.all_to_all(staged, 'inner', 0, 0, tiled=True)]
    ppermute x0 -> x6, starting transfers between devices: none -> 7.79 us  [exchange_sum(): lax.ppermute(piece, 'inner', [(peer, peer ^ mask) for peer in range(inner...]
    all_to_all x2 -> x0, waiting for transfers between devices: 7.35 us -> none  [exchange_sum(): first = lax.all_to_all(staged, 'inner', 0, 0, tiled=True)]
    ppermute x6, starting transfers between devices: 11 us -> 16.6 us  [exchange_sum(): lax.ppermute(piece, 'outer', [(peer, (peer + shift) % outer_size) for pee...]
    reduce_sum x2 -> x0, other arithmetic: 4.61 us -> none  [exchange_sum(): partial = jnp.sum(first.astype(jnp.float32), 0)]
    unnamed x375 -> x377, local copies, waits for them, and re-layouts: 30.3 us -> 32.1 us
  transfers between devices with their start and end apart: 21 -> 25, of which waited for: 8 -> 13; matrix products, arithmetic and copies ran while one was open for 40% -> 37% of each run, Pallas kernels for 0% -> 0%
where the time goes in v2:
time: 411 us; the launch traced here: 405 us
  matrix products  152 us (37%)
  local copies, waits for them, and re-layouts  71.3 us (17%)
  other arithmetic  68.3 us (17%)
  waiting for transfers between devices  67.8 us (16%)
  starting transfers between devices  28.3 us (7%)
  between operations  17 us (4%)
    dot_general x30, matrix products, project(): return jnp.dot(data, weight, preferred_element_type=jnp.float32)  71.6 us
    ppermute x6, waiting for transfers between devices, exchange_sum(): lax.ppermute(piece, 'inner', [(peer, peer ^ mask) for peer in range(inner...  47.4 us
    unnamed x377, local copies, waits for them, and re-layouts  32.1 us
    dot_general x6, matrix products, attend_backward(): jnp.einsum('qhe,khe->hqk', grad_piece, values[:end], preferred_element_ty...  22.7 us
    dot_general x6, matrix products, attend_forward(): jnp.einsum('hqk,khe->qhe', weights, values[:end], preferred_element_type=...  18.7 us
    ppermute x6, starting transfers between devices, exchange_sum(): lax.ppermute(piece, 'outer', [(peer, (peer + shift) % outer_size) for pee...  16.6 us
    reduce_sum x5, other arithmetic, attend_forward(): summed = jnp.sum(powers, -1, keepdims=True)  15.8 us
    ppermute x6, waiting for transfers between devices, exchange_sum(): lax.ppermute(piece, 'outer', [(peer, (peer + shift) % outer_size) for pee...  15.6 us
  transfers between devices with their start and end apart: 25, of which 13 were waited for; matrix products, arithmetic and copies ran while one was open for 37% of the time, Pallas kernels for 0%

profile of v2, /device:TPU:0, one launch (start us, length us, event | category | flops | bytes accessed | tf_op | source)
XLA Modules:
  0.0 404.6 jit_solution(17675104141425249613)
XLA Ops:
  12.4 2.5 add_convert_fusion.8
  21.4 2.4 multiply_convert_fusion.8
  31.0 2.2 fusion.188
  36.6 2.4 fusion.187
  42.8 2.9 fusion.186
  48.1 1.8 slice_select_fusion
  54.1 2.9 fusion.177
  63.2 6.6 %select_reduce_fusion = (f32[6,512]{1,0:T(8,128)S(1)}, f32[6,512,1024]{2,1,0:T(8,128)}) fusion(pred[512,1024]{1,0:T(8,128)(4,1)S(1)} %get-tuple-element.372, bf16[512,6,64]{0,2,1:T(8,128)(2,1)S(1)} %bitcast.383, bf16[1024,6,64]{0,2,1:T(8,128)(2,1)S(1)} %bitcast.369), kind=kOutput, calls=%fused_computation.12 | convolution fusion | flops 408941568 | bytes 14299136 | tf_op jit(solution)/shard_map/qhe,khe->hqk/dot_general | solution.py:54
  69.8 2.1 select_reduce_fusion.1
  72.0 12.1 %fusion = (f32[6,512]{1,0:T(8,128)S(1)}, f32[6,512]{1,0:T(8,128)S(1)}) fusion(f32[6,512,1024]{2,1,0:T(8,128)S(1)} %get-tuple-element.390, f32[6,512]{1,0:T(8,128)S(1)} %get-tuple-element.389, pred[512,1024]{1,0:T(8,128)(4,1)S(1)} %get-tuple-element.371, f32[6,512]{1,0:T(8,128)S(1)} %get-tuple-element.387, f32[6,512,1024]{2,1,0:T(8,128)} %get-tuple-element.388, ...), kind=kLoop, calls=%fused_computation.8 | loop fusion | flops 18868224 | bytes 26263552 | tf_op jit(solution)/shard_map/reduce_sum | solution.py:64
  84.1 6.9 %fusion.82 = f32[512,6,64]{0,2,1:T(8,128)S(1)} fusion(bf16[1024,6,64]{0,2,1:T(8,128)(2,1)S(1)} %bitcast.462, f32[6,512,1024]{2,1,0:T(8,128)} %get-tuple-element.388, f32[6,512]{1,0:T(8,128)S(1)} %get-tuple-element.407, f32[6,512]{1,0:T(8,128)S(1)} %get-tuple-element.387, pred[512,1024]{1,0:T(8,128)(4,1)S(1)} %get-tuple-element.372), kind=kOutput, calls=%fused_computation.190 | convolution fusion | flops 415236096 | bytes 14704640 | tf_op jit(solution)/shard_map/hqk,khe->qhe/dot_general | solution.py:67
  91.0 3.2 fusion.83
  97.4 1.9 collective-permute-done.2
  101.0 1.9 collective-permute-done.3
  103.4 18.2 %multiply_convert_fusion.3 = (bf16[1024,1536]{1,0:T(8,128)(2,1)S(1)}, f32[1024,1536]{1,0:T(8,128)}, f32[1024,1536]{1,0:T(8,128)}) fusion(f32[1536]{0:T(1024)S(1)} %convert_element_type.392, bf16[768,1536]{1,0:T(8,128)(2,1)S(1)} %copy-done, bf16[512,768]{0,1:T(8,128)(2,1)S(1)} %get-tuple-element.332, bf16[512,768]{0,1:T(8,128)(2,1)S(1)} %get-tuple-element.331), kind=kOutput, calls=%fused_computation.24 | convolution fusion | flops 2522873856 | bytes 19666944 | tf_op jit(solution)/shard_map/dot_general | solution.py:25
  121.7 3.8 convolution_convert_fusion.5
  126.4 1.8 copy.96
  128.2 2.7 copy.81
  130.9 1.8 copy.97
  132.7 1.8 copy.98
  134.5 1.8 copy.99
  138.3 3.2 fusion.174
  143.9 2.7 convert_reduce_fusion.2
  146.6 6.9 %convert_reduce_fusion = (f32[1536]{0:T(1024)S(1)}, bf16[1024,1536]{1,0:T(8,128)(2,1)S(1)}) fusion(f32[1024,1536]{1,0:T(8,128)S(1)} %bitcast.467, bf16[1536,768]{1,0:T(8,128)(2,1)S(1)} %copy-done.162, f32[1024,768]{0,1:T(8,128)S(1)} %get-tuple-element.306, f32[1024,1536]{1,0:T(8,128)} %get-tuple-element.391, f32[1536]{0:T(1024)S(1)} %copy-done.145), kind=kOutput, calls=%fused_computation.18 | convolution fusion | flops 2443442688 | bytes 21245952 | tf_op jit(solution)/shard_map/dot_general | solution.py:25
  153.5 2.6 convolution_convert_fusion.4
  157.7 2.8 convolution_convert_fusion
  164.7 3.0 convolution_convert_fusion.1
  167.7 2.8 pad_maximum_fusion
  170.5 2.7 copy.103
  178.6 7.3 %multiply_convert_fusion.1 = bf16[6,512,1024]{2,1,0:T(8,128)(2,1)S(1)} fusion(f32[6,512,1024]{2,1,0:T(8,128)} %copy-done.2, f32[6,512]{1,0:T(8,128)S(1)} %get-tuple-element.366, f32[6,512]{1,0:T(8,128)S(1)} %log_add_fusion.1, pred[512,1024]{1,0:T(8,128)(4,1)S(1)} %get-tuple-element.371, bf16[512,6,64]{0,2,1:T(8,128)(2,1)S(1)} %bitcast.437, ...), kind=kOutput, calls=%fused_computation.2 | convolution fusion | flops 418381824 | bytes 20602880 | tf_op jit(solution)/shard_map/qhe,khe->hqk/dot_general | solution.py:95
  186.0 2.0 convolution_convert_fusion.19
  189.3 2.9 fusion.5
  192.2 6.1 %multiply_convert_fusion = bf16[6,512,1024]{2,1,0:T(8,128)(2,1)S(1)} fusion(f32[6,512,1024]{2,1,0:T(8,128)S(1)} %bitcast.362, f32[6,512]{1,0:T(8,128)S(1)} %get-tuple-element.365, f32[6,512]{1,0:T(8,128)S(1)} %log_add_fusion, pred[512,1024]{1,0:T(8,128)(4,1)S(1)} %get-tuple-element.372, bf16[512,6,64]{0,2,1:T(8,128)(2,1)S(1)} %bitcast.440, ...), kind=kOutput, calls=%fused_computation | convolution fusion | flops 418381824 | bytes 20602880 | tf_op jit(solution)/shard_map/qhe,khe->hqk/dot_general | solution.py:95
  198.3 2.0 convolution_convert_fusion.18
  200.6 2.1 convolution_convert_fusion.2
  205.8 2.6 fusion.193
  208.4 3.4 convert_reduce_fusion.5
  213.6 3.1 add_convert_fusion.1
  223.4 1.6 add_add_fusion.5
  225.1 4.4 %copy.101 = bf16[768,1536]{1,0:T(8,128)(2,1)} copy(bf16[768,1536]{0,1:T(8,128)(2,1)} %pad_maximum_fusion.1) | data formatting | bytes 4718592 | tf_op jit(solution)/shard_map/optimization_barrier | solution.py:290
  229.6 2.0 copy.102
  234.6 2.7 collective-permute-start.20
  241.2 2.6 convert_add_fusion
  243.8 3.0 copy.105
  246.9 8.9 %collective-permute-done.20 = bf16[192,1536]{1,0:T(8,128)(2,1)S(1)} collective-permute-done((bf16[192,1536]{1,0:T(8,128)(2,1)}, bf16[192,1536]{1,0:T(8,128)(2,1)S(1)}, u32[]{:S(2)}, u32[]{:S(2)}) %collective-permute-start.20) | collective-permute-done | bytes 589856 | tf_op jit(solution)/shard_map/ppermute | solution.py:363
  255.8 13.6 %collective-permute-done.19 = bf16[192,1536]{1,0:T(8,128)(2,1)} collective-permute-done((bf16[192,1536]{1,0:T(8,128)(2,1)}, bf16[192,1536]{1,0:T(8,128)(2,1)}, u32[]{:S(2)}, u32[]{:S(2)}) %collective-permute-start.19) | collective-permute-done | bytes 589856 | tf_op jit(solution)/shard_map/ppermute | solution.py:363
  270.6 2.1 add_convert_fusion.11
  274.3 2.2 collective-permute-start.22
  279.1 2.3 collective-permute-done.23
  281.4 5.2 %collective-permute-done.22 = bf16[48,1536]{1,0:T(8,128)(2,1)S(1)} collective-permute-done((bf16[48,1536]{1,0:T(8,128)(2,1)S(1)}, bf16[48,1536]{1,0:T(8,128)(2,1)S(1)}, u32[]{:S(2)}, u32[]{:S(2)}) %collective-permute-start.22) | collective-permute-done | bytes 147488 | tf_op jit(solution)/shard_map/ppermute | solution.py:400
  300.6 2.0 multiply_convert_fusion.4
  304.2 1.7 convert_reduce_fusion.7
  305.9 5.6 %multiply_convert_fusion.2 = bf16[6,256,1024]{2,1,0:T(8,128)(2,1)S(1)} fusion(f32[6,256,1024]{2,1,0:T(8,128)} %copy-done.5, f32[6,256]{1,0:T(8,128)S(1)} %get-tuple-element.362, f32[6,256]{1,0:T(8,128)S(1)} %log_add_fusion.2, pred[256,1024]{1,0:T(8,128)(4,1)S(1)} %copy-done.44, bf16[256,6,64]{0,2,1:T(8,128)(2,1)} %bitcast.446, ...), kind=kOutput, calls=%fused_computation.19 | convolution fusion | flops 209190912 | bytes 10694656 | tf_op jit(solution)/shard_map/qhe,khe->hqk/dot_general | solution.py:95
  316.1 2.2 copy.95
  318.2 2.1 fusion.75
  324.9 3.2 fusion.88
  334.9 1.7 collective-permute-start.13
  340.3 10.0 %collective-permute-done.14 = bf16[206,1536]{1,0:T(8,128)(2,1)S(1)} collective-permute-done((bf16[206,1536]{1,0:T(8,128)(2,1)S(1)}, bf16[206,1536]{1,0:T(8,128)(2,1)S(1)}, u32[]{:S(2)}, u32[]{:S(2)}) %collective-permute-start.14) | collective-permute-done | bytes 632864 | tf_op jit(solution)/shard_map/ppermute | solution.py:363
  350.4 12.4 %collective-permute-done.12 = bf16[206,1536]{1,0:T(8,128)(2,1)S(1)} collective-permute-done((bf16[206,1536]{1,0:T(8,128)(2,1)S(1)}, bf16[206,1536]{1,0:T(8,128)(2,1)S(1)}, u32[]{:S(2)}, u32[]{:S(2)}) %collective-permute-start.12) | collective-permute-done | bytes 632864 | tf_op jit(solution)/shard_map/ppermute | solution.py:363
  365.9 10.0 %collective-permute-start.17 = (bf16[62,1536]{1,0:T(8,128)(2,1)}, bf16[62,1536]{1,0:T(8,128)(2,1)S(1)}, u32[]{:S(2)}, u32[]{:S(2)}) collective-permute-start(bf16[62,1536]{1,0:T(8,128)(2,1)} %get-tuple-element.335), channel_id=1, source_target_pairs={{0,8},{8,16},{16,24},{24,0},{1,9},{9,17},{17,25},{25,1},{2,10},{10... | collective-permute-start | bytes 571400 | tf_op jit(solution)/shard_map/ppermute | solution.py:400
  377.3 1.7 add_add_fusion.4
  379.0 3.2 copy.104
  382.1 3.5 collective-permute-done.15
  385.6 4.7 %collective-permute-done.16 = bf16[62,1536]{1,0:T(8,128)(2,1)} collective-permute-done((bf16[62,1536]{1,0:T(8,128)(2,1)}, bf16[62,1536]{1,0:T(8,128)(2,1)}, u32[]{:S(2)}, u32[]{:S(2)}) %collective-permute-start.16) | collective-permute-done | bytes 190496 | tf_op jit(solution)/shard_map/ppermute | solution.py:400
  (588 shorter events, 131.2 us)
Async XLA Ops:
  7.2 96.2 %copy-start = (bf16[768,1536]{1,0:T(8,128)(2,1)S(1)}, bf16[768,1536]{1,0:T(8,128)(2,1)}, u32[]{:S(2)}) copy-start(bf16[768,1536]{1,0:T(8,128)(2,1)} %param.88) | copy-start | bytes 7077892
  7.2 386.9 %reduce-scatter.2.cloned.1.call-start = ((), (), s32[]{:S(2)}) async-start(), calls=%async_computation.1 | async-start | bytes 5013504 | tf_op jit(solution)/shard_map/reduce_scatter | solution.py:418
  12.4 4.9 %copy-start.112 = (bf16[1024,768]{1,0:T(8,128)(2,1)S(1)}, bf16[1024,768]{1,0:T(8,128)(2,1)}, u32[]{:S(2)}) copy-start(bf16[1024,768]{1,0:T(8,128)(2,1)} %param.64) | copy-start | bytes 4718596
  18.2 20.8 %copy-start.28 = (bf16[1024,384]{0,1:T(8,128)(2,1)}, bf16[1024,384]{0,1:T(8,128)(2,1)S(1)}, u32[]{:S(2)}) copy-start(bf16[1024,384]{0,1:T(8,128)(2,1)S(1)} %convolution_convert_fusion.9) | copy-start | bytes 2359300
  19.0 10.0 %copy-start.45 = (bf16[512,384]{0,1:T(8,128)(2,1)}, bf16[512,384]{0,1:T(8,128)(2,1)S(1)}, u32[]{:S(2)}) copy-start(bf16[512,384]{0,1:T(8,128)(2,1)S(1)} %slice.659) | copy-start | bytes 1179652
  25.8 16.1 %copy-start.43 = (pred[256,1024]{1,0:T(8,128)(4,1)}, pred[256,1024]{1,0:T(8,128)(4,1)S(1)}, u32[]{:S(2)}) copy-start(pred[256,1024]{1,0:T(8,128)(4,1)S(1)} %fusion.94) | copy-start | bytes 786436
  28.8 17.0 %copy-start.81 = (f32[256,6,64]{0,2,1:T(8,128)}, f32[256,6,64]{0,2,1:T(8,128)S(1)}, u32[]{:S(2)}) copy-start(f32[256,6,64]{0,2,1:T(8,128)S(1)} %get-tuple-element.405) | copy-start | bytes 1179652
  33.2 12.5 %copy-start.83 = (f32[256,6,64]{0,2,1:T(8,128)}, f32[256,6,64]{0,2,1:T(8,128)S(1)}, u32[]{:S(2)}) copy-start(f32[256,6,64]{0,2,1:T(8,128)S(1)} %get-tuple-element.403) | copy-start | bytes 1179652
  39.0 6.8 %copy-start.85 = (f32[256,6,64]{0,2,1:T(8,128)}, f32[256,6,64]{0,2,1:T(8,128)S(1)}, u32[]{:S(2)}) copy-start(f32[256,6,64]{0,2,1:T(8,128)S(1)} %get-tuple-element.401) | copy-start | bytes 1179652
  50.2 3.9 collective-permute-start
  50.7 48.5 %copy-start.121 = (f32[768]{0:T(1024)}, f32[768]{0:T(1024)S(1)}, u32[]{:S(2)}) copy-start(f32[768]{0:T(1024)S(1)} %convert_element_type.372) | copy-start | bytes 9220
  57.0 42.3 %copy-start.3 = (f32[512,768]{0,1:T(8,128)}, f32[512,768]{0,1:T(8,128)S(1)}, u32[]{:S(2)}) copy-start(f32[512,768]{0,1:T(8,128)S(1)} %get-tuple-element.319) | copy-start | bytes 4718596
  57.0 42.2 %copy-start.124 = (f32[512]{0:T(512)}, f32[512]{0:T(512)S(1)}, u32[]{:S(2)}) copy-start(f32[512]{0:T(512)S(1)} %broadcast_multiply_fusion.2) | copy-start | bytes 6148
  57.3 41.9 %copy-start.126 = (f32[512]{0:T(512)}, f32[512]{0:T(512)S(1)}, u32[]{:S(2)}) copy-start(f32[512]{0:T(512)S(1)} %fusion.143) | copy-start | bytes 6148
  57.6 3.3 collective-permute-start.1
  60.0 9.8 %copy-start.26 = (bf16[1024,384]{0,1:T(8,128)(2,1)}, bf16[1024,384]{0,1:T(8,128)(2,1)S(1)}, u32[]{:S(2)}) copy-start(bf16[1024,384]{0,1:T(8,128)(2,1)S(1)} %convolution_convert_fusion.8) | copy-start | bytes 2359300
  60.9 30.1 %copy-start.170 = (bf16[1024,384]{0,1:T(8,128)(2,1)}, bf16[1024,384]{0,1:T(8,128)(2,1)S(1)}, u32[]{:S(2)}) copy-start(bf16[1024,384]{0,1:T(8,128)(2,1)S(1)} %add_convert_fusion.7) | copy-start | bytes 2359300
  63.2 6.6 %copy-start.39 = (bf16[512,384]{0,1:T(8,128)(2,1)}, bf16[512,384]{0,1:T(8,128)(2,1)S(1)}, u32[]{:S(2)}) copy-start(bf16[512,384]{0,1:T(8,128)(2,1)S(1)} %get-tuple-element.345) | copy-start | bytes 1179652
  63.2 6.6 %copy-start.41 = (bf16[512,384]{0,1:T(8,128)(2,1)}, bf16[512,384]{0,1:T(8,128)(2,1)S(1)}, u32[]{:S(2)}) copy-start(bf16[512,384]{0,1:T(8,128)(2,1)S(1)} %get-tuple-element.344) | copy-start | bytes 1179652
  72.0 19.0 %copy-start.2 = (f32[6,512,1024]{2,1,0:T(8,128)}, f32[6,512,1024]{2,1,0:T(8,128)S(1)}, u32[]{:S(2)}) copy-start(f32[6,512,1024]{2,1,0:T(8,128)S(1)} %get-tuple-element.390) | copy-start | bytes 37748740
  96.9 2.4 collective-permute-start.2
  100.5 2.4 collective-permute-start.3
  101.0 20.6 %copy-start.144 = (f32[1536]{0:T(1024)}, f32[1536]{0:T(1024)S(1)}, u32[]{:S(2)}) copy-start(f32[1536]{0:T(1024)S(1)} %convert_element_type.392) | copy-start | bytes 18436
  103.4 18.2 %copy-start.49 = (bf16[512,768]{0,1:T(8,128)(2,1)}, bf16[512,768]{0,1:T(8,128)(2,1)S(1)}, u32[]{:S(2)}) copy-start(bf16[512,768]{0,1:T(8,128)(2,1)S(1)} %get-tuple-element.331) | copy-start | bytes 2359300
  103.4 18.2 %copy-start.51 = (bf16[512,768]{0,1:T(8,128)(2,1)}, bf16[512,768]{0,1:T(8,128)(2,1)S(1)}, u32[]{:S(2)}) copy-start(bf16[512,768]{0,1:T(8,128)(2,1)S(1)} %get-tuple-element.332) | copy-start | bytes 2359300
  103.4 18.2 %copy-start.161 = (bf16[1536,768]{1,0:T(8,128)(2,1)S(1)}, bf16[1536,768]{1,0:T(8,128)(2,1)}, u32[]{:S(2)}) copy-start(bf16[1536,768]{1,0:T(8,128)(2,1)} %param.90) | copy-start | bytes 7077892
  125.4 12.8 %collective-permute-start.4 = (bf16[1024,768]{0,1:T(8,128)(2,1)}, bf16[1024,768]{0,1:T(8,128)(2,1)}, u32[]{:S(2)}, u32[]{:S(2)}) collective-permute-start(bf16[1024,768]{0,1:T(8,128)(2,1)} %convolution_convert_fusion.5), channel_id=1, source_target_pairs={{0,1},{1,0},{2,3},{3,2},{4,5},{5,4},{6,7},{7,6},{8,9},{9,8},{10,11... | collective-permute-start | bytes 4718600 | tf_op jit(solution)/shard_map/ppermute | solution.py:164
  126.4 9.8 %copy-start.129 = (f32[6,256]{1,0:T(8,128)S(1)}, f32[6,256]{1,0:T(8,128)}, u32[]{:S(2)}) copy-start(f32[6,256]{1,0:T(8,128)} %copy-done.128) | copy-start | bytes 18436
  126.4 9.8 %copy-start.131 = (f32[6,256]{1,0:T(8,128)S(1)}, f32[6,256]{1,0:T(8,128)}, u32[]{:S(2)}) copy-start(f32[6,256]{1,0:T(8,128)} %copy-done.130) | copy-start | bytes 18436
  141.5 5.1 %slice-start.10 = ((s8[6291456]{0:T(1024)(128)(4,1)}), s8[4194304]{0:T(1024)(128)(4,1)S(1)}, s32[]{:S(2)}) async-start(s8[6291456]{0:T(1024)(128)(4,1)} %bitcast.466), calls=%async_computation.12 | async-start | bytes 8388608
  156.3 4.3 %collective-permute-start.5 = (bf16[512,768]{0,1:T(8,128)(2,1)S(1)}, bf16[512,768]{0,1:T(8,128)(2,1)S(1)}, u32[]{:S(2)}, u32[]{:S(2)}) collective-permute-start(bf16[512,768]{0,1:T(8,128)(2,1)S(1)} %broadcast_select_fusion.7), channel_id=1, source_target_pairs={{0,1},{1,0},{2,3},{3,2},{4,5},{5,4},{6,7},{7,6},{8,9},{9,8},{10,11... | collective-permute-start | bytes 2359304 | tf_op jit(solution)/shard_map/ppermute | solution.py:164
  164.3 8.9 %collective-permute-start.6 = (bf16[512,768]{0,1:T(8,128)(2,1)}, bf16[512,768]{0,1:T(8,128)(2,1)}, u32[]{:S(2)}, u32[]{:S(2)}) collective-permute-start(bf16[512,768]{0,1:T(8,128)(2,1)} %add_convert_fusion.10), channel_id=1, source_target_pairs={{0,1},{1,0},{2,3},{3,2},{4,5},{5,4},{6,7},{7,6},{8,9},{9,8},{10,11... | collective-permute-start | bytes 2359304 | tf_op jit(solution)/shard_map/ppermute | solution.py:164
  178.6 7.3 %copy-start.27 = (bf16[1024,384]{0,1:T(8,128)(2,1)S(1)}, bf16[1024,384]{0,1:T(8,128)(2,1)}, u32[]{:S(2)}) copy-start(bf16[1024,384]{0,1:T(8,128)(2,1)} %copy-done.26) | copy-start | bytes 2359300
  178.6 10.6 %slice-start.3 = ((s8[12582912]{0:T(1024)(128)(4,1)}), s8[4194304]{0:T(1024)(128)(4,1)S(1)}, s32[]{:S(2)}) async-start(s8[12582912]{0:T(1024)(128)(4,1)} %bitcast.361), calls=%async_computation.5 | async-start | bytes 8388608
  178.6 10.6 %slice-start.4 = ((s8[12582912]{0:T(1024)(128)(4,1)}), s8[4194304]{0:T(1024)(128)(4,1)S(1)}, s32[]{:S(2)}) async-start(s8[12582912]{0:T(1024)(128)(4,1)} %bitcast.361), calls=%async_computation.6 | async-start | bytes 8388608
  188.0 12.6 %copy-start.79 = (bf16[6,64,512]{2,1,0:T(8,128)(2,1)}, bf16[6,64,512]{2,1,0:T(8,128)(2,1)S(1)}, u32[]{:S(2)}) copy-start(bf16[6,64,512]{2,1,0:T(8,128)(2,1)S(1)} %convolution_convert_fusion.19) | copy-start | bytes 1179652
  198.3 10.1 %slice-start = ((s8[12582912]{0:T(1024)(128)(4,1)}), s8[4194304]{0:T(1024)(128)(4,1)S(1)}, s32[]{:S(2)}) async-start(s8[12582912]{0:T(1024)(128)(4,1)} %bitcast.359), calls=%async_computation.2 | async-start | bytes 8388608
  200.6 7.8 %slice-start.1 = ((s8[12582912]{0:T(1024)(128)(4,1)}), s8[4194304]{0:T(1024)(128)(4,1)S(1)}, s32[]{:S(2)}) async-start(s8[12582912]{0:T(1024)(128)(4,1)} %bitcast.359), calls=%async_computation.3 | async-start | bytes 8388608
  202.7 5.6 %slice-start.2 = ((s8[12582912]{0:T(1024)(128)(4,1)}), s8[4194304]{0:T(1024)(128)(4,1)S(1)}, s32[]{:S(2)}) async-start(s8[12582912]{0:T(1024)(128)(4,1)} %bitcast.359), calls=%async_computation.4 | async-start | bytes 8388608
  213.4 9.4 %collective-permute-start.7 = (bf16[512,768]{0,1:T(8,128)(2,1)S(1)}, bf16[512,768]{0,1:T(8,128)(2,1)S(1)}, u32[]{:S(2)}, u32[]{:S(2)}) collective-permute-start(bf16[512,768]{0,1:T(8,128)(2,1)S(1)} %broadcast_select_fusion.4), channel_id=1, source_target_pairs={{0,1},{1,0},{2,3},{3,2},{4,5},{5,4},{6,7},{7,6},{8,9},{9,8},{10,11... | collective-permute-start | bytes 2359304 | tf_op jit(solution)/shard_map/ppermute | solution.py:164
  218.4 22.2 %collective-permute-start.10 = (bf16[512,768]{0,1:T(8,128)(2,1)}, bf16[512,768]{0,1:T(8,128)(2,1)}, u32[]{:S(2)}, u32[]{:S(2)}) collective-permute-start(bf16[512,768]{0,1:T(8,128)(2,1)} %broadcast_select_fusion), channel_id=1, source_target_pairs={{0,1},{1,0},{2,3},{3,2},{4,5},{5,4},{6,7},{7,6},{8,9},{9,8},{10,11... | collective-permute-start | bytes 2359304 | tf_op jit(solution)/shard_map/ppermute | solution.py:164
  233.0 13.9 %collective-permute-start.11 = (f32[3072]{0:T(1024)S(1)}, f32[3072]{0:T(1024)S(1)}, u32[]{:S(2)}, u32[]{:S(2)}) collective-permute-start(f32[3072]{0:T(1024)S(1)} %pad_maximum_fusion.16), channel_id=1, source_target_pairs={{0,1},{1,0},{2,3},{3,2},{4,5},{5,4},{6,7},{7,6},{8,9},{9,8},{10,11... | collective-permute-start | bytes 36872 | tf_op jit(solution)/shard_map/ppermute | solution.py:164
  234.6 21.2 %collective-permute-start.20 = (bf16[192,1536]{1,0:T(8,128)(2,1)}, bf16[192,1536]{1,0:T(8,128)(2,1)S(1)}, u32[]{:S(2)}, u32[]{:S(2)}) collective-permute-start(bf16[192,1536]{1,0:T(8,128)(2,1)} %get-tuple-element.324), channel_id=1, source_target_pairs={{0,2},{2,0},{4,6},{6,4},{1,3},{3,1},{5,7},{7,5},{8,10},{10,8},{12,... | collective-permute-start | bytes 1769480 | tf_op jit(solution)/shard_map/ppermute | solution.py:363
  237.3 32.2 %collective-permute-start.19 = (bf16[192,1536]{1,0:T(8,128)(2,1)}, bf16[192,1536]{1,0:T(8,128)(2,1)}, u32[]{:S(2)}, u32[]{:S(2)}) collective-permute-start(bf16[192,1536]{1,0:T(8,128)(2,1)} %get-tuple-element.325), channel_id=1, source_target_pairs={{0,4},{2,6},{4,0},{6,2},{1,5},{3,7},{5,1},{7,3},{8,12},{10,14},{12... | collective-permute-start | bytes 1769480 | tf_op jit(solution)/shard_map/ppermute | solution.py:363
  238.8 31.7 %collective-permute-start.18 = (bf16[192,1536]{1,0:T(8,128)(2,1)}, bf16[192,1536]{1,0:T(8,128)(2,1)}, u32[]{:S(2)}, u32[]{:S(2)}) collective-permute-start(bf16[192,1536]{1,0:T(8,128)(2,1)} %get-tuple-element.326), channel_id=1, source_target_pairs={{0,6},{2,4},{4,2},{6,0},{1,7},{3,5},{5,3},{7,1},{8,14},{10,12},{12... | collective-permute-start | bytes 1769480 | tf_op jit(solution)/shard_map/ppermute | solution.py:363
  240.6 46.8 %collective-permute-start.8 = (bf16[512,768]{0,1:T(8,128)(2,1)S(1)}, bf16[512,768]{0,1:T(8,128)(2,1)}, u32[]{:S(2)}, u32[]{:S(2)}) collective-permute-start(bf16[512,768]{0,1:T(8,128)(2,1)S(1)} %add_convert_fusion.9), channel_id=1, source_target_pairs={{0,1},{1,0},{2,3},{3,2},{4,5},{5,4},{6,7},{7,6},{8,9},{9,8},{10,11... | collective-permute-start | bytes 2359304 | tf_op jit(solution)/shard_map/ppermute | solution.py:164
  246.9 40.6 %copy-start.16 = (f32[512,768]{0,1:T(8,128)S(1)}, f32[512,768]{0,1:T(8,128)}, u32[]{:S(2)}) copy-start(f32[512,768]{0,1:T(8,128)} %copy-done.15) | copy-start | bytes 4718596
  255.8 13.6 %copy-start.111 = (bf16[192,1536]{1,0:T(8,128)(2,1)}, bf16[192,1536]{1,0:T(8,128)(2,1)S(1)}, u32[]{:S(2)}) copy-start(bf16[192,1536]{1,0:T(8,128)(2,1)S(1)} %collective-permute-done.20) | copy-start | bytes 1769476
  272.7 8.7 %collective-permute-start.23 = (bf16[48,1536]{1,0:T(8,128)(2,1)S(1)}, bf16[48,1536]{1,0:T(8,128)(2,1)S(1)}, u32[]{:S(2)}, u32[]{:S(2)}) collective-permute-start(bf16[48,1536]{1,0:T(8,128)(2,1)S(1)} %get-tuple-element.350), channel_id=1, source_target_pairs={{0,8},{8,16},{16,24},{24,0},{1,9},{9,17},{17,25},{25,1},{2,10},{10... | collective-permute-start | bytes 442376 | tf_op jit(solution)/shard_map/ppermute | solution.py:400
  274.3 12.3 %collective-permute-start.22 = (bf16[48,1536]{1,0:T(8,128)(2,1)S(1)}, bf16[48,1536]{1,0:T(8,128)(2,1)S(1)}, u32[]{:S(2)}, u32[]{:S(2)}) collective-permute-start(bf16[48,1536]{1,0:T(8,128)(2,1)S(1)} %get-tuple-element.351), channel_id=1, source_target_pairs={{0,16},{8,24},{16,0},{24,8},{1,17},{9,25},{17,1},{25,9},{2,18},{10... | collective-permute-start | bytes 442376 | tf_op jit(solution)/shard_map/ppermute | solution.py:400
  276.5 10.0 %collective-permute-start.21 = (bf16[48,1536]{1,0:T(8,128)(2,1)S(1)}, bf16[48,1536]{1,0:T(8,128)(2,1)S(1)}, u32[]{:S(2)}, u32[]{:S(2)}) collective-permute-start(bf16[48,1536]{1,0:T(8,128)(2,1)S(1)} %get-tuple-element.352), channel_id=1, source_target_pairs={{0,24},{8,0},{16,8},{24,16},{1,25},{9,1},{17,9},{25,17},{2,26},{10... | collective-permute-start | bytes 442376 | tf_op jit(solution)/shard_map/ppermute | solution.py:400
  290.0 14.1 %copy-start.96 = (bf16[256,384]{0,1:T(8,128)(2,1)}, bf16[256,384]{0,1:T(8,128)(2,1)S(1)}, u32[]{:S(2)}) copy-start(bf16[256,384]{0,1:T(8,128)(2,1)S(1)} %get-tuple-element.339) | copy-start | bytes 589828
  294.1 5.1 %slice-start.8 = ((s8[4718592]{0:T(1024)(128)(4,1)}), s8[4194304]{0:T(1024)(128)(4,1)S(1)}, s32[]{:S(2)}) async-start(s8[4718592]{0:T(1024)(128)(4,1)} %bitcast.365), calls=%async_computation.10 | async-start | bytes 8388608
  305.9 8.4 %copy-start.53 = (bf16[1024,6,64]{0,2,1:T(8,128)(2,1)}, bf16[1024,6,64]{0,2,1:T(8,128)(2,1)S(1)}, u32[]{:S(2)}) copy-start(bf16[1024,6,64]{0,2,1:T(8,128)(2,1)S(1)} %get-tuple-element.393) | copy-start | bytes 2359300
  305.9 5.6 %copy-start.29 = (bf16[1024,384]{0,1:T(8,128)(2,1)S(1)}, bf16[1024,384]{0,1:T(8,128)(2,1)}, u32[]{:S(2)}) copy-start(bf16[1024,384]{0,1:T(8,128)(2,1)} %copy-done.28) | copy-start | bytes 2359300
  333.0 17.3 %collective-permute-start.14 = (bf16[206,1536]{1,0:T(8,128)(2,1)S(1)}, bf16[206,1536]{1,0:T(8,128)(2,1)S(1)}, u32[]{:S(2)}, u32[]{:S(2)}) collective-permute-start(bf16[206,1536]{1,0:T(8,128)(2,1)S(1)} %get-tuple-element.321), channel_id=1, source_target_pairs={{0,2},{2,0},{4,6},{6,4},{1,3},{3,1},{5,7},{7,5},{8,10},{10,8},{12,... | collective-permute-start | bytes 1898504 | tf_op jit(solution)/shard_map/ppermute | solution.py:363
  334.7 28.0 %collective-permute-start.12 = (bf16[206,1536]{1,0:T(8,128)(2,1)S(1)}, bf16[206,1536]{1,0:T(8,128)(2,1)S(1)}, u32[]{:S(2)}, u32[]{:S(2)}) collective-permute-start(bf16[206,1536]{1,0:T(8,128)(2,1)S(1)} %get-tuple-element.322), channel_id=1, source_target_pairs={{0,6},{2,4},{4,2},{6,0},{1,7},{3,5},{5,3},{7,1},{8,14},{10,12},{12... | collective-permute-start | bytes 1898504 | tf_op jit(solution)/shard_map/ppermute | solution.py:363
  334.9 29.2 %collective-permute-start.13 = (bf16[206,1536]{1,0:T(8,128)(2,1)S(1)}, bf16[206,1536]{1,0:T(8,128)(2,1)S(1)}, u32[]{:S(2)}, u32[]{:S(2)}) collective-permute-start(bf16[206,1536]{1,0:T(8,128)(2,1)S(1)} %get-tuple-element.323), channel_id=1, source_target_pairs={{0,4},{2,6},{4,0},{6,2},{1,5},{3,7},{5,1},{7,3},{8,12},{10,14},{12... | collective-permute-start | bytes 1898504 | tf_op jit(solution)/shard_map/ppermute | solution.py:363
  340.2 37.1 %collective-permute-start.9 = (bf16[512,768]{0,1:T(8,128)(2,1)S(1)}, bf16[512,768]{0,1:T(8,128)(2,1)S(1)}, u32[]{:S(2)}, u32[]{:S(2)}) collective-permute-start(bf16[512,768]{0,1:T(8,128)(2,1)S(1)} %broadcast_select_fusion.1), channel_id=1, source_target_pairs={{0,1},{1,0},{2,3},{3,2},{4,5},{5,4},{6,7},{7,6},{8,9},{9,8},{10,11... | collective-permute-start | bytes 2359304 | tf_op jit(solution)/shard_map/ppermute | solution.py:164
  364.9 12.4 %copy-start.17 = (f32[512,768]{0,1:T(8,128)S(1)}, f32[512,768]{0,1:T(8,128)}, u32[]{:S(2)}) copy-start(f32[512,768]{0,1:T(8,128)} %copy-done.15) | copy-start | bytes 4718596
  365.9 16.3 %collective-permute-start.17 = (bf16[62,1536]{1,0:T(8,128)(2,1)}, bf16[62,1536]{1,0:T(8,128)(2,1)S(1)}, u32[]{:S(2)}, u32[]{:S(2)}) collective-permute-start(bf16[62,1536]{1,0:T(8,128)(2,1)} %get-tuple-element.335), channel_id=1, source_target_pairs={{0,8},{8,16},{16,24},{24,0},{1,9},{9,17},{17,25},{25,1},{2,10},{10... | collective-permute-start | bytes 571400 | tf_op jit(solution)/shard_map/ppermute | solution.py:400
  375.8 9.8 %collective-permute-start.15 = (bf16[62,1536]{1,0:T(8,128)(2,1)}, bf16[62,1536]{1,0:T(8,128)(2,1)S(1)}, u32[]{:S(2)}, u32[]{:S(2)}) collective-permute-start(bf16[62,1536]{1,0:T(8,128)(2,1)} %get-tuple-element.336), channel_id=1, source_target_pairs={{0,24},{8,0},{16,8},{24,16},{1,25},{9,1},{17,9},{25,17},{2,26},{10... | collective-permute-start | bytes 571400 | tf_op jit(solution)/shard_map/ppermute | solution.py:400
  375.8 14.5 %collective-permute-start.16 = (bf16[62,1536]{1,0:T(8,128)(2,1)}, bf16[62,1536]{1,0:T(8,128)(2,1)}, u32[]{:S(2)}, u32[]{:S(2)}) collective-permute-start(bf16[62,1536]{1,0:T(8,128)(2,1)} %get-tuple-element.337), channel_id=1, source_target_pairs={{0,16},{8,24},{16,0},{24,8},{1,17},{9,25},{17,1},{25,9},{2,18},{10... | collective-permute-start | bytes 571400 | tf_op jit(solution)/shard_map/ppermute | solution.py:400
  379.0 18.5 %copy-start.1 = (bf16[768,1536]{1,0:T(8,128)(2,1)S(1)}, bf16[768,1536]{1,0:T(8,128)(2,1)}, u32[]{:S(2)}) copy-start(bf16[768,1536]{1,0:T(8,128)(2,1)} %param.88) | copy-start | bytes 7077892
  (147 other events, 314.8 us)
Sparse Core Ops, SparseCore 0:
  170.6 151.9 reduce-scatter.1

commit v3 on v2

--- a/solution.py
+++ b/solution.py
@@ -354,7 +354,7 @@
             staged = jnp.concatenate(
                 [staged, jnp.broadcast_to(extra[None], (inner_size,) + extra.shape)], 1
             )
-        if inner_size == 4:
+        if inner_size == 4 and extra is not None:
             spot = lax.axis_index("inner")
             swapped = []
             for mask in range(inner_size):

time: 411 us -> 387 us (0.942)
  waiting for transfers between devices: 67.8 us -> 53.9 us
  starting transfers between devices: 28.3 us -> 22.3 us
    ppermute x6 -> x3, waiting for transfers between devices: 47.4 us -> 27.8 us  [exchange_sum(): lax.ppermute(piece, 'inner', [(peer, peer ^ mask) for peer in range(inner...]
    ppermute x6, starting transfers between devices: 16.6 us -> 9.1 us  [exchange_sum(): lax.ppermute(piece, 'outer', [(peer, (peer + shift) % outer_size) for pee...]
    ppermute x6, waiting for transfers between devices: 15.6 us -> 21.4 us  [exchange_sum(): lax.ppermute(piece, 'outer', [(peer, (peer + shift) % outer_size) for pee...]
    all_to_all x0 -> x1, starting transfers between devices: none -> 5.43 us  [exchange_sum(): first = lax.all_to_all(staged, 'inner', 0, 0, tiled=True)]
  transfers between devices with their start and end apart: 25 -> 23, of which waited for: 13 -> 11; matrix products, arithmetic and copies ran while one was open for 37% -> 38% of each run, Pallas kernels for 0% -> 0%
where the time goes in v3:
time: 387 us; the launch traced here: 381 us
  matrix products  149 us (39%)
  other arithmetic  70.1 us (18%)
  local copies, waits for them, and re-layouts  68.1 us (18%)
  waiting for transfers between devices  53.9 us (14%)
  starting transfers between devices  22.3 us (6%)
  between operations  16.9 us (4%)
    dot_general x30, matrix products, project(): return jnp.dot(data, weight, preferred_element_type=jnp.float32)  72.9 us
    unnamed x377, local copies, waits for them, and re-layouts  31.6 us
    ppermute x3, waiting for transfers between devices, exchange_sum(): lax.ppermute(piece, 'inner', [(peer, peer ^ mask) for peer in range(inner...  27.8 us
    ppermute x6, waiting for transfers between devices, exchange_sum(): lax.ppermute(piece, 'outer', [(peer, (peer + shift) % outer_size) for pee...  21.4 us
    dot_general x6, matrix products, attend_backward(): jnp.einsum('qhe,khe->hqk', grad_piece, values[:end], preferred_element_ty...  19.4 us
    dot_general x6, matrix products, attend_forward(): jnp.einsum('hqk,khe->qhe', weights, values[:end], preferred_element_type=...  18.7 us
    reduce_sum x5, other arithmetic, attend_forward(): summed = jnp.sum(powers, -1, keepdims=True)  15.8 us
    dot_general x6, matrix products, attend_forward(): jnp.einsum('qhe,khe->hqk', piece, keys[:end], preferred_element_type=jnp....  13.2 us
  transfers between devices with their start and end apart: 23, of which 11 were waited for; matrix products, arithmetic and copies ran while one was open for 38% of the time, Pallas kernels for 0%

profile of v3, /device:TPU:0, one launch (start us, length us, event | category | flops | bytes accessed | tf_op | source)
XLA Modules:
  0.0 380.8 jit_solution(3867660212897095227)
XLA Ops:
  12.4 2.5 add_convert_fusion.8
  21.4 2.4 multiply_convert_fusion.8
  31.0 2.2 fusion.180
  36.6 2.4 fusion.179
  42.8 2.9 fusion.178
  48.0 1.8 slice_select_fusion
  54.0 2.9 fusion.169
  63.2 6.6 %select_reduce_fusion = (f32[6,512]{1,0:T(8,128)S(1)}, f32[6,512,1024]{2,1,0:T(8,128)}) fusion(pred[512,1024]{1,0:T(8,128)(4,1)S(1)} %get-tuple-element.369, bf16[512,6,64]{0,2,1:T(8,128)(2,1)S(1)} %bitcast.347, bf16[1024,6,64]{0,2,1:T(8,128)(2,1)S(1)} %bitcast.334), kind=kOutput, calls=%fused_computation.12 | convolution fusion | flops 408941568 | bytes 14299136 | tf_op jit(solution)/shard_map/qhe,khe->hqk/dot_general | solution.py:54
  69.8 2.1 select_reduce_fusion.1
  71.9 12.1 %fusion = (f32[6,512]{1,0:T(8,128)S(1)}, f32[6,512]{1,0:T(8,128)S(1)}) fusion(f32[6,512,1024]{2,1,0:T(8,128)S(1)} %get-tuple-element.387, f32[6,512]{1,0:T(8,128)S(1)} %get-tuple-element.386, pred[512,1024]{1,0:T(8,128)(4,1)S(1)} %get-tuple-element.368, f32[6,512]{1,0:T(8,128)S(1)} %get-tuple-element.384, f32[6,512,1024]{2,1,0:T(8,128)} %get-tuple-element.385, ...), kind=kLoop, calls=%fused_computation.8 | loop fusion | flops 18868224 | bytes 26263552 | tf_op jit(solution)/shard_map/reduce_sum | solution.py:64
  84.0 6.9 %fusion.82 = f32[512,6,64]{0,2,1:T(8,128)S(1)} fusion(bf16[1024,6,64]{0,2,1:T(8,128)(2,1)S(1)} %bitcast.426, f32[6,512,1024]{2,1,0:T(8,128)} %get-tuple-element.385, f32[6,512]{1,0:T(8,128)S(1)} %get-tuple-element.404, f32[6,512]{1,0:T(8,128)S(1)} %get-tuple-element.384, pred[512,1024]{1,0:T(8,128)(4,1)S(1)} %get-tuple-element.369), kind=kOutput, calls=%fused_computation.190 | convolution fusion | flops 415236096 | bytes 14704640 | tf_op jit(solution)/shard_map/hqk,khe->qhe/dot_general | solution.py:67
  90.9 3.2 fusion.83
  97.3 1.9 collective-permute-done.2
  100.9 1.9 collective-permute-done.3
  103.3 18.2 %multiply_convert_fusion.3 = (bf16[1024,1536]{1,0:T(8,128)(2,1)S(1)}, f32[1024,1536]{1,0:T(8,128)}, f32[1024,1536]{1,0:T(8,128)}) fusion(f32[1536]{0:T(1024)S(1)} %convert_element_type.379, bf16[768,1536]{1,0:T(8,128)(2,1)S(1)} %copy-done, bf16[512,768]{0,1:T(8,128)(2,1)S(1)} %get-tuple-element.329, bf16[512,768]{0,1:T(8,128)(2,1)S(1)} %get-tuple-element.328), kind=kOutput, calls=%fused_computation.24 | convolution fusion | flops 2522873856 | bytes 19666944 | tf_op jit(solution)/shard_map/dot_general | solution.py:25
  121.6 3.8 convolution_convert_fusion.5
  126.9 1.8 copy.96
  128.7 2.7 copy.81
  131.4 1.8 copy.97
  133.2 1.7 copy.98
  134.9 1.8 copy.99
  139.3 3.2 fusion.166
  144.9 2.7 convert_reduce_fusion.2
  147.7 7.0 %convert_reduce_fusion = (f32[1536]{0:T(1024)S(1)}, bf16[1024,1536]{1,0:T(8,128)(2,1)S(1)}) fusion(f32[1024,1536]{1,0:T(8,128)S(1)} %bitcast.431, bf16[1536,768]{1,0:T(8,128)(2,1)S(1)} %copy-done.162, f32[1024,768]{0,1:T(8,128)S(1)} %get-tuple-element.306, f32[1024,1536]{1,0:T(8,128)} %get-tuple-element.388, f32[1536]{0:T(1024)S(1)} %copy-done.145), kind=kOutput, calls=%fused_computation.18 | convolution fusion | flops 2443442688 | bytes 21245952 | tf_op jit(solution)/shard_map/dot_general | solution.py:25
  154.6 2.6 convolution_convert_fusion.4
  159.4 2.8 convolution_convert_fusion
  166.3 3.0 convolution_convert_fusion.1
  169.4 2.8 pad_maximum_fusion
  172.2 2.7 copy.103
  180.3 7.3 %multiply_convert_fusion.1 = bf16[6,512,1024]{2,1,0:T(8,128)(2,1)S(1)} fusion(f32[6,512,1024]{2,1,0:T(8,128)} %copy-done.2, f32[6,512]{1,0:T(8,128)S(1)} %get-tuple-element.363, f32[6,512]{1,0:T(8,128)S(1)} %log_add_fusion.1, pred[512,1024]{1,0:T(8,128)(4,1)S(1)} %get-tuple-element.368, bf16[512,6,64]{0,2,1:T(8,128)(2,1)S(1)} %bitcast.401, ...), kind=kOutput, calls=%fused_computation.2 | convolution fusion | flops 418381824 | bytes 20602880 | tf_op jit(solution)/shard_map/qhe,khe->hqk/dot_general | solution.py:95
  187.6 2.0 convolution_convert_fusion.19
  190.9 2.9 fusion.5
  193.8 6.1 %multiply_convert_fusion = bf16[6,512,1024]{2,1,0:T(8,128)(2,1)S(1)} fusion(f32[6,512,1024]{2,1,0:T(8,128)S(1)} %bitcast.327, f32[6,512]{1,0:T(8,128)S(1)} %get-tuple-element.362, f32[6,512]{1,0:T(8,128)S(1)} %log_add_fusion, pred[512,1024]{1,0:T(8,128)(4,1)S(1)} %get-tuple-element.369, bf16[512,6,64]{0,2,1:T(8,128)(2,1)S(1)} %bitcast.404, ...), kind=kOutput, calls=%fused_computation | convolution fusion | flops 418381824 | bytes 20602880 | tf_op jit(solution)/shard_map/qhe,khe->hqk/dot_general | solution.py:95
  199.9 2.0 convolution_convert_fusion.18
  202.2 2.1 convolution_convert_fusion.2
  207.4 2.6 fusion.185
  210.0 3.4 convert_reduce_fusion.5
  215.3 3.1 add_convert_fusion.1
  226.8 2.9 copy.101
  231.3 5.4 %all-to-all-start = ((bf16[4,192,1536]{2,1,0:T(8,128)(2,1)}), bf16[4,192,1536]{2,1,0:T(8,128)(2,1)}, u32[]{:S(2)}, u32[]{:S(2)}) async-start(bf16[4,192,1536]{2,1,0:T(8,128)(2,1)} %bitcast.340), calls=%async_computation | async-start | bytes 4718592 | tf_op jit(solution)/shard_map/all_to_all | solution.py:375
  236.8 2.2 multiply_reduce_fusion.2
  241.5 2.6 convert_add_fusion
  244.1 3.1 copy.105
  262.1 1.7 multiply_convert_fusion.4
  264.0 2.5 convert_reduce_fusion.7
  266.6 2.5 multiply_convert_fusion.2
  272.4 3.2 fusion.90
  275.5 2.1 copy.95
  277.7 2.1 fusion.75
  284.4 3.2 fusion.88
  292.6 2.2 collective-permute-start.14
  300.1 9.9 %collective-permute-done.14 = bf16[206,1536]{1,0:T(8,128)(2,1)S(1)} collective-permute-done((bf16[206,1536]{1,0:T(8,128)(2,1)S(1)}, bf16[206,1536]{1,0:T(8,128)(2,1)S(1)}, u32[]{:S(2)}, u32[]{:S(2)}) %collective-permute-start.14) | collective-permute-done | bytes 632864 | tf_op jit(solution)/shard_map/ppermute | solution.py:363
  310.0 16.5 %collective-permute-done.12 = bf16[206,1536]{1,0:T(8,128)(2,1)S(1)} collective-permute-done((bf16[206,1536]{1,0:T(8,128)(2,1)S(1)}, bf16[206,1536]{1,0:T(8,128)(2,1)S(1)}, u32[]{:S(2)}, u32[]{:S(2)}) %collective-permute-start.12) | collective-permute-done | bytes 632864 | tf_op jit(solution)/shard_map/ppermute | solution.py:363
  328.9 2.0 collective-permute-start.17
  330.9 2.3 collective-permute-start.15
  334.2 1.7 add_add_fusion.4
  335.8 3.0 copy.104
  340.4 1.9 collective-permute-done.15
  342.3 9.2 %collective-permute-done.16 = bf16[62,1536]{1,0:T(8,128)(2,1)S(1)} collective-permute-done((bf16[62,1536]{1,0:T(8,128)(2,1)S(1)}, bf16[62,1536]{1,0:T(8,128)(2,1)S(1)}, u32[]{:S(2)}, u32[]{:S(2)}) %collective-permute-start.16) | collective-permute-done | bytes 190496 | tf_op jit(solution)/shard_map/ppermute | solution.py:400
  353.1 2.4 reduce_sum.386
  355.6 1.7 collective-permute-start.19
  357.3 2.1 collective-permute-start.18
  360.7 3.5 collective-permute-done.20
  364.2 5.2 %collective-permute-done.19 = bf16[48,1536]{1,0:T(8,128)(2,1)S(1)} collective-permute-done((bf16[48,1536]{1,0:T(8,128)(2,1)S(1)}, bf16[48,1536]{1,0:T(8,128)(2,1)S(1)}, u32[]{:S(2)}, u32[]{:S(2)}) %collective-permute-start.19) | collective-permute-done | bytes 147488 | tf_op jit(solution)/shard_map/ppermute | solution.py:400
  (583 shorter events, 124.8 us)
Async XLA Ops:
  7.2 96.1 %copy-start = (bf16[768,1536]{1,0:T(8,128)(2,1)S(1)}, bf16[768,1536]{1,0:T(8,128)(2,1)}, u32[]{:S(2)}) copy-start(bf16[768,1536]{1,0:T(8,128)(2,1)} %param.88) | copy-start | bytes 7077892
  7.2 363.1 %reduce-scatter.2.cloned.1.call-start = ((), (), s32[]{:S(2)}) async-start(), calls=%async_computation.2 | async-start | bytes 5013504 | tf_op jit(solution)/shard_map/reduce_scatter | solution.py:418
  12.4 5.0 %copy-start.102 = (bf16[768,384]{1,0:T(8,128)(2,1)S(1)}, bf16[768,384]{1,0:T(8,128)(2,1)}, u32[]{:S(2)}) copy-start(bf16[768,384]{1,0:T(8,128)(2,1)} %param.70) | copy-start | bytes 1769476
  12.4 5.0 %copy-start.109 = (bf16[1024,768]{1,0:T(8,128)(2,1)S(1)}, bf16[1024,768]{1,0:T(8,128)(2,1)}, u32[]{:S(2)}) copy-start(bf16[1024,768]{1,0:T(8,128)(2,1)} %param.64) | copy-start | bytes 4718596
  18.2 20.8 %copy-start.28 = (bf16[1024,384]{0,1:T(8,128)(2,1)}, bf16[1024,384]{0,1:T(8,128)(2,1)S(1)}, u32[]{:S(2)}) copy-start(bf16[1024,384]{0,1:T(8,128)(2,1)S(1)} %convolution_convert_fusion.9) | copy-start | bytes 2359300
  19.0 9.9 %copy-start.44 = (bf16[512,384]{0,1:T(8,128)(2,1)}, bf16[512,384]{0,1:T(8,128)(2,1)S(1)}, u32[]{:S(2)}) copy-start(bf16[512,384]{0,1:T(8,128)(2,1)S(1)} %slice.659) | copy-start | bytes 1179652
  25.7 16.1 %copy-start.42 = (pred[256,1024]{1,0:T(8,128)(4,1)}, pred[256,1024]{1,0:T(8,128)(4,1)S(1)}, u32[]{:S(2)}) copy-start(pred[256,1024]{1,0:T(8,128)(4,1)S(1)} %fusion.94) | copy-start | bytes 786436
  28.7 17.0 %copy-start.80 = (f32[256,6,64]{0,2,1:T(8,128)}, f32[256,6,64]{0,2,1:T(8,128)S(1)}, u32[]{:S(2)}) copy-start(f32[256,6,64]{0,2,1:T(8,128)S(1)} %get-tuple-element.402) | copy-start | bytes 1179652
  33.2 12.6 %copy-start.82 = (f32[256,6,64]{0,2,1:T(8,128)}, f32[256,6,64]{0,2,1:T(8,128)S(1)}, u32[]{:S(2)}) copy-start(f32[256,6,64]{0,2,1:T(8,128)S(1)} %get-tuple-element.400) | copy-start | bytes 1179652
  38.9 6.8 %copy-start.84 = (f32[256,6,64]{0,2,1:T(8,128)}, f32[256,6,64]{0,2,1:T(8,128)S(1)}, u32[]{:S(2)}) copy-start(f32[256,6,64]{0,2,1:T(8,128)S(1)} %get-tuple-element.398) | copy-start | bytes 1179652
  50.1 3.9 %collective-permute-start = (f32[512,768]{0,1:T(8,128)}, f32[512,768]{0,1:T(8,128)}, u32[]{:S(2)}, u32[]{:S(2)}) collective-permute-start(f32[512,768]{0,1:T(8,128)} %slice_select_fusion), channel_id=1, source_target_pairs={{0,1},{1,0},{2,3},{3,2},{4,5},{5,4},{6,7},{7,6},{8,9},{9,8},{10,11... | collective-permute-start | bytes 4718600 | tf_op jit(solution)/shard_map/ppermute | solution.py:164
  50.6 48.5 %copy-start.117 = (f32[768]{0:T(1024)}, f32[768]{0:T(1024)S(1)}, u32[]{:S(2)}) copy-start(f32[768]{0:T(1024)S(1)} %convert_element_type.359) | copy-start | bytes 9220
  56.9 42.3 %copy-start.3 = (f32[512,768]{0,1:T(8,128)}, f32[512,768]{0,1:T(8,128)S(1)}, u32[]{:S(2)}) copy-start(f32[512,768]{0,1:T(8,128)S(1)} %get-tuple-element.319) | copy-start | bytes 4718596
  56.9 42.2 %copy-start.120 = (f32[512]{0:T(512)}, f32[512]{0:T(512)S(1)}, u32[]{:S(2)}) copy-start(f32[512]{0:T(512)S(1)} %broadcast_multiply_fusion.2) | copy-start | bytes 6148
  57.2 42.0 %copy-start.122 = (f32[512]{0:T(512)}, f32[512]{0:T(512)S(1)}, u32[]{:S(2)}) copy-start(f32[512]{0:T(512)S(1)} %fusion.135) | copy-start | bytes 6148
  57.5 3.3 collective-permute-start.1
  59.9 9.8 %copy-start.26 = (bf16[1024,384]{0,1:T(8,128)(2,1)}, bf16[1024,384]{0,1:T(8,128)(2,1)S(1)}, u32[]{:S(2)}) copy-start(bf16[1024,384]{0,1:T(8,128)(2,1)S(1)} %convolution_convert_fusion.8) | copy-start | bytes 2359300
  60.8 30.1 %copy-start.170 = (bf16[1024,384]{0,1:T(8,128)(2,1)}, bf16[1024,384]{0,1:T(8,128)(2,1)S(1)}, u32[]{:S(2)}) copy-start(bf16[1024,384]{0,1:T(8,128)(2,1)S(1)} %add_convert_fusion.7) | copy-start | bytes 2359300
  63.1 6.6 %copy-start.38 = (bf16[512,384]{0,1:T(8,128)(2,1)}, bf16[512,384]{0,1:T(8,128)(2,1)S(1)}, u32[]{:S(2)}) copy-start(bf16[512,384]{0,1:T(8,128)(2,1)S(1)} %get-tuple-element.342) | copy-start | bytes 1179652
  63.1 6.6 %copy-start.40 = (bf16[512,384]{0,1:T(8,128)(2,1)}, bf16[512,384]{0,1:T(8,128)(2,1)S(1)}, u32[]{:S(2)}) copy-start(bf16[512,384]{0,1:T(8,128)(2,1)S(1)} %get-tuple-element.341) | copy-start | bytes 1179652
  71.9 19.0 %copy-start.2 = (f32[6,512,1024]{2,1,0:T(8,128)}, f32[6,512,1024]{2,1,0:T(8,128)S(1)}, u32[]{:S(2)}) copy-start(f32[6,512,1024]{2,1,0:T(8,128)S(1)} %get-tuple-element.387) | copy-start | bytes 37748740
  96.8 2.4 collective-permute-start.2
  100.5 2.4 collective-permute-start.3
  100.9 20.6 %copy-start.144 = (f32[1536]{0:T(1024)}, f32[1536]{0:T(1024)S(1)}, u32[]{:S(2)}) copy-start(f32[1536]{0:T(1024)S(1)} %convert_element_type.379) | copy-start | bytes 18436
  103.3 18.2 %copy-start.48 = (bf16[512,768]{0,1:T(8,128)(2,1)}, bf16[512,768]{0,1:T(8,128)(2,1)S(1)}, u32[]{:S(2)}) copy-start(bf16[512,768]{0,1:T(8,128)(2,1)S(1)} %get-tuple-element.328) | copy-start | bytes 2359300
  103.3 18.2 %copy-start.50 = (bf16[512,768]{0,1:T(8,128)(2,1)}, bf16[512,768]{0,1:T(8,128)(2,1)S(1)}, u32[]{:S(2)}) copy-start(bf16[512,768]{0,1:T(8,128)(2,1)S(1)} %get-tuple-element.329) | copy-start | bytes 2359300
  103.3 18.2 %copy-start.161 = (bf16[1536,768]{1,0:T(8,128)(2,1)S(1)}, bf16[1536,768]{1,0:T(8,128)(2,1)}, u32[]{:S(2)}) copy-start(bf16[1536,768]{1,0:T(8,128)(2,1)} %param.90) | copy-start | bytes 7077892
  125.3 14.0 %collective-permute-start.4 = (bf16[1024,768]{0,1:T(8,128)(2,1)}, bf16[1024,768]{0,1:T(8,128)(2,1)}, u32[]{:S(2)}, u32[]{:S(2)}) collective-permute-start(bf16[1024,768]{0,1:T(8,128)(2,1)} %convolution_convert_fusion.5), channel_id=1, source_target_pairs={{0,1},{1,0},{2,3},{3,2},{4,5},{5,4},{6,7},{7,6},{8,9},{9,8},{10,11... | collective-permute-start | bytes 4718600 | tf_op jit(solution)/shard_map/ppermute | solution.py:164
  126.9 9.8 %copy-start.125 = (f32[6,256]{1,0:T(8,128)S(1)}, f32[6,256]{1,0:T(8,128)}, u32[]{:S(2)}) copy-start(f32[6,256]{1,0:T(8,128)} %copy-done.124) | copy-start | bytes 18436
  126.9 9.8 %copy-start.127 = (f32[6,256]{1,0:T(8,128)S(1)}, f32[6,256]{1,0:T(8,128)}, u32[]{:S(2)}) copy-start(f32[6,256]{1,0:T(8,128)} %copy-done.126) | copy-start | bytes 18436
  142.5 5.1 %slice-start.10 = ((s8[6291456]{0:T(1024)(128)(4,1)}), s8[4194304]{0:T(1024)(128)(4,1)S(1)}, s32[]{:S(2)}) async-start(s8[6291456]{0:T(1024)(128)(4,1)} %bitcast.430), calls=%async_computation.13 | async-start | bytes 8388608
  157.4 4.9 %collective-permute-start.5 = (bf16[512,768]{0,1:T(8,128)(2,1)S(1)}, bf16[512,768]{0,1:T(8,128)(2,1)S(1)}, u32[]{:S(2)}, u32[]{:S(2)}) collective-permute-start(bf16[512,768]{0,1:T(8,128)(2,1)S(1)} %broadcast_select_fusion.7), channel_id=1, source_target_pairs={{0,1},{1,0},{2,3},{3,2},{4,5},{5,4},{6,7},{7,6},{8,9},{9,8},{10,11... | collective-permute-start | bytes 2359304 | tf_op jit(solution)/shard_map/ppermute | solution.py:164
  166.0 8.9 %collective-permute-start.6 = (bf16[512,768]{0,1:T(8,128)(2,1)}, bf16[512,768]{0,1:T(8,128)(2,1)}, u32[]{:S(2)}, u32[]{:S(2)}) collective-permute-start(bf16[512,768]{0,1:T(8,128)(2,1)} %add_convert_fusion.10), channel_id=1, source_target_pairs={{0,1},{1,0},{2,3},{3,2},{4,5},{5,4},{6,7},{7,6},{8,9},{9,8},{10,11... | collective-permute-start | bytes 2359304 | tf_op jit(solution)/shard_map/ppermute | solution.py:164
  180.3 7.3 %copy-start.27 = (bf16[1024,384]{0,1:T(8,128)(2,1)S(1)}, bf16[1024,384]{0,1:T(8,128)(2,1)}, u32[]{:S(2)}) copy-start(bf16[1024,384]{0,1:T(8,128)(2,1)} %copy-done.26) | copy-start | bytes 2359300
  180.3 10.6 %slice-start.3 = ((s8[12582912]{0:T(1024)(128)(4,1)}), s8[4194304]{0:T(1024)(128)(4,1)S(1)}, s32[]{:S(2)}) async-start(s8[12582912]{0:T(1024)(128)(4,1)} %bitcast.326), calls=%async_computation.6 | async-start | bytes 8388608
  180.3 10.6 %slice-start.4 = ((s8[12582912]{0:T(1024)(128)(4,1)}), s8[4194304]{0:T(1024)(128)(4,1)S(1)}, s32[]{:S(2)}) async-start(s8[12582912]{0:T(1024)(128)(4,1)} %bitcast.326), calls=%async_computation.7 | async-start | bytes 8388608
  189.7 12.6 %copy-start.78 = (bf16[6,64,512]{2,1,0:T(8,128)(2,1)}, bf16[6,64,512]{2,1,0:T(8,128)(2,1)S(1)}, u32[]{:S(2)}) copy-start(bf16[6,64,512]{2,1,0:T(8,128)(2,1)S(1)} %convolution_convert_fusion.19) | copy-start | bytes 1179652
  199.9 10.1 %slice-start = ((s8[12582912]{0:T(1024)(128)(4,1)}), s8[4194304]{0:T(1024)(128)(4,1)S(1)}, s32[]{:S(2)}) async-start(s8[12582912]{0:T(1024)(128)(4,1)} %bitcast.324), calls=%async_computation.3 | async-start | bytes 8388608
  202.2 7.8 %slice-start.1 = ((s8[12582912]{0:T(1024)(128)(4,1)}), s8[4194304]{0:T(1024)(128)(4,1)S(1)}, s32[]{:S(2)}) async-start(s8[12582912]{0:T(1024)(128)(4,1)} %bitcast.324), calls=%async_computation.4 | async-start | bytes 8388608
  204.4 5.7 %slice-start.2 = ((s8[12582912]{0:T(1024)(128)(4,1)}), s8[4194304]{0:T(1024)(128)(4,1)S(1)}, s32[]{:S(2)}) async-start(s8[12582912]{0:T(1024)(128)(4,1)} %bitcast.324), calls=%async_computation.5 | async-start | bytes 8388608
  215.1 9.4 %collective-permute-start.7 = (bf16[512,768]{0,1:T(8,128)(2,1)S(1)}, bf16[512,768]{0,1:T(8,128)(2,1)S(1)}, u32[]{:S(2)}, u32[]{:S(2)}) collective-permute-start(bf16[512,768]{0,1:T(8,128)(2,1)S(1)} %broadcast_select_fusion.4), channel_id=1, source_target_pairs={{0,1},{1,0},{2,3},{3,2},{4,5},{5,4},{6,7},{7,6},{8,9},{9,8},{10,11... | collective-permute-start | bytes 2359304 | tf_op jit(solution)/shard_map/ppermute | solution.py:164
  220.1 21.3 %collective-permute-start.10 = (bf16[512,768]{0,1:T(8,128)(2,1)}, bf16[512,768]{0,1:T(8,128)(2,1)}, u32[]{:S(2)}, u32[]{:S(2)}) collective-permute-start(bf16[512,768]{0,1:T(8,128)(2,1)} %broadcast_select_fusion), channel_id=1, source_target_pairs={{0,1},{1,0},{2,3},{3,2},{4,5},{5,4},{6,7},{7,6},{8,9},{9,8},{10,11... | collective-permute-start | bytes 2359304 | tf_op jit(solution)/shard_map/ppermute | solution.py:164
  231.3 5.5 %copy-start.4 = (f32[512,768]{0,1:T(8,128)S(1)}, f32[512,768]{0,1:T(8,128)}, u32[]{:S(2)}) copy-start(f32[512,768]{0,1:T(8,128)} %copy-done.3) | copy-start | bytes 4718596
  231.3 5.5 %copy-start.118 = (f32[768]{0:T(1024)S(1)}, f32[768]{0:T(1024)}, u32[]{:S(2)}) copy-start(f32[768]{0:T(1024)} %copy-done.117) | copy-start | bytes 9220
  231.3 5.5 %copy-start.121 = (f32[512]{0:T(512)S(1)}, f32[512]{0:T(512)}, u32[]{:S(2)}) copy-start(f32[512]{0:T(512)} %copy-done.120) | copy-start | bytes 6148
  231.3 5.5 %copy-start.123 = (f32[512]{0:T(512)S(1)}, f32[512]{0:T(512)}, u32[]{:S(2)}) copy-start(f32[512]{0:T(512)} %copy-done.122) | copy-start | bytes 6148
  231.3 121.8 %all-to-all-start = ((bf16[4,192,1536]{2,1,0:T(8,128)(2,1)}), bf16[4,192,1536]{2,1,0:T(8,128)(2,1)}, u32[]{:S(2)}, u32[]{:S(2)}) async-start(bf16[4,192,1536]{2,1,0:T(8,128)(2,1)} %bitcast.340), calls=%async_computation | async-start | bytes 4718592 | tf_op jit(solution)/shard_map/all_to_all | solution.py:375
  240.8 7.7 %collective-permute-start.8 = (bf16[512,768]{0,1:T(8,128)(2,1)S(1)}, bf16[512,768]{0,1:T(8,128)(2,1)}, u32[]{:S(2)}, u32[]{:S(2)}) collective-permute-start(bf16[512,768]{0,1:T(8,128)(2,1)S(1)} %add_convert_fusion.9), channel_id=1, source_target_pairs={{0,1},{1,0},{2,3},{3,2},{4,5},{5,4},{6,7},{7,6},{8,9},{9,8},{10,11... | collective-permute-start | bytes 2359304 | tf_op jit(solution)/shard_map/ppermute | solution.py:164
  240.9 6.3 %collective-permute-start.11 = (f32[3072]{0:T(1024)S(1)}, f32[3072]{0:T(1024)S(1)}, u32[]{:S(2)}, u32[]{:S(2)}) collective-permute-start(f32[3072]{0:T(1024)S(1)} %pad_maximum_fusion.16), channel_id=1, source_target_pairs={{0,1},{1,0},{2,3},{3,2},{4,5},{5,4},{6,7},{7,6},{8,9},{9,8},{10,11... | collective-permute-start | bytes 36872 | tf_op jit(solution)/shard_map/ppermute | solution.py:164
  255.6 5.1 %slice-start.8 = ((s8[4718592]{0:T(1024)(128)(4,1)}), s8[4194304]{0:T(1024)(128)(4,1)S(1)}, s32[]{:S(2)}) async-start(s8[4718592]{0:T(1024)(128)(4,1)} %bitcast.330), calls=%async_computation.11 | async-start | bytes 8388608
  263.8 6.3 %copy-start.30 = (bf16[6,256,768]{2,1,0:T(8,128)(2,1)}, bf16[6,256,768]{2,1,0:T(8,128)(2,1)S(1)}, u32[]{:S(2)}) copy-start(bf16[6,256,768]{2,1,0:T(8,128)(2,1)S(1)} %multiply_convert_fusion.4) | copy-start | bytes 7077892
  272.4 5.3 %copy-start.20 = (f32[1024,6,64]{0,2,1:T(8,128)S(1)}, f32[1024,6,64]{0,2,1:T(8,128)}, u32[]{:S(2)}) copy-start(f32[1024,6,64]{0,2,1:T(8,128)} %scatter-add.20) | copy-start | bytes 4718596
  292.6 17.4 %collective-permute-start.14 = (bf16[206,1536]{1,0:T(8,128)(2,1)S(1)}, bf16[206,1536]{1,0:T(8,128)(2,1)S(1)}, u32[]{:S(2)}, u32[]{:S(2)}) collective-permute-start(bf16[206,1536]{1,0:T(8,128)(2,1)S(1)} %get-tuple-element.321), channel_id=1, source_target_pairs={{0,2},{2,0},{4,6},{6,4},{1,3},{3,1},{5,7},{7,5},{8,10},{10,8},{12,... | collective-permute-start | bytes 1898504 | tf_op jit(solution)/shard_map/ppermute | solution.py:363
  294.7 31.8 %collective-permute-start.12 = (bf16[206,1536]{1,0:T(8,128)(2,1)S(1)}, bf16[206,1536]{1,0:T(8,128)(2,1)S(1)}, u32[]{:S(2)}, u32[]{:S(2)}) collective-permute-start(bf16[206,1536]{1,0:T(8,128)(2,1)S(1)} %get-tuple-element.322), channel_id=1, source_target_pairs={{0,6},{2,4},{4,2},{6,0},{1,7},{3,5},{5,3},{7,1},{8,14},{10,12},{12... | collective-permute-start | bytes 1898504 | tf_op jit(solution)/shard_map/ppermute | solution.py:363
  296.3 31.6 %collective-permute-start.13 = (bf16[206,1536]{1,0:T(8,128)(2,1)S(1)}, bf16[206,1536]{1,0:T(8,128)(2,1)S(1)}, u32[]{:S(2)}, u32[]{:S(2)}) collective-permute-start(bf16[206,1536]{1,0:T(8,128)(2,1)S(1)} %get-tuple-element.323), channel_id=1, source_target_pairs={{0,4},{2,6},{4,0},{6,2},{1,5},{3,7},{5,1},{7,3},{8,12},{10,14},{12... | collective-permute-start | bytes 1898504 | tf_op jit(solution)/shard_map/ppermute | solution.py:363
  300.0 34.1 %collective-permute-start.9 = (bf16[512,768]{0,1:T(8,128)(2,1)S(1)}, bf16[512,768]{0,1:T(8,128)(2,1)S(1)}, u32[]{:S(2)}, u32[]{:S(2)}) collective-permute-start(bf16[512,768]{0,1:T(8,128)(2,1)S(1)} %broadcast_select_fusion.1), channel_id=1, source_target_pairs={{0,1},{1,0},{2,3},{3,2},{4,5},{5,4},{6,7},{7,6},{8,9},{9,8},{10,11... | collective-permute-start | bytes 2359304 | tf_op jit(solution)/shard_map/ppermute | solution.py:164
  328.7 5.5 %copy-start.17 = (f32[512,768]{0,1:T(8,128)S(1)}, f32[512,768]{0,1:T(8,128)}, u32[]{:S(2)}) copy-start(f32[512,768]{0,1:T(8,128)} %copy-done.15) | copy-start | bytes 4718596
  328.9 11.5 %collective-permute-start.17 = (bf16[62,1536]{1,0:T(8,128)(2,1)S(1)}, bf16[62,1536]{1,0:T(8,128)(2,1)S(1)}, u32[]{:S(2)}, u32[]{:S(2)}) collective-permute-start(bf16[62,1536]{1,0:T(8,128)(2,1)S(1)} %get-tuple-element.332), channel_id=1, source_target_pairs={{0,8},{8,16},{16,24},{24,0},{1,9},{9,17},{17,25},{25,1},{2,10},{10... | collective-permute-start | bytes 571400 | tf_op jit(solution)/shard_map/ppermute | solution.py:400
  330.9 11.3 %collective-permute-start.15 = (bf16[62,1536]{1,0:T(8,128)(2,1)S(1)}, bf16[62,1536]{1,0:T(8,128)(2,1)S(1)}, u32[]{:S(2)}, u32[]{:S(2)}) collective-permute-start(bf16[62,1536]{1,0:T(8,128)(2,1)S(1)} %get-tuple-element.333), channel_id=1, source_target_pairs={{0,24},{8,0},{16,8},{24,16},{1,25},{9,1},{17,9},{25,17},{2,26},{10... | collective-permute-start | bytes 571400 | tf_op jit(solution)/shard_map/ppermute | solution.py:400
  333.2 18.3 %collective-permute-start.16 = (bf16[62,1536]{1,0:T(8,128)(2,1)S(1)}, bf16[62,1536]{1,0:T(8,128)(2,1)S(1)}, u32[]{:S(2)}, u32[]{:S(2)}) collective-permute-start(bf16[62,1536]{1,0:T(8,128)(2,1)S(1)} %get-tuple-element.334), channel_id=1, source_target_pairs={{0,16},{8,24},{16,0},{24,8},{1,17},{9,25},{17,1},{25,9},{2,18},{10... | collective-permute-start | bytes 571400 | tf_op jit(solution)/shard_map/ppermute | solution.py:400
  353.1 20.6 %copy-start.1 = (bf16[768,1536]{1,0:T(8,128)(2,1)S(1)}, bf16[768,1536]{1,0:T(8,128)(2,1)}, u32[]{:S(2)}) copy-start(bf16[768,1536]{1,0:T(8,128)(2,1)} %param.88) | copy-start | bytes 7077892
  355.6 8.7 %collective-permute-start.20 = (bf16[48,1536]{1,0:T(8,128)(2,1)S(1)}, bf16[48,1536]{1,0:T(8,128)(2,1)S(1)}, u32[]{:S(2)}, u32[]{:S(2)}) collective-permute-start(bf16[48,1536]{1,0:T(8,128)(2,1)S(1)} %get-tuple-element.347), channel_id=1, source_target_pairs={{0,8},{8,16},{16,24},{24,0},{1,9},{9,17},{17,25},{25,1},{2,10},{10... | collective-permute-start | bytes 442376 | tf_op jit(solution)/shard_map/ppermute | solution.py:400
  355.6 13.8 %collective-permute-start.19 = (bf16[48,1536]{1,0:T(8,128)(2,1)S(1)}, bf16[48,1536]{1,0:T(8,128)(2,1)S(1)}, u32[]{:S(2)}, u32[]{:S(2)}) collective-permute-start(bf16[48,1536]{1,0:T(8,128)(2,1)S(1)} %get-tuple-element.348), channel_id=1, source_target_pairs={{0,16},{8,24},{16,0},{24,8},{1,17},{9,25},{17,1},{25,9},{2,18},{10... | collective-permute-start | bytes 442376 | tf_op jit(solution)/shard_map/ppermute | solution.py:400
  357.3 12.1 %collective-permute-start.18 = (bf16[48,1536]{1,0:T(8,128)(2,1)S(1)}, bf16[48,1536]{1,0:T(8,128)(2,1)S(1)}, u32[]{:S(2)}, u32[]{:S(2)}) collective-permute-start(bf16[48,1536]{1,0:T(8,128)(2,1)S(1)} %get-tuple-element.349), channel_id=1, source_target_pairs={{0,24},{8,0},{16,8},{24,16},{1,25},{9,1},{17,9},{25,17},{2,26},{10... | collective-permute-start | bytes 442376 | tf_op jit(solution)/shard_map/ppermute | solution.py:400
  (145 other events, 298.9 us)
Sparse Core Ops, SparseCore 0:
  172.3 168.5 reduce-scatter.1

commit v4 on v1

--- a/solution.py
+++ b/solution.py
@@ -369,7 +369,7 @@
             middle = jnp.concatenate(
                 [middle, jnp.broadcast_to(pair[None], (outer_size,) + pair.shape)], 1
             )
-        if outer_size > 4:
+        if outer_size > 4 or extra is not None:
             second = lax.all_to_all(middle, "outer", 0, 0, tiled=True)
             return jnp.sum(second.astype(jnp.float32), 0)
         place = lax.axis_index("outer")

time: 375 us -> 389 us (1.037)
  local copies, waits for them, and re-layouts: 68 us -> 77.9 us
  other arithmetic: 72.9 us -> 78.3 us
  matrix products: 148 us -> 144 us
    all_to_all x2, waiting for transfers between devices: 7.35 us -> 15.7 us  [exchange_sum(): first = lax.all_to_all(staged, 'inner', 0, 0, tiled=True)]
    ppermute x6 -> x3, waiting for transfers between devices: 26 us -> 19.1 us  [exchange_sum(): lax.ppermute(piece, 'outer', [(peer, (peer + shift) % outer_size) for pee...]
    unnamed x375 -> x371, local copies, waits for them, and re-layouts: 30.3 us -> 35.8 us
    ppermute x6 -> x3, starting transfers between devices: 11 us -> 5.9 us  [exchange_sum(): lax.ppermute(piece, 'outer', [(peer, (peer + shift) % outer_size) for pee...]
    all_to_all x0 -> x1, starting transfers between devices: none -> 4.59 us  [exchange_sum(): second = lax.all_to_all(middle, 'outer', 0, 0, tiled=True)]
  transfers between devices with their start and end apart: 21 -> 19, of which waited for: 8 -> 6; matrix products, arithmetic and copies ran while one was open for 40% -> 41% of each run, Pallas kernels for 0% -> 0%
where the time goes in v4:
time: 389 us; the launch traced here: 381 us
  matrix products  144 us (37%)
  other arithmetic  78.3 us (20%)
  local copies, waits for them, and re-layouts  77.9 us (20%)
  waiting for transfers between devices  39.5 us (10%)
  starting transfers between devices  24.6 us (6%)
  between operations  16.9 us (4%)
    dot_general x30, matrix products, project(): return jnp.dot(data, weight, preferred_element_type=jnp.float32)  68.8 us
    unnamed x371, local copies, waits for them, and re-layouts  35.8 us
    dot_general x6, matrix products, attend_backward(): jnp.einsum('qhe,khe->hqk', grad_piece, values[:end], preferred_element_ty...  19.3 us
    ppermute x3, waiting for transfers between devices, exchange_sum(): lax.ppermute(piece, 'outer', [(peer, (peer + shift) % outer_size) for pee...  19.1 us
    dot_general x6, matrix products, attend_forward(): jnp.einsum('hqk,khe->qhe', weights, values[:end], preferred_element_type=...  18.7 us
    reduce_sum x5, other arithmetic, attend_forward(): summed = jnp.sum(powers, -1, keepdims=True)  15.8 us
    all_to_all x2, waiting for transfers between devices, exchange_sum(): first = lax.all_to_all(staged, 'inner', 0, 0, tiled=True)  15.7 us
    dot_general x6, matrix products, attend_forward(): jnp.einsum('qhe,khe->hqk', piece, keys[:end], preferred_element_type=jnp....  13.2 us
  transfers between devices with their start and end apart: 19, of which 6 were waited for; matrix products, arithmetic and copies ran while one was open for 41% of the time, Pallas kernels for 0%

profile of v4, /device:TPU:0, one launch (start us, length us, event | category | flops | bytes accessed | tf_op | source)
XLA Modules:
  0.0 381.5 jit_solution(2980677039696170745)
XLA Ops:
  12.4 2.5 add_convert_fusion.8
  21.4 2.4 multiply_convert_fusion.8
  31.0 2.2 fusion.164
  36.6 2.3 fusion.163
  42.8 2.9 fusion.162
  48.1 1.8 slice_select_fusion
  54.0 2.9 fusion.153
  63.2 6.6 %select_reduce_fusion = (f32[6,512]{1,0:T(8,128)S(1)}, f32[6,512,1024]{2,1,0:T(8,128)}) fusion(pred[512,1024]{1,0:T(8,128)(4,1)S(1)} %get-tuple-element.417, bf16[512,6,64]{0,2,1:T(8,128)(2,1)S(1)} %bitcast.324, bf16[1024,6,64]{0,2,1:T(8,128)(2,1)S(1)} %bitcast.312), kind=kOutput, calls=%fused_computation.12 | convolution fusion | flops 408941568 | bytes 14299136 | tf_op jit(solution)/shard_map/qhe,khe->hqk/dot_general | solution.py:54
  69.8 2.1 select_reduce_fusion.1
  72.0 12.1 %fusion = (f32[6,512]{1,0:T(8,128)S(1)}, f32[6,512]{1,0:T(8,128)S(1)}) fusion(f32[6,512,1024]{2,1,0:T(8,128)S(1)} %get-tuple-element.435, f32[6,512]{1,0:T(8,128)S(1)} %get-tuple-element.434, pred[512,1024]{1,0:T(8,128)(4,1)S(1)} %get-tuple-element.416, f32[6,512]{1,0:T(8,128)S(1)} %get-tuple-element.432, f32[6,512,1024]{2,1,0:T(8,128)} %get-tuple-element.433, ...), kind=kLoop, calls=%fused_computation.8 | loop fusion | flops 18868224 | bytes 26263552 | tf_op jit(solution)/shard_map/reduce_sum | solution.py:64
  84.1 6.9 %fusion.82 = f32[512,6,64]{0,2,1:T(8,128)S(1)} fusion(bf16[1024,6,64]{0,2,1:T(8,128)(2,1)S(1)} %bitcast.404, f32[6,512,1024]{2,1,0:T(8,128)} %get-tuple-element.433, f32[6,512]{1,0:T(8,128)S(1)} %get-tuple-element.452, f32[6,512]{1,0:T(8,128)S(1)} %get-tuple-element.432, pred[512,1024]{1,0:T(8,128)(4,1)S(1)} %get-tuple-element.417), kind=kOutput, calls=%fused_computation.181 | convolution fusion | flops 415236096 | bytes 14704640 | tf_op jit(solution)/shard_map/hqk,khe->qhe/dot_general | solution.py:67
  91.0 3.2 fusion.83
  97.4 1.9 collective-permute-done.2
  100.9 1.9 collective-permute-done.3
  103.4 18.2 %multiply_convert_fusion.3 = (bf16[1024,1536]{1,0:T(8,128)(2,1)S(1)}, f32[1024,1536]{1,0:T(8,128)}, f32[1024,1536]{1,0:T(8,128)}) fusion(f32[1536]{0:T(1024)S(1)} %convert_element_type.361, bf16[768,1536]{1,0:T(8,128)(2,1)S(1)} %copy-done, bf16[512,768]{0,1:T(8,128)(2,1)S(1)} %get-tuple-element.380, bf16[512,768]{0,1:T(8,128)(2,1)S(1)} %get-tuple-element.379), kind=kOutput, calls=%fused_computation.24 | convolution fusion | flops 2522873856 | bytes 19666944 | tf_op jit(solution)/shard_map/dot_general | solution.py:25
  121.6 3.8 convolution_convert_fusion.5
  127.0 1.8 copy.150
  128.8 2.7 copy.135
  131.5 1.7 copy.151
  133.3 1.8 copy.152
  135.0 1.7 copy.153
  140.1 3.2 fusion.150
  145.7 2.7 convert_reduce_fusion.3
  148.4 6.9 %convert_reduce_fusion = (f32[1536]{0:T(1024)S(1)}, bf16[1024,1536]{1,0:T(8,128)(2,1)S(1)}) fusion(f32[1024,1536]{1,0:T(8,128)S(1)} %bitcast.409, bf16[1536,768]{1,0:T(8,128)(2,1)S(1)} %copy-done.159, f32[1024,768]{0,1:T(8,128)S(1)} %get-tuple-element.360, f32[1024,1536]{1,0:T(8,128)} %get-tuple-element.436, f32[1536]{0:T(1024)S(1)} %copy-done.141), kind=kOutput, calls=%fused_computation.18 | convolution fusion | flops 2443442688 | bytes 21245952 | tf_op jit(solution)/shard_map/dot_general | solution.py:25
  155.4 2.6 convolution_convert_fusion.4
  160.2 2.8 convolution_convert_fusion
  166.4 3.0 convolution_convert_fusion.1
  169.5 2.8 pad_maximum_fusion
  177.2 7.1 %multiply_convert_fusion.1 = bf16[6,512,1024]{2,1,0:T(8,128)(2,1)S(1)} fusion(f32[6,512,1024]{2,1,0:T(8,128)} %copy-done.2, f32[6,512]{1,0:T(8,128)S(1)} %get-tuple-element.411, f32[6,512]{1,0:T(8,128)S(1)} %log_add_fusion.1, pred[512,1024]{1,0:T(8,128)(4,1)S(1)} %get-tuple-element.416, bf16[512,6,64]{0,2,1:T(8,128)(2,1)S(1)} %bitcast.379, ...), kind=kOutput, calls=%fused_computation.2 | convolution fusion | flops 418381824 | bytes 20602880 | tf_op jit(solution)/shard_map/qhe,khe->hqk/dot_general | solution.py:95
  184.4 2.0 convolution_convert_fusion.19
  187.7 2.9 fusion.5
  190.6 6.1 %multiply_convert_fusion = bf16[6,512,1024]{2,1,0:T(8,128)(2,1)S(1)} fusion(f32[6,512,1024]{2,1,0:T(8,128)S(1)} %bitcast.307, f32[6,512]{1,0:T(8,128)S(1)} %get-tuple-element.410, f32[6,512]{1,0:T(8,128)S(1)} %log_add_fusion, pred[512,1024]{1,0:T(8,128)(4,1)S(1)} %get-tuple-element.417, bf16[512,6,64]{0,2,1:T(8,128)(2,1)S(1)} %bitcast.382, ...), kind=kOutput, calls=%fused_computation | convolution fusion | flops 418381824 | bytes 20602880 | tf_op jit(solution)/shard_map/qhe,khe->hqk/dot_general | solution.py:95
  196.7 2.0 convolution_convert_fusion.18
  203.1 3.4 convert_reduce_fusion.7
  211.9 1.7 convolution_convert_fusion.14
  213.6 2.3 convolution_convert_fusion.17
  220.0 1.6 add_add_fusion.5
  226.6 2.9 copy.156
  229.4 1.7 copy.157
  231.1 5.1 %all-to-all-start.2 = ((bf16[4,192,1536]{2,1,0:T(8,128)(2,1)}), bf16[4,192,1536]{2,1,0:T(8,128)(2,1)}, u32[]{:S(2)}, u32[]{:S(2)}) async-start(bf16[4,192,1536]{2,1,0:T(8,128)(2,1)} %bitcast.319), calls=%async_computation.2 | async-start | bytes 4718592 | tf_op jit(solution)/shard_map/all_to_all | solution.py:357
  248.9 1.7 multiply_convert_fusion.4
  250.8 2.5 convert_reduce_fusion.9
  253.3 2.5 multiply_convert_fusion.2
  263.0 3.2 fusion.90
  272.8 1.6 fusion.88
  275.1 2.1 copy.149
  277.2 2.1 copy.148
  279.3 2.1 copy.147
  286.1 1.6 pad_maximum_fusion.1
  287.7 4.8 %all-to-all-start = ((bf16[4,206,1536]{2,1,0:T(8,128)(2,1)}), bf16[4,206,1536]{2,1,0:T(8,128)(2,1)}, u32[]{:S(2)}, u32[]{:S(2)}) async-start(bf16[4,206,1536]{2,1,0:T(8,128)(2,1)} %pad_maximum_fusion.1), calls=%async_computation | async-start | bytes 5111808 | tf_op jit(solution)/shard_map/all_to_all | solution.py:357
  292.7 2.6 copy.158
  295.3 3.1 convert_add_fusion
  298.4 3.1 copy.160
  307.2 3.0 reduce_sum.406
  310.3 15.7 %all-to-all-done = bf16[4,206,1536]{2,1,0:T(8,128)(2,1)} async-done(((bf16[4,206,1536]{2,1,0:T(8,128)(2,1)}), bf16[4,206,1536]{2,1,0:T(8,128)(2,1)}, u32[]{:S(2)}, u32[]{:S(2)}) %all-to-all-start) | async-done | bytes 2531360 | tf_op jit(solution)/shard_map/all_to_all | solution.py:357
  325.9 2.3 convert_reduce_fusion.1
  329.3 4.6 %all-to-all-start.1 = ((bf16[4,62,1536]{2,1,0:T(8,128)(2,1)}), bf16[4,62,1536]{2,1,0:T(8,128)(2,1)S(1)}, u32[]{:S(2)}, u32[]{:S(2)}) async-start(bf16[4,62,1536]{2,1,0:T(8,128)(2,1)} %pad_maximum_fusion.11), calls=%async_computation.1 | async-start | bytes 1572864 | tf_op jit(solution)/shard_map/all_to_all | solution.py:373
  335.0 2.1 collective-permute-start.14
  337.1 2.4 collective-permute-start.13
  340.9 3.2 add_add_fusion.4
  344.1 3.0 copy.159
  347.1 9.6 %collective-permute-done.14 = bf16[48,1536]{1,0:T(8,128)(2,1)S(1)} collective-permute-done((bf16[48,1536]{1,0:T(8,128)(2,1)S(1)}, bf16[48,1536]{1,0:T(8,128)(2,1)S(1)}, u32[]{:S(2)}, u32[]{:S(2)}) %collective-permute-start.14) | collective-permute-done | bytes 147488 | tf_op jit(solution)/shard_map/ppermute | solution.py:382
  356.7 9.5 %collective-permute-done.13 = bf16[48,1536]{1,0:T(8,128)(2,1)S(1)} collective-permute-done((bf16[48,1536]{1,0:T(8,128)(2,1)S(1)}, bf16[48,1536]{1,0:T(8,128)(2,1)S(1)}, u32[]{:S(2)}, u32[]{:S(2)}) %collective-permute-start.13) | collective-permute-done | bytes 147488 | tf_op jit(solution)/shard_map/ppermute | solution.py:382
  372.7 1.6 slice.717
  (569 shorter events, 127.9 us)
Async XLA Ops:
  7.2 96.2 %copy-start = (bf16[768,1536]{1,0:T(8,128)(2,1)S(1)}, bf16[768,1536]{1,0:T(8,128)(2,1)}, u32[]{:S(2)}) copy-start(bf16[768,1536]{1,0:T(8,128)(2,1)} %param.88) | copy-start | bytes 7077892
  7.2 363.7 %reduce-scatter.2.cloned.1.call-start = ((), (), s32[]{:S(2)}) async-start(), calls=%async_computation.4 | async-start | bytes 5013504 | tf_op jit(solution)/shard_map/reduce_scatter | solution.py:400
  12.4 5.0 %copy-start.108 = (bf16[768,384]{1,0:T(8,128)(2,1)S(1)}, bf16[768,384]{1,0:T(8,128)(2,1)}, u32[]{:S(2)}) copy-start(bf16[768,384]{1,0:T(8,128)(2,1)} %param.70) | copy-start | bytes 1769476
  12.4 5.0 %copy-start.115 = (bf16[1024,768]{1,0:T(8,128)(2,1)S(1)}, bf16[1024,768]{1,0:T(8,128)(2,1)}, u32[]{:S(2)}) copy-start(bf16[1024,768]{1,0:T(8,128)(2,1)} %param.64) | copy-start | bytes 4718596
  18.2 20.7 %copy-start.27 = (bf16[1024,384]{0,1:T(8,128)(2,1)}, bf16[1024,384]{0,1:T(8,128)(2,1)S(1)}, u32[]{:S(2)}) copy-start(bf16[1024,384]{0,1:T(8,128)(2,1)S(1)} %convolution_convert_fusion.9) | copy-start | bytes 2359300
  19.0 9.9 %copy-start.45 = (bf16[512,384]{0,1:T(8,128)(2,1)}, bf16[512,384]{0,1:T(8,128)(2,1)S(1)}, u32[]{:S(2)}) copy-start(bf16[512,384]{0,1:T(8,128)(2,1)S(1)} %slice.659) | copy-start | bytes 1179652
  25.8 16.0 %copy-start.43 = (pred[256,1024]{1,0:T(8,128)(4,1)}, pred[256,1024]{1,0:T(8,128)(4,1)S(1)}, u32[]{:S(2)}) copy-start(pred[256,1024]{1,0:T(8,128)(4,1)S(1)} %fusion.94) | copy-start | bytes 786436
  28.7 17.0 %copy-start.87 = (f32[256,6,64]{0,2,1:T(8,128)}, f32[256,6,64]{0,2,1:T(8,128)S(1)}, u32[]{:S(2)}) copy-start(f32[256,6,64]{0,2,1:T(8,128)S(1)} %get-tuple-element.450) | copy-start | bytes 1179652
  33.2 12.6 %copy-start.89 = (f32[256,6,64]{0,2,1:T(8,128)}, f32[256,6,64]{0,2,1:T(8,128)S(1)}, u32[]{:S(2)}) copy-start(f32[256,6,64]{0,2,1:T(8,128)S(1)} %get-tuple-element.448) | copy-start | bytes 1179652
  39.0 6.9 %copy-start.91 = (f32[256,6,64]{0,2,1:T(8,128)}, f32[256,6,64]{0,2,1:T(8,128)S(1)}, u32[]{:S(2)}) copy-start(f32[256,6,64]{0,2,1:T(8,128)S(1)} %get-tuple-element.446) | copy-start | bytes 1179652
  41.8 4.0 %copy-start.132 = (f32[6,256]{1,0:T(8,128)}, f32[6,256]{1,0:T(8,128)S(1)}, u32[]{:S(2)}) copy-start(f32[6,256]{1,0:T(8,128)S(1)} %fusion.22) | copy-start | bytes 18436
  50.2 3.9 %collective-permute-start = (f32[512,768]{0,1:T(8,128)}, f32[512,768]{0,1:T(8,128)}, u32[]{:S(2)}, u32[]{:S(2)}) collective-permute-start(f32[512,768]{0,1:T(8,128)} %slice_select_fusion), channel_id=1, source_target_pairs={{0,1},{1,0},{2,3},{3,2},{4,5},{5,4},{6,7},{7,6},{8,9},{9,8},{10,11... | collective-permute-start | bytes 4718600 | tf_op jit(solution)/shard_map/ppermute | solution.py:164
  57.0 42.3 %copy-start.3 = (f32[512,768]{0,1:T(8,128)}, f32[512,768]{0,1:T(8,128)S(1)}, u32[]{:S(2)}) copy-start(f32[512,768]{0,1:T(8,128)S(1)} %get-tuple-element.373) | copy-start | bytes 4718596
  57.6 3.3 collective-permute-start.1
  60.0 9.8 %copy-start.25 = (bf16[1024,384]{0,1:T(8,128)(2,1)}, bf16[1024,384]{0,1:T(8,128)(2,1)S(1)}, u32[]{:S(2)}) copy-start(bf16[1024,384]{0,1:T(8,128)(2,1)S(1)} %convolution_convert_fusion.8) | copy-start | bytes 2359300
  60.8 30.1 %copy-start.167 = (bf16[1024,384]{0,1:T(8,128)(2,1)}, bf16[1024,384]{0,1:T(8,128)(2,1)S(1)}, u32[]{:S(2)}) copy-start(bf16[1024,384]{0,1:T(8,128)(2,1)S(1)} %add_convert_fusion.7) | copy-start | bytes 2359300
  63.2 6.7 %copy-start.39 = (bf16[512,384]{0,1:T(8,128)(2,1)}, bf16[512,384]{0,1:T(8,128)(2,1)S(1)}, u32[]{:S(2)}) copy-start(bf16[512,384]{0,1:T(8,128)(2,1)S(1)} %get-tuple-element.390) | copy-start | bytes 1179652
  63.2 6.7 %copy-start.41 = (bf16[512,384]{0,1:T(8,128)(2,1)}, bf16[512,384]{0,1:T(8,128)(2,1)S(1)}, u32[]{:S(2)}) copy-start(bf16[512,384]{0,1:T(8,128)(2,1)S(1)} %get-tuple-element.389) | copy-start | bytes 1179652
  72.0 19.0 %copy-start.2 = (f32[6,512,1024]{2,1,0:T(8,128)}, f32[6,512,1024]{2,1,0:T(8,128)S(1)}, u32[]{:S(2)}) copy-start(f32[6,512,1024]{2,1,0:T(8,128)S(1)} %get-tuple-element.435) | copy-start | bytes 37748740
  96.9 2.4 collective-permute-start.2
  100.5 2.4 collective-permute-start.3
  100.9 20.6 %copy-start.140 = (f32[1536]{0:T(1024)}, f32[1536]{0:T(1024)S(1)}, u32[]{:S(2)}) copy-start(f32[1536]{0:T(1024)S(1)} %convert_element_type.361) | copy-start | bytes 18436
  103.3 18.2 %copy-start.51 = (bf16[512,768]{0,1:T(8,128)(2,1)}, bf16[512,768]{0,1:T(8,128)(2,1)S(1)}, u32[]{:S(2)}) copy-start(bf16[512,768]{0,1:T(8,128)(2,1)S(1)} %get-tuple-element.379) | copy-start | bytes 2359300
  103.3 18.2 %copy-start.53 = (bf16[512,768]{0,1:T(8,128)(2,1)}, bf16[512,768]{0,1:T(8,128)(2,1)S(1)}, u32[]{:S(2)}) copy-start(bf16[512,768]{0,1:T(8,128)(2,1)S(1)} %get-tuple-element.380) | copy-start | bytes 2359300
  103.4 18.2 %copy-start.158 = (bf16[1536,768]{1,0:T(8,128)(2,1)S(1)}, bf16[1536,768]{1,0:T(8,128)(2,1)}, u32[]{:S(2)}) copy-start(bf16[1536,768]{1,0:T(8,128)(2,1)} %param.90) | copy-start | bytes 7077892
  121.6 3.8 %copy-start.169 = (bf16[1024,1536]{1,0:T(8,128)(2,1)}, bf16[1024,1536]{1,0:T(8,128)(2,1)S(1)}, u32[]{:S(2)}) copy-start(bf16[1024,1536]{1,0:T(8,128)(2,1)S(1)} %get-tuple-element.368) | copy-start | bytes 9437188
  121.6 4.2 %copy-start.151 = (bf16[768]{0:T(1024)(128)(2,1)S(1)}, bf16[768]{0:T(1024)(128)(2,1)}, u32[]{:S(2)}) copy-start(bf16[768]{0:T(1024)(128)(2,1)} %param.86) | copy-start | bytes 4612
  121.6 4.2 %copy-start.152 = (bf16[768]{0:T(1024)(128)(2,1)S(1)}, bf16[768]{0:T(1024)(128)(2,1)}, u32[]{:S(2)}) copy-start(bf16[768]{0:T(1024)(128)(2,1)} %param.87) | copy-start | bytes 4612
  121.6 4.8 %copy-start.153 = (bf16[768]{0:T(1024)(128)(2,1)S(1)}, bf16[768]{0:T(1024)(128)(2,1)}, u32[]{:S(2)}) copy-start(bf16[768]{0:T(1024)(128)(2,1)} %param.91) | copy-start | bytes 4612
  125.4 14.7 %collective-permute-start.4 = (bf16[1024,768]{0,1:T(8,128)(2,1)}, bf16[1024,768]{0,1:T(8,128)(2,1)}, u32[]{:S(2)}, u32[]{:S(2)}) collective-permute-start(bf16[1024,768]{0,1:T(8,128)(2,1)} %convolution_convert_fusion.5), channel_id=1, source_target_pairs={{0,1},{1,0},{2,3},{3,2},{4,5},{5,4},{6,7},{7,6},{8,9},{9,8},{10,11... | collective-permute-start | bytes 4718600 | tf_op jit(solution)/shard_map/ppermute | solution.py:164
  127.0 9.8 %copy-start.126 = (f32[6,256]{1,0:T(8,128)S(1)}, f32[6,256]{1,0:T(8,128)}, u32[]{:S(2)}) copy-start(f32[6,256]{1,0:T(8,128)} %copy-done.125) | copy-start | bytes 18436
  127.0 9.8 %copy-start.129 = (f32[6,256]{1,0:T(8,128)S(1)}, f32[6,256]{1,0:T(8,128)}, u32[]{:S(2)}) copy-start(f32[6,256]{1,0:T(8,128)} %copy-done.128) | copy-start | bytes 18436
  143.3 5.1 %slice-start.10 = ((s8[6291456]{0:T(1024)(128)(4,1)}), s8[4194304]{0:T(1024)(128)(4,1)S(1)}, s32[]{:S(2)}) async-start(s8[6291456]{0:T(1024)(128)(4,1)} %bitcast.408), calls=%async_computation.15 | async-start | bytes 8388608
  144.1 4.3 %slice-start.11 = ((s8[6291456]{0:T(1024)(128)(4,1)}), s8[2097152]{0:T(1024)(128)(4,1)S(1)}, s32[]{:S(2)}) async-start(s8[6291456]{0:T(1024)(128)(4,1)} %bitcast.408), calls=%async_computation.16 | async-start | bytes 4194304
  155.4 4.8 %copy-start.170 = (bf16[1024,1536]{1,0:T(8,128)(2,1)S(1)}, bf16[1024,1536]{1,0:T(8,128)(2,1)}, u32[]{:S(2)}) copy-start(bf16[1024,1536]{1,0:T(8,128)(2,1)} %copy-done.169) | copy-start | bytes 9437188
  158.1 4.9 %collective-permute-start.5 = (bf16[512,768]{0,1:T(8,128)(2,1)S(1)}, bf16[512,768]{0,1:T(8,128)(2,1)S(1)}, u32[]{:S(2)}, u32[]{:S(2)}) collective-permute-start(bf16[512,768]{0,1:T(8,128)(2,1)S(1)} %broadcast_select_fusion.7), channel_id=1, source_target_pairs={{0,1},{1,0},{2,3},{3,2},{4,5},{5,4},{6,7},{7,6},{8,9},{9,8},{10,11... | collective-permute-start | bytes 2359304 | tf_op jit(solution)/shard_map/ppermute | solution.py:164
  165.8 6.4 %collective-permute-start.6 = (bf16[512,768]{0,1:T(8,128)(2,1)S(1)}, bf16[512,768]{0,1:T(8,128)(2,1)}, u32[]{:S(2)}, u32[]{:S(2)}) collective-permute-start(bf16[512,768]{0,1:T(8,128)(2,1)S(1)} %add_convert_fusion.10), channel_id=1, source_target_pairs={{0,1},{1,0},{2,3},{3,2},{4,5},{5,4},{6,7},{7,6},{8,9},{9,8},{10,11... | collective-permute-start | bytes 2359304 | tf_op jit(solution)/shard_map/ppermute | solution.py:164
  174.9 36.2 %copy-start.59 = (bf16[512,768]{0,1:T(8,128)(2,1)}, bf16[512,768]{0,1:T(8,128)(2,1)S(1)}, u32[]{:S(2)}) copy-start(bf16[512,768]{0,1:T(8,128)(2,1)S(1)} %get-tuple-element.377) | copy-start | bytes 2359300
  175.0 36.2 %copy-start.61 = (bf16[512,768]{0,1:T(8,128)(2,1)}, bf16[512,768]{0,1:T(8,128)(2,1)S(1)}, u32[]{:S(2)}) copy-start(bf16[512,768]{0,1:T(8,128)(2,1)S(1)} %get-tuple-element.378) | copy-start | bytes 2359300
  177.2 7.2 %copy-start.26 = (bf16[1024,384]{0,1:T(8,128)(2,1)S(1)}, bf16[1024,384]{0,1:T(8,128)(2,1)}, u32[]{:S(2)}) copy-start(bf16[1024,384]{0,1:T(8,128)(2,1)} %copy-done.25) | copy-start | bytes 2359300
  177.2 10.4 %slice-start.3 = ((s8[12582912]{0:T(1024)(128)(4,1)}), s8[4194304]{0:T(1024)(128)(4,1)S(1)}, s32[]{:S(2)}) async-start(s8[12582912]{0:T(1024)(128)(4,1)} %bitcast.306), calls=%async_computation.8 | async-start | bytes 8388608
  177.2 10.4 %slice-start.4 = ((s8[12582912]{0:T(1024)(128)(4,1)}), s8[4194304]{0:T(1024)(128)(4,1)S(1)}, s32[]{:S(2)}) async-start(s8[12582912]{0:T(1024)(128)(4,1)} %bitcast.306), calls=%async_computation.9 | async-start | bytes 8388608
  186.4 20.1 %copy-start.85 = (bf16[6,64,512]{2,1,0:T(8,128)(2,1)}, bf16[6,64,512]{2,1,0:T(8,128)(2,1)S(1)}, u32[]{:S(2)}) copy-start(bf16[6,64,512]{2,1,0:T(8,128)(2,1)S(1)} %convolution_convert_fusion.19) | copy-start | bytes 1179652
  196.7 6.1 %slice-start = ((s8[12582912]{0:T(1024)(128)(4,1)}), s8[4194304]{0:T(1024)(128)(4,1)S(1)}, s32[]{:S(2)}) async-start(s8[12582912]{0:T(1024)(128)(4,1)} %bitcast.304), calls=%async_computation.5 | async-start | bytes 8388608
  198.8 4.1 %slice-start.1 = ((s8[12582912]{0:T(1024)(128)(4,1)}), s8[4194304]{0:T(1024)(128)(4,1)S(1)}, s32[]{:S(2)}) async-start(s8[12582912]{0:T(1024)(128)(4,1)} %bitcast.304), calls=%async_computation.6 | async-start | bytes 8388608
  198.8 4.4 %slice-start.2 = ((s8[12582912]{0:T(1024)(128)(4,1)}), s8[4194304]{0:T(1024)(128)(4,1)S(1)}, s32[]{:S(2)}) async-start(s8[12582912]{0:T(1024)(128)(4,1)} %bitcast.304), calls=%async_computation.7 | async-start | bytes 8388608
  208.7 10.1 %collective-permute-start.7 = (bf16[512,768]{0,1:T(8,128)(2,1)}, bf16[512,768]{0,1:T(8,128)(2,1)}, u32[]{:S(2)}, u32[]{:S(2)}) collective-permute-start(bf16[512,768]{0,1:T(8,128)(2,1)} %broadcast_select_fusion.4), channel_id=1, source_target_pairs={{0,1},{1,0},{2,3},{3,2},{4,5},{5,4},{6,7},{7,6},{8,9},{9,8},{10,11... | collective-permute-start | bytes 2359304 | tf_op jit(solution)/shard_map/ppermute | solution.py:164
  224.1 13.3 %collective-permute-start.8 = (bf16[512,768]{0,1:T(8,128)(2,1)}, bf16[512,768]{0,1:T(8,128)(2,1)}, u32[]{:S(2)}, u32[]{:S(2)}) collective-permute-start(bf16[512,768]{0,1:T(8,128)(2,1)} %add_convert_fusion.9), channel_id=1, source_target_pairs={{0,1},{1,0},{2,3},{3,2},{4,5},{5,4},{6,7},{7,6},{8,9},{9,8},{10,11... | collective-permute-start | bytes 2359304 | tf_op jit(solution)/shard_map/ppermute | solution.py:164
  225.4 10.8 %collective-permute-start.11 = (f32[3072]{0:T(1024)S(1)}, f32[3072]{0:T(1024)S(1)}, u32[]{:S(2)}, u32[]{:S(2)}) collective-permute-start(f32[3072]{0:T(1024)S(1)} %pad_maximum_fusion.18), channel_id=1, source_target_pairs={{0,1},{1,0},{2,3},{3,2},{4,5},{5,4},{6,7},{7,6},{8,9},{9,8},{10,11... | collective-permute-start | bytes 36872 | tf_op jit(solution)/shard_map/ppermute | solution.py:164
  226.4 68.9 %collective-permute-start.10 = (bf16[512,768]{0,1:T(8,128)(2,1)}, bf16[512,768]{0,1:T(8,128)(2,1)}, u32[]{:S(2)}, u32[]{:S(2)}) collective-permute-start(bf16[512,768]{0,1:T(8,128)(2,1)} %broadcast_select_fusion), channel_id=1, source_target_pairs={{0,1},{1,0},{2,3},{3,2},{4,5},{5,4},{6,7},{7,6},{8,9},{9,8},{10,11... | collective-permute-start | bytes 2359304 | tf_op jit(solution)/shard_map/ppermute | solution.py:164
  231.1 6.4 %copy-start.14 = (f32[512,768]{0,1:T(8,128)S(1)}, f32[512,768]{0,1:T(8,128)}, u32[]{:S(2)}) copy-start(f32[512,768]{0,1:T(8,128)} %copy-done.13) | copy-start | bytes 4718596
  231.1 56.7 %all-to-all-start.2 = ((bf16[4,192,1536]{2,1,0:T(8,128)(2,1)}), bf16[4,192,1536]{2,1,0:T(8,128)(2,1)}, u32[]{:S(2)}, u32[]{:S(2)}) async-start(bf16[4,192,1536]{2,1,0:T(8,128)(2,1)} %bitcast.319), calls=%async_computation.2 | async-start | bytes 4718592 | tf_op jit(solution)/shard_map/all_to_all | solution.py:357
  238.8 20.1 %copy-start.31 = (bf16[512,768]{0,1:T(8,128)(2,1)}, bf16[512,768]{0,1:T(8,128)(2,1)S(1)}, u32[]{:S(2)}) copy-start(bf16[512,768]{0,1:T(8,128)(2,1)S(1)} %get-tuple-element.376) | copy-start | bytes 2359300
  250.7 6.3 %copy-start.29 = (bf16[6,256,768]{2,1,0:T(8,128)(2,1)}, bf16[6,256,768]{2,1,0:T(8,128)(2,1)S(1)}, u32[]{:S(2)}) copy-start(bf16[6,256,768]{2,1,0:T(8,128)(2,1)S(1)} %multiply_convert_fusion.4) | copy-start | bytes 7077892
  258.9 4.1 %copy-start.49 = (bf16[1024,6,64]{0,2,1:T(8,128)(2,1)S(1)}, bf16[1024,6,64]{0,2,1:T(8,128)(2,1)}, u32[]{:S(2)}) copy-start(bf16[1024,6,64]{0,2,1:T(8,128)(2,1)} %get-tuple-element.438) | copy-start | bytes 2359300
  274.4 7.0 %copy-start.134 = (f32[1,1536]{1,0:T(1,128)S(1)}, f32[1,1536]{1,0:T(1,128)}, u32[]{:S(2)}) copy-start(f32[1,1536]{1,0:T(1,128)} %stack.28) | copy-start | bytes 18436
  274.4 8.4 %copy-start.32 = (bf16[512,768]{0,1:T(8,128)(2,1)S(1)}, bf16[512,768]{0,1:T(8,128)(2,1)}, u32[]{:S(2)}) copy-start(bf16[512,768]{0,1:T(8,128)(2,1)} %copy-done.31) | copy-start | bytes 2359300
  287.7 38.2 %all-to-all-start = ((bf16[4,206,1536]{2,1,0:T(8,128)(2,1)}), bf16[4,206,1536]{2,1,0:T(8,128)(2,1)}, u32[]{:S(2)}, u32[]{:S(2)}) async-start(bf16[4,206,1536]{2,1,0:T(8,128)(2,1)} %pad_maximum_fusion.1), calls=%async_computation | async-start | bytes 5111808 | tf_op jit(solution)/shard_map/all_to_all | solution.py:357
  307.2 33.7 %collective-permute-start.9 = (bf16[512,768]{0,1:T(8,128)(2,1)}, bf16[512,768]{0,1:T(8,128)(2,1)}, u32[]{:S(2)}, u32[]{:S(2)}) collective-permute-start(bf16[512,768]{0,1:T(8,128)(2,1)} %broadcast_select_fusion.1), channel_id=1, source_target_pairs={{0,1},{1,0},{2,3},{3,2},{4,5},{5,4},{6,7},{7,6},{8,9},{9,8},{10,11... | collective-permute-start | bytes 2359304 | tf_op jit(solution)/shard_map/ppermute | solution.py:164
  329.3 38.9 %all-to-all-start.1 = ((bf16[4,62,1536]{2,1,0:T(8,128)(2,1)}), bf16[4,62,1536]{2,1,0:T(8,128)(2,1)S(1)}, u32[]{:S(2)}, u32[]{:S(2)}) async-start(bf16[4,62,1536]{2,1,0:T(8,128)(2,1)} %pad_maximum_fusion.11), calls=%async_computation.1 | async-start | bytes 1572864 | tf_op jit(solution)/shard_map/all_to_all | solution.py:373
  335.0 21.7 %collective-permute-start.14 = (bf16[48,1536]{1,0:T(8,128)(2,1)S(1)}, bf16[48,1536]{1,0:T(8,128)(2,1)S(1)}, u32[]{:S(2)}, u32[]{:S(2)}) collective-permute-start(bf16[48,1536]{1,0:T(8,128)(2,1)S(1)} %get-tuple-element.395), channel_id=1, source_target_pairs={{0,8},{8,16},{16,24},{24,0},{1,9},{9,17},{17,25},{25,1},{2,10},{10... | collective-permute-start | bytes 442376 | tf_op jit(solution)/shard_map/ppermute | solution.py:382
  337.1 29.1 %collective-permute-start.13 = (bf16[48,1536]{1,0:T(8,128)(2,1)S(1)}, bf16[48,1536]{1,0:T(8,128)(2,1)S(1)}, u32[]{:S(2)}, u32[]{:S(2)}) collective-permute-start(bf16[48,1536]{1,0:T(8,128)(2,1)S(1)} %get-tuple-element.396), channel_id=1, source_target_pairs={{0,16},{8,24},{16,0},{24,8},{1,17},{9,25},{17,1},{25,9},{2,18},{10... | collective-permute-start | bytes 442376 | tf_op jit(solution)/shard_map/ppermute | solution.py:382
  339.4 26.8 %collective-permute-start.12 = (bf16[48,1536]{1,0:T(8,128)(2,1)S(1)}, bf16[48,1536]{1,0:T(8,128)(2,1)}, u32[]{:S(2)}, u32[]{:S(2)}) collective-permute-start(bf16[48,1536]{1,0:T(8,128)(2,1)S(1)} %get-tuple-element.397), channel_id=1, source_target_pairs={{0,24},{8,0},{16,8},{24,16},{1,25},{9,1},{17,9},{25,17},{2,26},{10... | collective-permute-start | bytes 442376 | tf_op jit(solution)/shard_map/ppermute | solution.py:382
  366.2 8.1 %copy-start.1 = (bf16[768,1536]{1,0:T(8,128)(2,1)S(1)}, bf16[768,1536]{1,0:T(8,128)(2,1)}, u32[]{:S(2)}) copy-start(bf16[768,1536]{1,0:T(8,128)(2,1)} %param.88) | copy-start | bytes 7077892
  (138 other events, 276.5 us)
Sparse Core Ops, SparseCore 0:
  172.4 173.8 reduce-scatter.1

commit v5 on v1

--- a/solution.py
+++ b/solution.py
@@ -44,7 +44,7 @@
 
 def attend_forward(queries, keys, values, segment, causal):
     length = queries.shape[0]
-    block_rows = min(256 if causal else 512, length)
+    block_rows = min(512, length)
     contexts = []
     totals = []
     for index in range(length // block_rows):

time: 375 us -> 405 us (1.080)
  matrix products: 148 us -> 168 us
  other arithmetic: 72.9 us -> 90.9 us
  waiting for transfers between devices: 38.1 us -> 21.1 us
  local copies, waits for them, and re-layouts: 68 us -> 78.7 us
    dot_general x0 -> x4, matrix products: none -> 10.4 us  [attend_backward(): jnp.einsum('qhe,khe->hqk', piece, near_keys, preferred_element_type=jnp.f...]
    dot_general x6, matrix products: 10.7 us -> 19.2 us  [attend_backward(): jnp.einsum('hqk,qhe->khe', probs.astype(jnp.bfloat16), grad_piece, prefer...]
    unnamed x375 -> x393, local copies, waits for them, and re-layouts: 30.3 us -> 38.3 us
    all_to_all x2, waiting for transfers between devices: 7.35 us -> 0.01 us  [exchange_sum(): first = lax.all_to_all(staged, 'inner', 0, 0, tiled=True)]
    dot_general x30, matrix products: 71.8 us -> 77.5 us  [project(): return jnp.dot(data, weight, preferred_element_type=jnp.float32)]
    ppermute x6, waiting for transfers between devices: 26 us -> 20.3 us  [exchange_sum(): lax.ppermute(piece, 'outer', [(peer, (peer + shift) % outer_size) for pee...]
    reduce_sum x5 -> x3, other arithmetic: 15.8 us -> 13.7 us  [attend_forward(): summed = jnp.sum(powers, -1, keepdims=True)]
    dot_general x6 -> x4, matrix products: 18.7 us -> 17.4 us  [attend_forward(): jnp.einsum('hqk,khe->qhe', weights, values[:end], preferred_element_type=...]
  transfers between devices with their start and end apart: 21 -> 21, of which waited for: 8 -> 4; matrix products, arithmetic and copies ran while one was open for 40% -> 49% of each run, Pallas kernels for 0% -> 0%
where the time goes in v5:
time: 405 us; the launch traced here: 400 us
  matrix products  168 us (41%)
  other arithmetic  90.9 us (22%)
  local copies, waits for them, and re-layouts  78.7 us (19%)
  starting transfers between devices  24 us (6%)
  waiting for transfers between devices  21.1 us (5%)
  between operations  16.8 us (4%)
    dot_general x30, matrix products, project(): return jnp.dot(data, weight, preferred_element_type=jnp.float32)  77.5 us
    unnamed x393, local copies, waits for them, and re-layouts  38.3 us
    ppermute x6, waiting for transfers between devices, exchange_sum(): lax.ppermute(piece, 'outer', [(peer, (peer + shift) % outer_size) for pee...  20.3 us
    dot_general x6, matrix products, attend_backward(): jnp.einsum('hqk,qhe->khe', probs.astype(jnp.bfloat16), grad_piece, prefer...  19.2 us
    dot_general x6, matrix products, attend_backward(): jnp.einsum('qhe,khe->hqk', grad_piece, values[:end], preferred_element_ty...  18.8 us
    dot_general x4, matrix products, attend_forward(): jnp.einsum('hqk,khe->qhe', weights, values[:end], preferred_element_type=...  17.4 us
    reduce_sum x3, other arithmetic, attend_forward(): summed = jnp.sum(powers, -1, keepdims=True)  13.7 us
    dot_general x4, matrix products, attend_forward(): jnp.einsum('qhe,khe->hqk', piece, keys[:end], preferred_element_type=jnp....  13.6 us
  transfers between devices with their start and end apart: 21, of which 4 were waited for; matrix products, arithmetic and copies ran while one was open for 49% of the time, Pallas kernels for 0%

profile of v5, /device:TPU:0, one launch (start us, length us, event | category | flops | bytes accessed | tf_op | source)
XLA Modules:
  0.0 399.8 jit_solution(10738353392227193553)
XLA Ops:
  9.0 2.4 convolution_convert_fusion.9
  16.7 2.1 broadcast_compare_fusion.1
  18.9 3.1 select_reduce_fusion
  22.0 3.4 fusion.4
  25.4 4.3 %fusion.161 = (bf16[512,6,64]{0,2,1:T(8,128)(2,1)}, f32[512,6,64]{0,2,1:T(8,128)S(1)}) fusion(bf16[1024,6,64]{0,2,1:T(8,128)(2,1)S(1)} %bitcast.387, f32[6,512,1024]{2,1,0:T(8,128)S(1)} %get-tuple-element.381, f32[6,512]{1,0:T(8,128)S(1)} %fusion.4, f32[6,512]{1,0:T(8,128)S(1)} %get-tuple-element.380, pred[512,1024]{1,0:T(8,128)(4,1)S(1)} %get-tuple-element.370), kind=kOutput, calls=%fused_computation.357 | convolution fusion | flops 415432704 | bytes 15097856 | tf_op jit(solution)/shard_map/hqk,khe->qhe/dot_general | solution.py:67
  32.0 2.5 fusion.162
  35.9 2.7 fusion.163
  38.6 3.4 slice_select_fusion
  45.7 2.1 constant_dynamic-slice_fusion
  47.7 2.3 copy.117
  62.8 3.1 copy.75
  68.4 1.9 copy.87
  70.3 1.9 copy.86
  74.4 2.9 fusion.152
  83.6 2.1 select_reduce_fusion.2
  85.8 7.2 %select_reduce_fusion.1 = (f32[6,512]{1,0:T(8,128)S(1)}, f32[6,512,1024]{2,1,0:T(8,128)}) fusion(pred[512,1024]{1,0:T(8,128)(4,1)S(1)} %copy-done.23, bf16[512,6,64]{0,2,1:T(8,128)(2,1)S(1)} %bitcast.350, bf16[1024,6,64]{0,2,1:T(8,128)(2,1)S(1)} %bitcast.336), kind=kOutput, calls=%fused_computation.16 | convolution fusion | flops 408941568 | bytes 14299136 | tf_op jit(solution)/shard_map/qhe,khe->hqk/dot_general | solution.py:54
  93.0 9.2 %fusion = (f32[6,512]{1,0:T(8,128)S(1)}, f32[6,512]{1,0:T(8,128)S(1)}) fusion(f32[6,512,1024]{2,1,0:T(8,128)S(1)} %get-tuple-element.387, f32[6,512]{1,0:T(8,128)S(1)} %get-tuple-element.386, pred[512,1024]{1,0:T(8,128)(4,1)S(1)} %copy-done.21, f32[6,512]{1,0:T(8,128)S(1)} %get-tuple-element.384, f32[6,512,1024]{2,1,0:T(8,128)} %get-tuple-element.385, ...), kind=kLoop, calls=%fused_computation.11 | loop fusion | flops 18868224 | bytes 26263552 | tf_op jit(solution)/shard_map/reduce_sum | solution.py:64
  102.2 3.4 fusion.81
  105.7 7.2 %fusion.80 = f32[512,6,64]{0,2,1:T(8,128)S(1)} fusion(bf16[1024,6,64]{0,2,1:T(8,128)(2,1)S(1)} %bitcast.426, f32[6,512,1024]{2,1,0:T(8,128)} %get-tuple-element.385, f32[6,512]{1,0:T(8,128)S(1)} %get-tuple-element.400, f32[6,512]{1,0:T(8,128)S(1)} %get-tuple-element.384, pred[512,1024]{1,0:T(8,128)(4,1)S(1)} %copy-done.23), kind=kOutput, calls=%fused_computation.177 | convolution fusion | flops 415236096 | bytes 14704640 | tf_op jit(solution)/shard_map/hqk,khe->qhe/dot_general | solution.py:67
  121.8 18.3 %multiply_convert_fusion.3 = (bf16[1024,1536]{1,0:T(8,128)(2,1)S(1)}, f32[1024,1536]{1,0:T(8,128)}, f32[1024,1536]{1,0:T(8,128)}) fusion(f32[1536]{0:T(1024)S(1)} %copy-done.168, bf16[768,1536]{1,0:T(8,128)(2,1)S(1)} %copy-done, bf16[512,768]{0,1:T(8,128)(2,1)S(1)} %get-tuple-element.326, bf16[512,768]{0,1:T(8,128)(2,1)S(1)} %get-tuple-element.325), kind=kOutput, calls=%fused_computation.28 | convolution fusion | flops 2522873856 | bytes 19666944 | tf_op jit(solution)/shard_map/dot_general | solution.py:25
  140.1 2.7 convolution_convert_fusion.5
  144.9 2.3 fusion.165
  147.2 2.9 fusion.166
  150.1 3.6 fusion.167
  156.5 2.1 fusion.30
  158.7 3.2 convert_reduce_fusion.3
  161.9 9.9 %convert_reduce_fusion = (f32[1536]{0:T(1024)}, bf16[1024,1536]{1,0:T(8,128)(2,1)}) fusion(f32[1024,1536]{1,0:T(8,128)} %get-tuple-element.315, bf16[1536,768]{1,0:T(8,128)(2,1)S(1)} %copy-done.173, f32[1024,768]{0,1:T(8,128)S(1)} %get-tuple-element.306, f32[1024,1536]{1,0:T(8,128)} %get-tuple-element.388, f32[1536]{0:T(1024)S(1)} %copy-done.168), kind=kOutput, calls=%fused_computation.22 | convolution fusion | flops 2443442688 | bytes 21245952 | tf_op jit(solution)/shard_map/dot_general | solution.py:25
  171.8 4.5 %convolution_convert_fusion.4 = bf16[1024,768]{0,1:T(8,128)(2,1)S(1)} fusion(bf16[1024,1536]{1,0:T(8,128)(2,1)} %get-tuple-element.394, bf16[768,1536]{1,0:T(8,128)(2,1)S(1)} %copy-done), kind=kOutput, calls=%fused_computation.98 | convolution fusion | flops 2416705536 | bytes 7077888 | tf_op jit(solution)/shard_map/dot_general | solution.py:25
  176.7 2.8 convolution_convert_fusion
  183.5 2.8 convolution_convert_fusion.1
  186.3 2.8 pad_maximum_fusion
  197.0 7.2 %multiply_convert_fusion.1 = bf16[6,512,1024]{2,1,0:T(8,128)(2,1)S(1)} fusion(f32[6,512,1024]{2,1,0:T(8,128)} %copy-done.2, f32[6,512]{1,0:T(8,128)S(1)} %get-tuple-element.362, f32[6,512]{1,0:T(8,128)S(1)} %log_add_fusion.1, pred[512,1024]{1,0:T(8,128)(4,1)S(1)} %copy-done.22, bf16[512,6,64]{0,2,1:T(8,128)(2,1)S(1)} %bitcast.404, ...), kind=kOutput, calls=%fused_computation.2 | convolution fusion | flops 418381824 | bytes 20602880 | tf_op jit(solution)/shard_map/qhe,khe->hqk/dot_general | solution.py:95
  204.2 2.0 convolution_convert_fusion.19
  207.7 2.9 fusion.6
  210.6 5.6 %multiply_convert_fusion = bf16[6,512,1024]{2,1,0:T(8,128)(2,1)S(1)} fusion(f32[6,512,1024]{2,1,0:T(8,128)S(1)} %bitcast.327, f32[6,512]{1,0:T(8,128)S(1)} %get-tuple-element.361, f32[6,512]{1,0:T(8,128)S(1)} %copy-done.143, pred[512,1024]{1,0:T(8,128)(4,1)S(1)} %copy-done.24, bf16[512,6,64]{0,2,1:T(8,128)(2,1)} %bitcast.406, bf16[1024,6,64]{0,2,1:T(8,128)(2,1)} %bitcast.427), kind=kOutput, calls=%fused_computation | convolution fusion | flops 418381824 | bytes 20602880 | tf_op jit(solution)/shard_map/qhe,khe->hqk/dot_general | solution.py:95
  216.2 2.0 convolution_convert_fusion.18
  225.5 4.0 %convert_reduce_fusion.6 = (f32[6,64]{1,0:T(8,128)}, bf16[6,64,1024]{2,1,0:T(8,128)(2,1)S(1)}) fusion(f32[6,64,1024]{2,1,0:T(8,128)S(1)} %fusion.6, bf16[512,6,64]{0,2,1:T(8,128)(2,1)S(1)} %bitcast.405, f32[6,512,1024]{2,1,0:T(8,128)S(1)} %bitcast.325, f32[6,512]{1,0:T(8,128)S(1)} %log_add_fusion.1, pred[512,1024]{1,0:T(8,128)(4,1)S(1)} %copy-done.22), kind=kOutput, calls=%fused_computation.121 | convolution fusion | flops 413662848 | bytes 15873536 | tf_op jit(solution)/shard_map/hqk,qhe->khe/dot_general | solution.py:107
  233.9 2.5 convolution_convert_fusion.17
  248.3 2.5 copy.89
  250.8 3.3 copy.90
  254.1 5.4 %all-to-all-start.1 = ((bf16[4,192,1536]{2,1,0:T(8,128)(2,1)}), bf16[4,192,1536]{2,1,0:T(8,128)(2,1)}, u32[]{:S(2)}, u32[]{:S(2)}) async-start(bf16[4,192,1536]{2,1,0:T(8,128)(2,1)} %bitcast.340), calls=%async_computation.1 | async-start | bytes 4718592 | tf_op jit(solution)/shard_map/all_to_all | solution.py:357
  275.0 2.4 multiply_convert_fusion.2
  281.6 2.2 copy.83
  284.0 2.8 fusion.77
  286.9 3.8 fusion.63
  290.7 4.6 %convert_reduce_fusion.8 = (f32[6,64]{1,0:T(8,128)S(1)}, bf16[1024,6,64]{0,2,1:T(8,128)(2,1)S(1)}) fusion(f32[1024,6,64]{0,2,1:T(8,128)S(1)} %fusion.63, bf16[256,6,64]{0,2,1:T(8,128)(2,1)S(1)} %bitcast.413, f32[6,256,1024]{2,1,0:T(8,128)} %fusion.167, f32[6,256]{1,0:T(8,128)S(1)} %copy-done.150, pred[256,1024]{1,0:T(8,128)(4,1)S(1)} %copy-done.91), kind=kOutput, calls=%fused_computation.123 | convolution fusion | flops 207617664 | bytes 9117184 | tf_op jit(solution)/shard_map/hqk,qhe->khe/dot_general | solution.py:107
  297.9 2.1 copy.85
  307.3 2.2 copy.84
  314.9 3.6 pad_maximum_fusion.1
  318.5 2.7 fusion.145
  321.2 2.8 fusion.168
  324.0 5.0 %all-to-all-start = ((bf16[4,206,1536]{2,1,0:T(8,128)(2,1)}), bf16[4,206,1536]{2,1,0:T(8,128)(2,1)}, u32[]{:S(2)}, u32[]{:S(2)}) async-start(bf16[4,206,1536]{2,1,0:T(8,128)(2,1)} %pad_maximum_fusion.1), calls=%async_computation | async-start | bytes 5111808 | tf_op jit(solution)/shard_map/all_to_all | solution.py:357
  329.0 3.8 add_convert_fusion.2
  334.3 2.6 copy.91
  336.8 3.1 convert_add_fusion
  340.0 3.0 copy.93
  343.0 2.3 reduce_sum.376
  346.0 4.8 %collective-permute-start.15 = (bf16[48,1536]{1,0:T(8,128)(2,1)}, bf16[48,1536]{1,0:T(8,128)(2,1)S(1)}, u32[]{:S(2)}, u32[]{:S(2)}) collective-permute-start(bf16[48,1536]{1,0:T(8,128)(2,1)} %get-tuple-element.348), channel_id=1, source_target_pairs={{0,24},{8,0},{16,8},{24,16},{1,25},{9,1},{17,9},{25,17},{2,26},{10... | collective-permute-start | bytes 442376 | tf_op jit(solution)/shard_map/ppermute | solution.py:382
  351.9 3.2 add_add_fusion.4
  355.0 3.0 copy.92
  358.0 6.1 %collective-permute-done.16 = bf16[48,1536]{1,0:T(8,128)(2,1)S(1)} collective-permute-done((bf16[48,1536]{1,0:T(8,128)(2,1)}, bf16[48,1536]{1,0:T(8,128)(2,1)S(1)}, u32[]{:S(2)}, u32[]{:S(2)}) %collective-permute-start.16) | collective-permute-done | bytes 147488 | tf_op jit(solution)/shard_map/ppermute | solution.py:382
  364.3 2.2 convert_reduce_fusion.1
  369.6 1.9 collective-permute-start.14
  373.6 12.9 %collective-permute-done.13 = bf16[62,1536]{1,0:T(8,128)(2,1)S(1)} collective-permute-done((bf16[62,1536]{1,0:T(8,128)(2,1)S(1)}, bf16[62,1536]{1,0:T(8,128)(2,1)S(1)}, u32[]{:S(2)}, u32[]{:S(2)}) %collective-permute-start.13) | collective-permute-done | bytes 190496 | tf_op jit(solution)/shard_map/ppermute | solution.py:382
  (592 shorter events, 137.1 us)
Async XLA Ops:
  7.2 114.5 %copy-start = (bf16[768,1536]{1,0:T(8,128)(2,1)S(1)}, bf16[768,1536]{1,0:T(8,128)(2,1)}, u32[]{:S(2)}) copy-start(bf16[768,1536]{1,0:T(8,128)(2,1)} %param.88) | copy-start | bytes 7077892
  7.2 382.1 %reduce-scatter.2.cloned.1.call-start = ((), (), s32[]{:S(2)}) async-start(), calls=%async_computation.3 | async-start | bytes 5013504 | tf_op jit(solution)/shard_map/reduce_scatter | solution.py:400
  8.2 8.6 %copy-start.144 = (s32[512]{0:T(512)}, s32[512]{0:T(512)S(1)}, u32[]{:S(2)}) copy-start(s32[512]{0:T(512)S(1)} %get-tuple-element.378) | copy-start | bytes 6148
  29.7 4.8 %copy-start.43 = (f32[512,6,64]{0,2,1:T(8,128)}, f32[512,6,64]{0,2,1:T(8,128)S(1)}, u32[]{:S(2)}) copy-start(f32[512,6,64]{0,2,1:T(8,128)S(1)} %get-tuple-element.396) | copy-start | bytes 2359300
  42.0 32.3 %collective-permute-start = (f32[512,768]{0,1:T(8,128)}, f32[512,768]{0,1:T(8,128)}, u32[]{:S(2)}, u32[]{:S(2)}) collective-permute-start(f32[512,768]{0,1:T(8,128)} %slice_select_fusion), channel_id=1, source_target_pairs={{0,1},{1,0},{2,3},{3,2},{4,5},{5,4},{6,7},{7,6},{8,9},{9,8},{10,11... | collective-permute-start | bytes 4718600 | tf_op jit(solution)/shard_map/ppermute | solution.py:164
  77.3 40.3 %copy-start.3 = (f32[512,768]{0,1:T(8,128)}, f32[512,768]{0,1:T(8,128)S(1)}, u32[]{:S(2)}) copy-start(f32[512,768]{0,1:T(8,128)S(1)} %get-tuple-element.319) | copy-start | bytes 4718596
  77.4 40.2 %copy-start.135 = (f32[512]{0:T(512)}, f32[512]{0:T(512)S(1)}, u32[]{:S(2)}) copy-start(f32[512]{0:T(512)S(1)} %broadcast_multiply_fusion.2) | copy-start | bytes 6148
  77.7 39.9 %copy-start.137 = (f32[512]{0:T(512)}, f32[512]{0:T(512)S(1)}, u32[]{:S(2)}) copy-start(f32[512]{0:T(512)S(1)} %fusion.119) | copy-start | bytes 6148
  78.0 3.2 collective-permute-start.1
  80.4 5.4 %copy-start.16 = (bf16[1024,384]{0,1:T(8,128)(2,1)}, bf16[1024,384]{0,1:T(8,128)(2,1)S(1)}, u32[]{:S(2)}) copy-start(bf16[1024,384]{0,1:T(8,128)(2,1)S(1)} %convolution_convert_fusion.8) | copy-start | bytes 2359300
  81.2 24.5 %copy-start.181 = (bf16[1024,384]{0,1:T(8,128)(2,1)}, bf16[1024,384]{0,1:T(8,128)(2,1)S(1)}, u32[]{:S(2)}) copy-start(bf16[1024,384]{0,1:T(8,128)(2,1)S(1)} %add_convert_fusion.7) | copy-start | bytes 2359300
  85.8 16.5 %copy-start.2 = (f32[6,512,1024]{2,1,0:T(8,128)}, f32[6,512,1024]{2,1,0:T(8,128)S(1)}, u32[]{:S(2)}) copy-start(f32[6,512,1024]{2,1,0:T(8,128)S(1)} %get-tuple-element.387) | copy-start | bytes 37748740
  105.7 7.2 %copy-start.47 = (f32[512,6,64]{0,2,1:T(8,128)}, f32[512,6,64]{0,2,1:T(8,128)S(1)}, u32[]{:S(2)}) copy-start(f32[512,6,64]{0,2,1:T(8,128)S(1)} %fusion.81) | copy-start | bytes 2359300
  105.7 8.4 %copy-start.177 = (bf16[384,768]{1,0:T(8,128)(2,1)S(1)}, bf16[384,768]{1,0:T(8,128)(2,1)}, u32[]{:S(2)}) copy-start(bf16[384,768]{1,0:T(8,128)(2,1)} %param.80) | copy-start | bytes 1769476
  115.2 2.4 collective-permute-start.2
  118.8 2.4 collective-permute-start.3
  121.1 22.2 %copy-start.79 = (bf16[256,384]{0,1:T(8,128)(2,1)}, bf16[256,384]{0,1:T(8,128)(2,1)S(1)}, u32[]{:S(2)}) copy-start(bf16[256,384]{0,1:T(8,128)(2,1)S(1)} %get-tuple-element.336) | copy-start | bytes 589828
  121.1 23.8 %copy-start.63 = (bf16[256,384]{0,1:T(8,128)(2,1)}, bf16[256,384]{0,1:T(8,128)(2,1)S(1)}, u32[]{:S(2)}) copy-start(bf16[256,384]{0,1:T(8,128)(2,1)S(1)} %get-tuple-element.339) | copy-start | bytes 589828
  121.1 26.0 %copy-start.61 = (bf16[256,384]{0,1:T(8,128)(2,1)}, bf16[256,384]{0,1:T(8,128)(2,1)S(1)}, u32[]{:S(2)}) copy-start(bf16[256,384]{0,1:T(8,128)(2,1)S(1)} %get-tuple-element.338) | copy-start | bytes 589828
  121.1 28.9 %copy-start.71 = (bf16[256,384]{0,1:T(8,128)(2,1)}, bf16[256,384]{0,1:T(8,128)(2,1)S(1)}, u32[]{:S(2)}) copy-start(bf16[256,384]{0,1:T(8,128)(2,1)S(1)} %get-tuple-element.337) | copy-start | bytes 589828
  121.8 18.3 %copy-start.173 = (bf16[1536,768]{1,0:T(8,128)(2,1)S(1)}, bf16[1536,768]{1,0:T(8,128)(2,1)}, u32[]{:S(2)}) copy-start(bf16[1536,768]{1,0:T(8,128)(2,1)} %param.90) | copy-start | bytes 7077892
  142.8 11.5 %collective-permute-start.4 = (bf16[1024,768]{0,1:T(8,128)(2,1)S(1)}, bf16[1024,768]{0,1:T(8,128)(2,1)S(1)}, u32[]{:S(2)}, u32[]{:S(2)}) collective-permute-start(bf16[1024,768]{0,1:T(8,128)(2,1)S(1)} %convolution_convert_fusion.5), channel_id=1, source_target_pairs={{0,1},{1,0},{2,3},{3,2},{4,5},{5,4},{6,7},{7,6},{8,9},{9,8},{10,11... | collective-permute-start | bytes 4718600 | tf_op jit(solution)/shard_map/ppermute | solution.py:164
  176.4 3.0 collective-permute-start.5
  181.5 11.6 %copy-start.8 = (f32[512,768]{0,1:T(8,128)}, f32[512,768]{0,1:T(8,128)S(1)}, u32[]{:S(2)}) copy-start(f32[512,768]{0,1:T(8,128)S(1)} %get-tuple-element.310) | copy-start | bytes 4718596
  182.2 10.9 %collective-permute-start.6 = (bf16[512,768]{0,1:T(8,128)(2,1)S(1)}, bf16[512,768]{0,1:T(8,128)(2,1)}, u32[]{:S(2)}, u32[]{:S(2)}) collective-permute-start(bf16[512,768]{0,1:T(8,128)(2,1)S(1)} %add_convert_fusion.10), channel_id=1, source_target_pairs={{0,1},{1,0},{2,3},{3,2},{4,5},{5,4},{6,7},{7,6},{8,9},{9,8},{10,11... | collective-permute-start | bytes 2359304 | tf_op jit(solution)/shard_map/ppermute | solution.py:164
  189.1 5.3 %copy-start.178 = (bf16[384,768]{1,0:T(8,128)(2,1)S(1)}, bf16[384,768]{1,0:T(8,128)(2,1)}, u32[]{:S(2)}) copy-start(bf16[384,768]{1,0:T(8,128)(2,1)} %param.80) | copy-start | bytes 1769476
  194.4 37.2 %copy-start.51 = (bf16[512,768]{0,1:T(8,128)(2,1)}, bf16[512,768]{0,1:T(8,128)(2,1)S(1)}, u32[]{:S(2)}) copy-start(bf16[512,768]{0,1:T(8,128)(2,1)S(1)} %get-tuple-element.323) | copy-start | bytes 2359300
  194.4 37.2 %copy-start.53 = (bf16[512,768]{0,1:T(8,128)(2,1)}, bf16[512,768]{0,1:T(8,128)(2,1)S(1)}, u32[]{:S(2)}) copy-start(bf16[512,768]{0,1:T(8,128)(2,1)S(1)} %get-tuple-element.324) | copy-start | bytes 2359300
  197.0 7.2 %copy-start.17 = (bf16[1024,384]{0,1:T(8,128)(2,1)S(1)}, bf16[1024,384]{0,1:T(8,128)(2,1)}, u32[]{:S(2)}) copy-start(bf16[1024,384]{0,1:T(8,128)(2,1)} %copy-done.16) | copy-start | bytes 2359300
  197.0 10.5 %slice-start.3 = ((s8[12582912]{0:T(1024)(128)(4,1)}), s8[4194304]{0:T(1024)(128)(4,1)S(1)}, s32[]{:S(2)}) async-start(s8[12582912]{0:T(1024)(128)(4,1)} %bitcast.326), calls=%async_computation.7 | async-start | bytes 8388608
  197.0 10.6 %slice-start.4 = ((s8[12582912]{0:T(1024)(128)(4,1)}), s8[4194304]{0:T(1024)(128)(4,1)S(1)}, s32[]{:S(2)}) async-start(s8[12582912]{0:T(1024)(128)(4,1)} %bitcast.326), calls=%async_computation.8 | async-start | bytes 8388608
  206.3 16.6 %copy-start.81 = (bf16[6,64,512]{2,1,0:T(8,128)(2,1)}, bf16[6,64,512]{2,1,0:T(8,128)(2,1)S(1)}, u32[]{:S(2)}) copy-start(bf16[6,64,512]{2,1,0:T(8,128)(2,1)S(1)} %convolution_convert_fusion.19) | copy-start | bytes 1179652
  218.2 4.7 %copy-start.83 = (bf16[6,64,512]{2,1,0:T(8,128)(2,1)}, bf16[6,64,512]{2,1,0:T(8,128)(2,1)S(1)}, u32[]{:S(2)}) copy-start(bf16[6,64,512]{2,1,0:T(8,128)(2,1)S(1)} %convolution_convert_fusion.18) | copy-start | bytes 1179652
  218.3 7.2 %slice-start = ((s8[12582912]{0:T(1024)(128)(4,1)}), s8[4194304]{0:T(1024)(128)(4,1)S(1)}, s32[]{:S(2)}) async-start(s8[12582912]{0:T(1024)(128)(4,1)} %bitcast.324), calls=%async_computation.4 | async-start | bytes 8388608
  218.3 7.2 %slice-start.1 = ((s8[12582912]{0:T(1024)(128)(4,1)}), s8[4194304]{0:T(1024)(128)(4,1)S(1)}, s32[]{:S(2)}) async-start(s8[12582912]{0:T(1024)(128)(4,1)} %bitcast.324), calls=%async_computation.5 | async-start | bytes 8388608
  223.9 5.6 %copy-start.31 = (bf16[1024,768]{0,1:T(8,128)(2,1)}, bf16[1024,768]{0,1:T(8,128)(2,1)S(1)}, u32[]{:S(2)}) copy-start(bf16[1024,768]{0,1:T(8,128)(2,1)S(1)} %convolution_convert_fusion.2) | copy-start | bytes 4718596
  225.0 14.3 %collective-permute-start.7 = (bf16[512,768]{0,1:T(8,128)(2,1)}, bf16[512,768]{0,1:T(8,128)(2,1)}, u32[]{:S(2)}, u32[]{:S(2)}) collective-permute-start(bf16[512,768]{0,1:T(8,128)(2,1)} %broadcast_select_fusion.4), channel_id=1, source_target_pairs={{0,1},{1,0},{2,3},{3,2},{4,5},{5,4},{6,7},{7,6},{8,9},{9,8},{10,11... | collective-permute-start | bytes 2359304 | tf_op jit(solution)/shard_map/ppermute | solution.py:164
  246.0 15.4 %collective-permute-start.8 = (bf16[512,768]{0,1:T(8,128)(2,1)}, bf16[512,768]{0,1:T(8,128)(2,1)}, u32[]{:S(2)}, u32[]{:S(2)}) collective-permute-start(bf16[512,768]{0,1:T(8,128)(2,1)} %add_convert_fusion.9), channel_id=1, source_target_pairs={{0,1},{1,0},{2,3},{3,2},{4,5},{5,4},{6,7},{7,6},{8,9},{9,8},{10,11... | collective-permute-start | bytes 2359304 | tf_op jit(solution)/shard_map/ppermute | solution.py:164
  247.2 12.2 %collective-permute-start.11 = (f32[3072]{0:T(1024)}, f32[3072]{0:T(1024)}, u32[]{:S(2)}, u32[]{:S(2)}) collective-permute-start(f32[3072]{0:T(1024)} %pad_maximum_fusion.17), channel_id=1, source_target_pairs={{0,1},{1,0},{2,3},{3,2},{4,5},{5,4},{6,7},{7,6},{8,9},{9,8},{10,11... | collective-permute-start | bytes 36872 | tf_op jit(solution)/shard_map/ppermute | solution.py:164
  248.3 88.5 %collective-permute-start.10 = (bf16[512,768]{0,1:T(8,128)(2,1)}, bf16[512,768]{0,1:T(8,128)(2,1)}, u32[]{:S(2)}, u32[]{:S(2)}) collective-permute-start(bf16[512,768]{0,1:T(8,128)(2,1)} %broadcast_select_fusion), channel_id=1, source_target_pairs={{0,1},{1,0},{2,3},{3,2},{4,5},{5,4},{6,7},{7,6},{8,9},{9,8},{10,11... | collective-permute-start | bytes 2359304 | tf_op jit(solution)/shard_map/ppermute | solution.py:164
  254.1 7.4 %copy-start.7 = (f32[512,768]{0,1:T(8,128)S(1)}, f32[512,768]{0,1:T(8,128)}, u32[]{:S(2)}) copy-start(f32[512,768]{0,1:T(8,128)} %copy-done.6) | copy-start | bytes 4718596
  254.1 69.9 %all-to-all-start.1 = ((bf16[4,192,1536]{2,1,0:T(8,128)(2,1)}), bf16[4,192,1536]{2,1,0:T(8,128)(2,1)}, u32[]{:S(2)}, u32[]{:S(2)}) async-start(bf16[4,192,1536]{2,1,0:T(8,128)(2,1)} %bitcast.340), calls=%async_computation.1 | async-start | bytes 4718592 | tf_op jit(solution)/shard_map/all_to_all | solution.py:357
  264.5 6.6 %copy-start.102 = (bf16[256,384]{0,1:T(8,128)(2,1)}, bf16[256,384]{0,1:T(8,128)(2,1)S(1)}, u32[]{:S(2)}) copy-start(bf16[256,384]{0,1:T(8,128)(2,1)S(1)} %get-tuple-element.334) | copy-start | bytes 589828
  264.5 9.9 %copy-start.100 = (bf16[256,384]{0,1:T(8,128)(2,1)}, bf16[256,384]{0,1:T(8,128)(2,1)S(1)}, u32[]{:S(2)}) copy-start(bf16[256,384]{0,1:T(8,128)(2,1)S(1)} %get-tuple-element.333) | copy-start | bytes 589828
  265.0 6.1 %slice-start.8 = ((s8[4718592]{0:T(1024)(128)(4,1)}), s8[4194304]{0:T(1024)(128)(4,1)S(1)}, s32[]{:S(2)}) async-start(s8[4718592]{0:T(1024)(128)(4,1)} %bitcast.330), calls=%async_computation.12 | async-start | bytes 8388608
  268.1 11.0 %copy-start.65 = (bf16[6,64,256]{2,1,0:T(8,128)(2,1)}, bf16[6,64,256]{2,1,0:T(8,128)(2,1)S(1)}, u32[]{:S(2)}) copy-start(bf16[6,64,256]{2,1,0:T(8,128)(2,1)S(1)} %convolution_convert_fusion.23) | copy-start | bytes 589828
  268.6 5.8 %slice-start.6 = ((s8[6291456]{0:T(1024)(128)(4,1)}), s8[4194304]{0:T(1024)(128)(4,1)S(1)}, s32[]{:S(2)}) async-start(s8[6291456]{0:T(1024)(128)(4,1)} %bitcast.328), calls=%async_computation.10 | async-start | bytes 8388608
  270.6 8.5 %copy-start.67 = (bf16[6,64,256]{2,1,0:T(8,128)(2,1)}, bf16[6,64,256]{2,1,0:T(8,128)(2,1)S(1)}, u32[]{:S(2)}) copy-start(bf16[6,64,256]{2,1,0:T(8,128)(2,1)S(1)} %convolution_convert_fusion.21) | copy-start | bytes 589828
  273.9 5.1 %copy-start.69 = (bf16[6,64,256]{2,1,0:T(8,128)(2,1)}, bf16[6,64,256]{2,1,0:T(8,128)(2,1)S(1)}, u32[]{:S(2)}) copy-start(bf16[6,64,256]{2,1,0:T(8,128)(2,1)S(1)} %convolution_convert_fusion.22) | copy-start | bytes 589828
  290.7 5.5 %copy-start.123 = (bf16[1024,768]{1,0:T(8,128)(2,1)S(1)}, bf16[1024,768]{1,0:T(8,128)(2,1)}, u32[]{:S(2)}) copy-start(bf16[1024,768]{1,0:T(8,128)(2,1)} %param.64) | copy-start | bytes 4718596
  305.7 5.1 %copy-start.26 = (bf16[512,768]{0,1:T(8,128)(2,1)S(1)}, bf16[512,768]{0,1:T(8,128)(2,1)}, u32[]{:S(2)}) copy-start(bf16[512,768]{0,1:T(8,128)(2,1)} %copy-done.25) | copy-start | bytes 2359300
  305.7 5.1 %copy-start.28 = (bf16[512,768]{0,1:T(8,128)(2,1)S(1)}, bf16[512,768]{0,1:T(8,128)(2,1)}, u32[]{:S(2)}) copy-start(bf16[512,768]{0,1:T(8,128)(2,1)} %copy-done.27) | copy-start | bytes 2359300
  324.0 5.0 %copy-start.40 = (bf16[1024,6,64]{0,2,1:T(8,128)(2,1)S(1)}, bf16[1024,6,64]{0,2,1:T(8,128)(2,1)}, u32[]{:S(2)}) copy-start(bf16[1024,6,64]{0,2,1:T(8,128)(2,1)} %copy-done.39) | copy-start | bytes 2359300
  324.0 5.0 %copy-start.115 = (bf16[768,384]{1,0:T(8,128)(2,1)S(1)}, bf16[768,384]{1,0:T(8,128)(2,1)}, u32[]{:S(2)}) copy-start(bf16[768,384]{1,0:T(8,128)(2,1)} %param.71) | copy-start | bytes 1769476
  324.0 40.3 %all-to-all-start = ((bf16[4,206,1536]{2,1,0:T(8,128)(2,1)}), bf16[4,206,1536]{2,1,0:T(8,128)(2,1)}, u32[]{:S(2)}, u32[]{:S(2)}) async-start(bf16[4,206,1536]{2,1,0:T(8,128)(2,1)} %pad_maximum_fusion.1), calls=%async_computation | async-start | bytes 5111808 | tf_op jit(solution)/shard_map/all_to_all | solution.py:357
  334.0 17.8 %collective-permute-start.9 = (bf16[512,768]{0,1:T(8,128)(2,1)S(1)}, bf16[512,768]{0,1:T(8,128)(2,1)}, u32[]{:S(2)}, u32[]{:S(2)}) collective-permute-start(bf16[512,768]{0,1:T(8,128)(2,1)S(1)} %broadcast_select_fusion.1), channel_id=1, source_target_pairs={{0,1},{1,0},{2,3},{3,2},{4,5},{5,4},{6,7},{7,6},{8,9},{9,8},{10,11... | collective-permute-start | bytes 2359304 | tf_op jit(solution)/shard_map/ppermute | solution.py:164
  343.0 8.9 %copy-start.152 = (f32[512]{0:T(512)S(1)}, f32[512]{0:T(512)}, u32[]{:S(2)}) copy-start(f32[512]{0:T(512)} %copy-done.151) | copy-start | bytes 6148
  346.0 12.0 %collective-permute-start.15 = (bf16[48,1536]{1,0:T(8,128)(2,1)}, bf16[48,1536]{1,0:T(8,128)(2,1)S(1)}, u32[]{:S(2)}, u32[]{:S(2)}) collective-permute-start(bf16[48,1536]{1,0:T(8,128)(2,1)} %get-tuple-element.348), channel_id=1, source_target_pairs={{0,24},{8,0},{16,8},{24,16},{1,25},{9,1},{17,9},{25,17},{2,26},{10... | collective-permute-start | bytes 442376 | tf_op jit(solution)/shard_map/ppermute | solution.py:382
  350.8 13.3 %collective-permute-start.16 = (bf16[48,1536]{1,0:T(8,128)(2,1)}, bf16[48,1536]{1,0:T(8,128)(2,1)S(1)}, u32[]{:S(2)}, u32[]{:S(2)}) collective-permute-start(bf16[48,1536]{1,0:T(8,128)(2,1)} %get-tuple-element.347), channel_id=1, source_target_pairs={{0,16},{8,24},{16,0},{24,8},{1,17},{9,25},{17,1},{25,9},{2,18},{10... | collective-permute-start | bytes 442376 | tf_op jit(solution)/shard_map/ppermute | solution.py:382
  350.9 13.3 %collective-permute-start.17 = (bf16[48,1536]{1,0:T(8,128)(2,1)}, bf16[48,1536]{1,0:T(8,128)(2,1)S(1)}, u32[]{:S(2)}, u32[]{:S(2)}) collective-permute-start(bf16[48,1536]{1,0:T(8,128)(2,1)} %get-tuple-element.346), channel_id=1, source_target_pairs={{0,8},{8,16},{16,24},{24,0},{1,9},{9,17},{17,25},{25,1},{2,10},{10... | collective-permute-start | bytes 442376 | tf_op jit(solution)/shard_map/ppermute | solution.py:382
  366.7 6.9 %collective-permute-start.12 = (bf16[62,1536]{1,0:T(8,128)(2,1)S(1)}, bf16[62,1536]{1,0:T(8,128)(2,1)S(1)}, u32[]{:S(2)}, u32[]{:S(2)}) collective-permute-start(bf16[62,1536]{1,0:T(8,128)(2,1)S(1)} %get-tuple-element.330), channel_id=1, source_target_pairs={{0,24},{8,0},{16,8},{24,16},{1,25},{9,1},{17,9},{25,17},{2,26},{10... | collective-permute-start | bytes 571400 | tf_op jit(solution)/shard_map/ppermute | solution.py:382
  368.1 18.4 %collective-permute-start.13 = (bf16[62,1536]{1,0:T(8,128)(2,1)S(1)}, bf16[62,1536]{1,0:T(8,128)(2,1)S(1)}, u32[]{:S(2)}, u32[]{:S(2)}) collective-permute-start(bf16[62,1536]{1,0:T(8,128)(2,1)S(1)} %get-tuple-element.331), channel_id=1, source_target_pairs={{0,16},{8,24},{16,0},{24,8},{1,17},{9,25},{17,1},{25,9},{2,18},{10... | collective-permute-start | bytes 571400 | tf_op jit(solution)/shard_map/ppermute | solution.py:382
  369.6 23.2 %copy-start.1 = (bf16[768,1536]{1,0:T(8,128)(2,1)S(1)}, bf16[768,1536]{1,0:T(8,128)(2,1)}, u32[]{:S(2)}) copy-start(bf16[768,1536]{1,0:T(8,128)(2,1)} %param.88) | copy-start | bytes 7077892
  369.6 16.9 %collective-permute-start.14 = (bf16[62,1536]{1,0:T(8,128)(2,1)S(1)}, bf16[62,1536]{1,0:T(8,128)(2,1)S(1)}, u32[]{:S(2)}, u32[]{:S(2)}) collective-permute-start(bf16[62,1536]{1,0:T(8,128)(2,1)S(1)} %get-tuple-element.329), channel_id=1, source_target_pairs={{0,8},{8,16},{16,24},{24,0},{1,9},{9,17},{17,25},{25,1},{2,10},{10... | collective-permute-start | bytes 571400 | tf_op jit(solution)/shard_map/ppermute | solution.py:382
  (151 other events, 352.5 us)
Sparse Core Ops, SparseCore 0:
  189.3 154.3 reduce-scatter.1
